TPU v7x, 32 devices: a whole 2x2x4 slice. The times are simulated.
32 devices in a mesh: cuts: 4 (over z), dom: 8 (over y, x, core).
Axes of the slice: x: 2, y: 2, z: 4, core: 2. Of those that a mesh axis runs over, the one named last changes fastest.
Arguments:
- radiation: float32 [256, 8, 512], P('dom', 'cuts'), may hold values from -6 to 6
- electrons: float32 [2, 8, 16384], P(None, 'cuts', 'dom'), may hold values from -6 to 6
- cell_index: int32 [2, 8, 16384], P(None, 'cuts', 'dom'), may hold values from 0 to 254
- cell_offset: float32 [2, 8, 16384], P(None, 'cuts', 'dom'), may hold values from 0 to 1
- kernel_x: float32 [2, 256, 256], replicated, may hold values from -0.25 to 0.25
- kernel_y: float32 [2, 256, 256], replicated, may hold values from -0.25 to 0.25
Outputs:
- radiation_out: float32 [256, 8, 512], P('dom', 'cuts')
- electrons_out: float32 [2, 8, 16384], P(None, 'cuts', 'dom')
Inputs may be any that keep to these rules, and one draw needn't show every extreme that they name: `cell_index`: the field is interpolated between cell and cell + 1 in each dimension, so every index stays below 255.
All inputs are finite; a program needn't handle non-finite values.
Results may differ from a plain program's by a relative error of at most 0.0003.
Values sent between devices are 32-bit elements; how exact they have to be, the bound alone decides.
No kernel may reach another device: no remote copies, remote signals or barrier semaphores. Data moves between devices by JAX's collectives and lax.ppermute only.
A program may use at most 64 MiB of HBM per device.

v0:
```python
import math

import jax
import jax.numpy as jnp
from jax import lax
from jax.experimental import pallas as pl
from jax.experimental.pallas import tpu as pltpu
from jax.sharding import PartitionSpec as P


ITERS = 4
TILE = 256
BATCH = 8
VMEM_LIMIT = 20 * 2**20

coupling = 0.5
phase_step = 1.0
current_gain = 1.0

f32 = jnp.float32
bf16 = jnp.bfloat16


def split(value):
    high = value.astype(bf16)
    return high, (value - high.astype(f32)).astype(bf16)


def dot(left, right):
    return jnp.dot(left, right, preferred_element_type=f32)


def dot_t(left, right):
    return lax.dot_general(left, right, (((1,), (1,)), ((), ())), preferred_element_type=f32)


def dot3(left, right, product=dot):
    return product(left[0], right[0]) + product(left[1], right[0]) + product(left[0], right[1])


def tent(rows, index, offset):
    distance = lax.broadcasted_iota(jnp.int32, (rows, index.shape[1]), 0).astype(f32) - index
    return jnp.where(distance == 0.0, 1.0 - offset, jnp.where(distance == 1.0, offset, 0.0))


def complex_rows(real, imag):
    rows = real.shape[0] // 2
    return jnp.concatenate([real[:rows] - imag[rows:], real[rows:] + imag[:rows]], axis=0)


def propagate(field, kernel_x, kernel_y):
    half = field.shape[0] // 2
    left = split(kernel_x)
    mixed = split(complex_rows(dot3(left, split(field[:half])), dot3(left, split(field[half:]))))
    return complex_rows(dot3(mixed, split(kernel_y[0])), dot3(mixed, split(kernel_y[1])))


def cell_masks(rows, index):
    shape = (rows, index.shape[1])
    cell = lax.broadcasted_iota(jnp.int32, shape, 0).astype(f32).astype(bf16)
    at = lambda value: jnp.broadcast_to(value.astype(bf16), shape)
    return cell == at(index), cell == at(index + 1.0)


def place(masks, low, high):
    spread = lambda value: jnp.broadcast_to(value, masks[0].shape)
    return jnp.where(masks[0], spread(low), jnp.where(masks[1], spread(high), jnp.zeros(masks[0].shape, low.dtype)))


def place_split(masks, low, high):
    return tuple(place(masks, *pair) for pair in zip(split(low), split(high)))


def gather_tiles(field_ref, cells_ref, high_ref, low_ref, amp_ref):
    half = field_ref.shape[0] // 2
    columns = field_ref.shape[1]
    high, low = split(field_ref[...])
    high_ref[...] = high
    low_ref[...] = low

    def body(t, carry):
        row = lambda n: cells_ref[n, pl.ds(t, 1), :]
        wy = place_split(cell_masks(columns, row(1)), 1.0 - row(3), row(3))
        wx = tent(half, row(0), row(2))
        out = dot3((high_ref[...], low_ref[...]), wy)
        amp_ref[0, pl.ds(t, 1), :] = jnp.sum(out[:half] * wx, axis=0, keepdims=True)
        amp_ref[1, pl.ds(t, 1), :] = jnp.sum(out[half:] * wx, axis=0, keepdims=True)
        return carry

    tiles = cells_ref.shape[1]
    lax.fori_loop(0, tiles, body, 0, unroll=math.gcd(tiles, BATCH))


def first_kernel(where_ref, *refs):
    *blocks, field_ref, amp_ref, state_ref, cells_ref, high_ref, low_ref = refs
    half = field_ref.shape[0] // 2
    count = len(blocks) // 2
    rows = half // len(blocks)
    tiles = cells_ref.shape[1] // count
    for n, ref in enumerate(blocks):
        at = pl.multiple_of(where_ref[n] * rows, rows)
        field_ref[pl.ds(at, rows), :] = ref[:rows, :]
        field_ref[pl.ds(half + at, rows), :] = ref[rows : 2 * rows, :]
        if n < count:
            for k in range(6):
                line = ref[2 * rows + k * tiles : 2 * rows + (k + 1) * tiles, :]
                target = state_ref.at[k] if k < 2 else cells_ref.at[k - 2]
                target[n * tiles : (n + 1) * tiles, :] = line
    gather_tiles(field_ref, cells_ref, high_ref, low_ref, amp_ref)


def gather_kernel(
    fresh_ref, old_ref, own_ref, other_ref, kx_ref, ky_ref, cells_ref, field_ref, amp_ref, high_ref, low_ref
):
    half = field_ref.shape[0] // 2
    total = old_ref[...] + current_gain * (own_ref[...] + other_ref[...])
    moved = propagate(total, kx_ref[...].reshape(2 * half, half), ky_ref)
    field_ref[...] = jnp.where(fresh_ref[0] == 1, 0.0, moved)
    gather_tiles(field_ref, cells_ref, high_ref, low_ref, amp_ref)


def push_kernel(amp_ref, state_ref, cells_ref, current_ref, out_ref, cos_ref, sin_ref):
    half = current_ref.shape[0] // 2
    columns = current_ref.shape[1]
    phase = state_ref[0]
    energy = state_ref[1] - coupling * (amp_ref[0] * jnp.cos(phase) - amp_ref[1] * jnp.sin(phase))
    phase = phase + phase_step * energy
    out_ref[0] = phase
    out_ref[1] = energy
    cos_ref[...] = jnp.cos(phase)
    sin_ref[...] = -jnp.sin(phase)
    current_ref[...] = jnp.zeros_like(current_ref)
    tiles = cells_ref.shape[1]
    batch = math.gcd(tiles, BATCH)

    def weights(t):
        row = lambda n: cells_ref[n, pl.ds(t, 1), :]
        wy = place_split(cell_masks(columns, row(1)), 1.0 - row(3), row(3))
        masks = cell_masks(half, row(0))
        parts = []
        for ref in (cos_ref, sin_ref):
            value = ref[pl.ds(t, 1), :]
            parts.append(place_split(masks, (1.0 - row(2)) * value, row(2) * value))
        return wy, tuple(jnp.concatenate(pair, axis=0) for pair in zip(*parts))

    def body(n, carry):
        built = [weights(n * batch + k) for k in range(batch)]
        join = lambda side, part: jnp.concatenate([item[side][part] for item in built], axis=1)
        wy = join(0, 0), join(0, 1)
        values = join(1, 0), join(1, 1)
        current_ref[...] += dot3(values, wy, dot_t)
        return carry

    lax.fori_loop(0, tiles // batch, body, 0)


def last_kernel(where_ref, old_ref, own_ref, other_ref, kx_ref, ky_ref, rows_ref):
    count, rows = rows_ref.shape[0], rows_ref.shape[1] // 2
    total = old_ref[...] + current_gain * (own_ref[...] + other_ref[...])
    starts = [pl.multiple_of(where_ref[n] * rows, rows) for n in range(count)]
    block = jnp.concatenate([kx_ref[part, pl.ds(at, rows), :] for part in (0, 1) for at in starts], axis=0)
    moved = propagate(total, block, ky_ref)
    for n in range(count):
        rows_ref[n, :rows] = moved[n * rows : (n + 1) * rows]
        rows_ref[n, rows:] = moved[(count + n) * rows : (count + n + 1) * rows]


vmem = pl.BlockSpec(memory_space=pltpu.VMEM)
smem = pl.BlockSpec(memory_space=pltpu.SMEM)


def call(kernel, inputs, outs, scratch, flops):
    shapes = [jax.ShapeDtypeStruct(shape, f32) for shape in outs]
    moved = sum(4 * array.size for array in inputs) + sum(4 * shape.size for shape in shapes)
    return pl.pallas_call(
        kernel,
        out_shape=shapes,
        in_specs=[smem if array.dtype == jnp.int32 else vmem for array in inputs],
        out_specs=[vmem] * len(outs),
        scratch_shapes=scratch,
        compiler_params=pltpu.CompilerParams(vmem_limit_bytes=VMEM_LIMIT),
        cost_estimate=pl.CostEstimate(flops=flops, bytes_accessed=moved, transcendentals=0),
    )(*inputs)


def shards(radiation, electrons, cell_index, cell_offset, kernel_x, kernel_y):
    cuts, dom = lax.axis_size("cuts"), lax.axis_size("dom")
    rows, slices, _ = radiation.shape
    half = kernel_x.shape[1]
    columns = kernel_y.shape[1]
    team = dom // slices
    groups = cuts * slices
    me = lax.axis_index("dom")
    mine = me // team
    cut = lax.axis_index("cuts")

    def seat(cut, number):
        return (1 - cut % 2) * number + (cut % 2) * (slices - 1 - number)

    def number(cut, team_number):
        return cut * slices + seat(cut, team_number)

    group = number(cut, mine)
    tiles = electrons.shape[2] // TILE

    def move(value, target):
        route = []
        for cut in range(cuts):
            for place in range(dom):
                to_cut, to_place = target(cut, place)
                route.append((cut * dom + place, to_cut * dom + to_place))
        return lax.ppermute(value, ("cuts", "dom"), route)

    def pick(array, which):
        return lax.dynamic_index_in_dim(array, which, 0, keepdims=False)

    def to_group(shift, turn=0):
        def target(cut, place):
            home = (number(cut, place // team) + shift) % groups
            return home // slices, seat(home // slices, (home + turn) % slices) * team + place % team

        return target

    def across(value):
        return move(value, lambda cut, place: (cut, place ^ 1))

    parts = jnp.concatenate([electrons, cell_index.astype(f32), cell_offset], axis=0)
    parts = parts.transpose(1, 0, 2).reshape(slices, 6 * tiles, TILE)
    fields = jnp.concatenate([radiation[:, :, :columns], radiation[:, :, columns:]], axis=0).transpose(1, 0, 2)
    payload = jnp.concatenate([fields, parts], axis=1)
    masks = range(0, dom, 2)
    own_blocks = []
    for mask in masks:
        block = pick(payload, seat(cut, (me ^ mask) // team))
        if mask:
            block = move(block, lambda cut, place: (cut, place ^ mask))
        own_blocks.append(block)
    other_blocks = [across(block[: 2 * rows]) for block in own_blocks]
    where = jnp.stack([me ^ mask for mask in masks] + [me ^ 1 ^ mask for mask in masks]).astype(jnp.int32)

    field_shape = (2 * half, columns)
    state_shape = (2, len(masks) * tiles, TILE)
    cells_shape = (4,) + state_shape[1:]
    splits = [pltpu.VMEM(field_shape, bf16)] * 2
    work = 6 * 2 * half * columns * state_shape[1] * TILE
    field, amp, state, cells = call(
        first_kernel,
        [where] + own_blocks + other_blocks,
        [field_shape, state_shape, state_shape, cells_shape],
        splits,
        work,
    )
    cells_of = [cells]
    for step in range(ITERS):
        if step > 0:
            fresh = ((group + step) % groups == 0).astype(jnp.int32).reshape(1)
            field, amp = call(
                gather_kernel,
                [fresh, field, own, other, kernel_x, kernel_y, cells_of[step]],
                [field_shape, state_shape],
                splits,
                work,
            )
        own, state = call(
            push_kernel,
            [amp, state, cells_of[step]],
            [field_shape, state_shape],
            [pltpu.VMEM(state_shape[1:], f32)] * 2,
            work,
        )
        other = across(own)
        if step == 0:
            cells, _ = lax.optimization_barrier((cells, state))
            for later in range(1, ITERS):
                cells_of.append(move(cells, to_group(-later)))
        if step < ITERS - 1:
            state = move(state, to_group(-1))

    def places(home):
        return [seat(home // slices, (home + turn) % slices) * team + me % team for turn in range(slices)]

    field_home = (group + ITERS) % groups
    (blocks,) = call(
        last_kernel,
        [jnp.stack(places(field_home)).astype(jnp.int32), field, own, other, kernel_x, kernel_y],
        [(slices, 2 * rows, columns)],
        [],
        work // 16,
    )
    blocks, state = lax.optimization_barrier((blocks, state))
    landed = []
    for turn in range(slices):
        landed.append(move(blocks[turn], to_group(ITERS, turn)))
    state_home = (group + ITERS - 1) % groups
    seats = places(state_home)
    returned = []
    for turn in range(slices):
        chunk = (seats[turn] ^ seats[0]) // 2
        block = lax.dynamic_slice_in_dim(state, chunk * tiles, tiles, 1)
        returned.append(move(block, to_group(ITERS - 1, turn)))
    order = [(seat(cut, mine) - number) % slices for number in range(slices)]
    landed = jnp.stack(landed)
    landed = [pick(landed, which) for which in order]
    returned = jnp.stack(returned)
    returned = [pick(returned, which).reshape(2, tiles * TILE) for which in order]
    landed[0] = jnp.where(cut == 0, 0.0, landed[0])
    radiation_out = jnp.stack([jnp.concatenate([block[:rows], block[rows:]], axis=1) for block in landed], axis=1)
    return radiation_out, jnp.stack(returned, axis=1)


def solution(mesh):
    placed = (
        P("dom", "cuts", None),
        P(None, "cuts", "dom"),
        P(None, "cuts", "dom"),
        P(None, "cuts", "dom"),
        P(),
        P(),
    )

    return jax.shard_map(
        shards,
        mesh=mesh,
        in_specs=placed,
        out_specs=(P("dom", "cuts", None), P(None, "cuts", "dom")),
        check_vma=False,
    )
```

profile of v0, /device:TPU:0, one launch (start us, length us, event | category | flops | bytes accessed | tf_op | source)
XLA Modules:
  0.0 127.8 jit_solution(11226045916120707284)
XLA Ops:
  0.8 0.8 copy-done.4
  3.4 3.0 %collective-permute-start = (f32[112,256]{1,0:T(8,128)S(1)}, f32[112,256]{1,0:T(8,128)S(1)}, u32[]{:S(2)}, u32[]{:S(2)}) collective-permute-start(f32[112,256]{1,0:T(8,128)S(1)} %get-tuple-element.50), channel_id=1, source_target_pairs={{0,2},{1,3},{2,0},{3,1},{4,6},{5,7},{6,4},{7,5},{8,10},{9,11},{10,... | collective-permute-start | bytes 344072 | tf_op jit(solution)/shard_map/ppermute | solution.py:212
  6.4 1.5 %collective-permute-start.1 = (f32[112,256]{1,0:T(8,128)S(1)}, f32[112,256]{1,0:T(8,128)S(1)}, u32[]{:S(2)}, u32[]{:S(2)}) collective-permute-start(f32[112,256]{1,0:T(8,128)S(1)} %get-tuple-element.51), channel_id=1, source_target_pairs={{0,4},{1,5},{2,6},{3,7},{4,0},{5,1},{6,2},{7,3},{8,12},{9,13},{10,... | collective-permute-start | bytes 344072 | tf_op jit(solution)/shard_map/ppermute | solution.py:212
  8.0 1.9 %collective-permute-done.refs_1_ = f32[112,256]{1,0:T(8,128)S(1)} collective-permute-done((f32[112,256]{1,0:T(8,128)S(1)}, f32[112,256]{1,0:T(8,128)S(1)}, u32[]{:S(2)}, u32[]{:S(2)}) %collective-permute-start) | collective-permute-done | bytes 114720 | tf_op jit(solution)/shard_map/ppermute | solution.py:212
  9.9 3.7 %collective-permute-done.1.refs_2_ = f32[112,256]{1,0:T(8,128)S(1)} collective-permute-done((f32[112,256]{1,0:T(8,128)S(1)}, f32[112,256]{1,0:T(8,128)S(1)}, u32[]{:S(2)}, u32[]{:S(2)}) %collective-permute-start.1) | collective-permute-done | bytes 114720 | tf_op jit(solution)/shard_map/ppermute | solution.py:212
  15.1 8.1 %shard_map.77 = (f32[512,256]{1,0:T(8,128)S(1)}, f32[2,32,256]{2,1,0:T(8,128)S(1)}, f32[2,32,256]{2,1,0:T(8,128)S(1)}, f32[4,32,256]{2,1,0:T(8,128)S(1)}) custom-call(s32[8]{0:T(128)S(1)} %stack.77.where_ref, f32[112,256]{1,0:T(8,128)S(1)} %bitcast.50, f32[112,256]{1,0:T(8,128)S(1)} %collective-permute-done.refs_1_, ...), custom_call_target="tpu_custom_call" | custom-call | flops 6442450944 | bytes 1507360 | tf_op jit(solution)/shard_map/pallas_call | solution.py:175
  23.3 7.8 %shard_map.78 = (f32[512,256]{1,0:T(8,128)S(1)}, f32[2,32,256]{2,1,0:T(8,128)S(1)}) custom-call(f32[2,32,256]{2,1,0:T(8,128)S(1)} %get-tuple-element.24.amp_ref, f32[2,32,256]{2,1,0:T(8,128)S(1)} %get-tuple-element.25.state_ref, f32[4,32,256]{2,1,0:T(8,128)S(1)} %get-tuple-element.29.cells_ref), custom_call_target="tpu_custom_call" | custom-call | flops 6442450944 | bytes 851968 | tf_op jit(solution)/shard_map/pallas_call | solution.py:175
  31.5 3.6 %collective-permute-start.8 = (f32[4,32,256]{2,1,0:T(8,128)S(1)}, f32[4,32,256]{2,1,0:T(8,128)S(1)}, u32[]{:S(2)}, u32[]{:S(2)}) collective-permute-start(f32[4,32,256]{2,1,0:T(8,128)S(1)} %get-tuple-element.29.cells_ref), channel_id=1, source_target_pairs={{0,24},{1,25},{2,26},{3,27},{4,0},{5,1},{6,2},{7,3},{8,12},{9,13},... | collective-permute-start | bytes 393224 | tf_op jit(solution)/shard_map/ppermute | solution.py:212
  35.1 1.3 %collective-permute-start.9 = (f32[2,32,256]{2,1,0:T(8,128)S(1)}, f32[2,32,256]{2,1,0:T(8,128)S(1)}, u32[]{:S(2)}, u32[]{:S(2)}) collective-permute-start(f32[2,32,256]{2,1,0:T(8,128)S(1)} %get-tuple-element.28), channel_id=1, source_target_pairs={{0,24},{1,25},{2,26},{3,27},{4,0},{5,1},{6,2},{7,3},{8,12},{9,13},... | collective-permute-start | bytes 196616 | tf_op jit(solution)/shard_map/ppermute | solution.py:212
  36.4 2.4 %collective-permute-done.8.cells_ref = f32[4,32,256]{2,1,0:T(8,128)S(1)} collective-permute-done((f32[4,32,256]{2,1,0:T(8,128)S(1)}, f32[4,32,256]{2,1,0:T(8,128)S(1)}, u32[]{:S(2)}, u32[]{:S(2)}) %collective-permute-start.8) | collective-permute-done | bytes 131104 | tf_op jit(solution)/shard_map/ppermute | solution.py:212
  38.9 9.2 %shard_map.79 = (f32[512,256]{1,0:T(8,128)S(1)}, f32[2,32,256]{2,1,0:T(8,128)S(1)}) custom-call(s32[1]{0:T(128)} %bitcast.4.fresh_ref, f32[512,256]{1,0:T(8,128)S(1)} %get-tuple-element.23.old_ref, f32[512,256]{1,0:T(8,128)S(1)} %get-tuple-element.27.own_ref, f32[512,256]{1,0:T(8,128)S(1)} %collective-permute-done.7.other_ref, f32[2,256,256]{2,1,0:T(8,128)S(1)} %copy-done, ...), custom_call_target="tpu_custom_call" | custom-call | flops 6442450944 | bytes 3342340 | tf_op jit(solution)/shard_map/pallas_call | solution.py:175
  48.1 0.8 copy-done.2
  48.9 7.8 %shard_map.80 = (f32[512,256]{1,0:T(8,128)S(1)}, f32[2,32,256]{2,1,0:T(8,128)S(1)}) custom-call(f32[2,32,256]{2,1,0:T(8,128)S(1)} %get-tuple-element.31.amp_ref, f32[2,32,256]{2,1,0:T(8,128)S(1)} %collective-permute-done.9.state_ref, f32[4,32,256]{2,1,0:T(8,128)S(1)} %collective-permute-done.8.cells_ref), custom_call_target="tpu_custom_call" | custom-call | flops 6442450944 | bytes 851968 | tf_op jit(solution)/shard_map/pallas_call | solution.py:175
  56.7 3.3 %collective-permute-start.11 = (f32[4,32,256]{2,1,0:T(8,128)S(1)}, f32[4,32,256]{2,1,0:T(8,128)S(1)}, u32[]{:S(2)}, u32[]{:S(2)}) collective-permute-start(f32[4,32,256]{2,1,0:T(8,128)S(1)} %get-tuple-element.29.cells_ref), channel_id=1, source_target_pairs={{0,28},{1,29},{2,30},{3,31},{4,24},{5,25},{6,26},{7,27},{8,4},{9,5... | collective-permute-start | bytes 393224 | tf_op jit(solution)/shard_map/ppermute | solution.py:212
  60.1 1.3 %collective-permute-start.12 = (f32[2,32,256]{2,1,0:T(8,128)S(1)}, f32[2,32,256]{2,1,0:T(8,128)S(1)}, u32[]{:S(2)}, u32[]{:S(2)}) collective-permute-start(f32[2,32,256]{2,1,0:T(8,128)S(1)} %get-tuple-element.35), channel_id=1, source_target_pairs={{0,24},{1,25},{2,26},{3,27},{4,0},{5,1},{6,2},{7,3},{8,12},{9,13},... | collective-permute-start | bytes 196616 | tf_op jit(solution)/shard_map/ppermute | solution.py:212
  61.4 2.6 %collective-permute-done.11.cells_ref = f32[4,32,256]{2,1,0:T(8,128)S(1)} collective-permute-done((f32[4,32,256]{2,1,0:T(8,128)S(1)}, f32[4,32,256]{2,1,0:T(8,128)S(1)}, u32[]{:S(2)}, u32[]{:S(2)}) %collective-permute-start.11) | collective-permute-done | bytes 131104 | tf_op jit(solution)/shard_map/ppermute | solution.py:212
  64.0 1.0 copy-done.3
  65.0 9.2 %shard_map.81 = (f32[512,256]{1,0:T(8,128)S(1)}, f32[2,32,256]{2,1,0:T(8,128)S(1)}) custom-call(s32[1]{0:T(128)} %bitcast.3.fresh_ref, f32[512,256]{1,0:T(8,128)S(1)} %copy-done.3, f32[512,256]{1,0:T(8,128)S(1)} %get-tuple-element.32.own_ref, f32[512,256]{1,0:T(8,128)S(1)} %collective-permute-done.10.other_ref, f32[2,256,256]{2,1,0:T(8,128)S(1)} %copy-done, ...), custom_call_target="tpu_custom_call" | custom-call | flops 6442450944 | bytes 3342340 | tf_op jit(solution)/shard_map/pallas_call | solution.py:175
  74.2 7.8 %shard_map.82 = (f32[512,256]{1,0:T(8,128)S(1)}, f32[2,32,256]{2,1,0:T(8,128)S(1)}) custom-call(f32[2,32,256]{2,1,0:T(8,128)S(1)} %get-tuple-element.34.amp_ref, f32[2,32,256]{2,1,0:T(8,128)S(1)} %collective-permute-done.12.state_ref, f32[4,32,256]{2,1,0:T(8,128)S(1)} %collective-permute-done.11.cells_ref), custom_call_target="tpu_custom_call" | custom-call | flops 6442450944 | bytes 851968 | tf_op jit(solution)/shard_map/pallas_call | solution.py:175
  82.1 2.8 %collective-permute-start.14 = (f32[4,32,256]{2,1,0:T(8,128)S(1)}, f32[4,32,256]{2,1,0:T(8,128)S(1)}, u32[]{:S(2)}, u32[]{:S(2)}) collective-permute-start(f32[4,32,256]{2,1,0:T(8,128)S(1)} %get-tuple-element.29.cells_ref), channel_id=1, source_target_pairs={{0,20},{1,21},{2,22},{3,23},{4,28},{5,29},{6,30},{7,31},{8,0},{9,1... | collective-permute-start | bytes 393224 | tf_op jit(solution)/shard_map/ppermute | solution.py:212
  84.9 3.1 %collective-permute-start.15 = (f32[2,32,256]{2,1,0:T(8,128)S(1)}, f32[2,32,256]{2,1,0:T(8,128)S(1)}, u32[]{:S(2)}, u32[]{:S(2)}) collective-permute-start(f32[2,32,256]{2,1,0:T(8,128)S(1)} %get-tuple-element.39), channel_id=1, source_target_pairs={{0,24},{1,25},{2,26},{3,27},{4,0},{5,1},{6,2},{7,3},{8,12},{9,13},... | collective-permute-start | bytes 196616 | tf_op jit(solution)/shard_map/ppermute | solution.py:212
  87.9 2.8 %collective-permute-done.14.cells_ref = f32[4,32,256]{2,1,0:T(8,128)S(1)} collective-permute-done((f32[4,32,256]{2,1,0:T(8,128)S(1)}, f32[4,32,256]{2,1,0:T(8,128)S(1)}, u32[]{:S(2)}, u32[]{:S(2)}) %collective-permute-start.14) | collective-permute-done | bytes 131104 | tf_op jit(solution)/shard_map/ppermute | solution.py:212
  90.8 9.2 %shard_map.83 = (f32[512,256]{1,0:T(8,128)S(1)}, f32[2,32,256]{2,1,0:T(8,128)S(1)}) custom-call(s32[1]{0:T(128)} %bitcast.2.fresh_ref, f32[512,256]{1,0:T(8,128)S(1)} %get-tuple-element.33.old_ref, f32[512,256]{1,0:T(8,128)S(1)} %get-tuple-element.36.own_ref, f32[512,256]{1,0:T(8,128)S(1)} %collective-permute-done.13.other_ref, f32[2,256,256]{2,1,0:T(8,128)S(1)} %copy-done, ...), custom_call_target="tpu_custom_call" | custom-call | flops 6442450944 | bytes 3342340 | tf_op jit(solution)/shard_map/pallas_call | solution.py:175
  100.0 7.8 %shard_map.84 = (f32[512,256]{1,0:T(8,128)S(1)}, f32[2,32,256]{2,1,0:T(8,128)S(1)}) custom-call(f32[2,32,256]{2,1,0:T(8,128)S(1)} %get-tuple-element.38.amp_ref, f32[2,32,256]{2,1,0:T(8,128)S(1)} %collective-permute-done.15.state_ref, f32[4,32,256]{2,1,0:T(8,128)S(1)} %collective-permute-done.14.cells_ref), custom_call_target="tpu_custom_call" | custom-call | flops 6442450944 | bytes 851968 | tf_op jit(solution)/shard_map/pallas_call | solution.py:175
  108.2 1.6 %collective-permute-done.16.other_ref = f32[512,256]{1,0:T(8,128)S(1)} collective-permute-done((f32[512,256]{1,0:T(8,128)S(1)}, f32[512,256]{1,0:T(8,128)S(1)}, u32[]{:S(2)}, u32[]{:S(2)}) %collective-permute-start.16) | collective-permute-done | bytes 524320 | tf_op jit(solution)/shard_map/ppermute | solution.py:212
  109.8 1.2 shard_map.85
  111.0 1.6 %collective-permute-start.19 = (f32[2,8,256]{2,1,0:T(8,128)S(1)}, f32[2,8,256]{2,1,0:T(8,128)S(1)}, u32[]{:S(2)}, u32[]{:S(2)}) collective-permute-start(f32[2,8,256]{2,1,0:T(8,128)S(1)} %get-tuple-element.59), channel_id=1, source_target_pairs={{0,8},{1,9},{2,10},{3,11},{4,16},{5,17},{6,18},{7,19},{8,28},{9,29... | collective-permute-start | bytes 49160 | tf_op jit(solution)/shard_map/ppermute | solution.py:212
  112.6 2.8 %collective-permute-start.20 = (f32[2,8,256]{2,1,0:T(8,128)S(1)}, f32[2,8,256]{2,1,0:T(8,128)S(1)}, u32[]{:S(2)}, u32[]{:S(2)}) collective-permute-start(f32[2,8,256]{2,1,0:T(8,128)S(1)} %get-tuple-element.58), channel_id=1, source_target_pairs={{0,12},{1,13},{2,14},{3,15},{4,20},{5,21},{6,22},{7,23},{8,24},{9,... | collective-permute-start | bytes 49160 | tf_op jit(solution)/shard_map/ppermute | solution.py:212
  115.4 3.4 %collective-permute-start.17 = (f32[64,256]{1,0:T(8,128)S(1)}, f32[64,256]{1,0:T(8,128)S(1)}, u32[]{:S(2)}, u32[]{:S(2)}) collective-permute-start(f32[64,256]{1,0:T(8,128)S(1)} %get-tuple-element.55), channel_id=1, source_target_pairs={{0,16},{1,17},{2,18},{3,19},{4,20},{5,21},{6,22},{7,23},{8,24},{9,... | collective-permute-start | bytes 196616 | tf_op jit(solution)/shard_map/ppermute | solution.py:212
  119.8 1.9 %collective-permute-done.17 = f32[64,256]{1,0:T(8,128)S(1)} collective-permute-done((f32[64,256]{1,0:T(8,128)S(1)}, f32[64,256]{1,0:T(8,128)S(1)}, u32[]{:S(2)}, u32[]{:S(2)}) %collective-permute-start.17) | collective-permute-done | bytes 65568 | tf_op jit(solution)/shard_map/ppermute | solution.py:212
  121.7 5.2 %collective-permute-done.18 = f32[64,256]{1,0:T(8,128)S(1)} collective-permute-done((f32[64,256]{1,0:T(8,128)S(1)}, f32[64,256]{1,0:T(8,128)S(1)}, u32[]{:S(2)}, u32[]{:S(2)}) %collective-permute-start.18) | collective-permute-done | bytes 65568 | tf_op jit(solution)/shard_map/ppermute | solution.py:212
  127.0 0.8 copy.15
  (63 shorter events, 5.2 us)
Async XLA Ops:
  0.6 0.9 copy-start.4
  1.6 0.8 copy-start.5
  2.3 0.8 copy-start.6
  2.3 0.8 copy-start.7
  3.4 6.6 %collective-permute-start = (f32[112,256]{1,0:T(8,128)S(1)}, f32[112,256]{1,0:T(8,128)S(1)}, u32[]{:S(2)}, u32[]{:S(2)}) collective-permute-start(f32[112,256]{1,0:T(8,128)S(1)} %get-tuple-element.50), channel_id=1, source_target_pairs={{0,2},{1,3},{2,0},{3,1},{4,6},{5,7},{6,4},{7,5},{8,10},{9,11},{10,... | collective-permute-start | bytes 344072 | tf_op jit(solution)/shard_map/ppermute | solution.py:212
  6.4 7.2 %collective-permute-start.1 = (f32[112,256]{1,0:T(8,128)S(1)}, f32[112,256]{1,0:T(8,128)S(1)}, u32[]{:S(2)}, u32[]{:S(2)}) collective-permute-start(f32[112,256]{1,0:T(8,128)S(1)} %get-tuple-element.51), channel_id=1, source_target_pairs={{0,4},{1,5},{2,6},{3,7},{4,0},{5,1},{6,2},{7,3},{8,12},{9,13},{10,... | collective-permute-start | bytes 344072 | tf_op jit(solution)/shard_map/ppermute | solution.py:212
  7.9 5.7 %collective-permute-start.2 = (f32[112,256]{1,0:T(8,128)S(1)}, f32[112,256]{1,0:T(8,128)S(1)}, u32[]{:S(2)}, u32[]{:S(2)}) collective-permute-start(f32[112,256]{1,0:T(8,128)S(1)} %get-tuple-element.48), channel_id=1, source_target_pairs={{0,6},{1,7},{2,4},{3,5},{4,2},{5,3},{6,0},{7,1},{8,14},{9,15},{10,... | collective-permute-start | bytes 344072 | tf_op jit(solution)/shard_map/ppermute | solution.py:212
  7.9 6.4 %collective-permute-start.3 = (f32[64,256]{1,0:T(8,128)S(1)}, f32[64,256]{1,0:T(8,128)S(1)}, u32[]{:S(2)}, u32[]{:S(2)}) collective-permute-start(f32[64,256]{1,0:T(8,128)S(1)} %slice_bitcast_fusion), channel_id=1, source_target_pairs={{0,1},{1,0},{2,3},{3,2},{4,5},{5,4},{6,7},{7,6},{8,9},{9,8},{10,11... | collective-permute-start | bytes 196616 | tf_op jit(solution)/shard_map/ppermute | solution.py:212
  9.9 4.4 %collective-permute-start.4 = (f32[64,256]{1,0:T(8,128)S(1)}, f32[64,256]{1,0:T(8,128)S(1)}, u32[]{:S(2)}, u32[]{:S(2)}) collective-permute-start(f32[64,256]{1,0:T(8,128)S(1)} %slice.70), channel_id=1, source_target_pairs={{0,1},{1,0},{2,3},{3,2},{4,5},{5,4},{6,7},{7,6},{8,9},{9,8},{10,11... | collective-permute-start | bytes 196616 | tf_op jit(solution)/shard_map/ppermute | solution.py:212
  13.7 1.3 collective-permute-start.5
  13.7 1.5 %collective-permute-start.6 = (f32[64,256]{1,0:T(8,128)S(1)}, f32[64,256]{1,0:T(8,128)S(1)}, u32[]{:S(2)}, u32[]{:S(2)}) collective-permute-start(f32[64,256]{1,0:T(8,128)S(1)} %slice.72), channel_id=1, source_target_pairs={{0,1},{1,0},{2,3},{3,2},{4,5},{5,4},{6,7},{7,6},{8,9},{9,8},{10,11... | collective-permute-start | bytes 196616 | tf_op jit(solution)/shard_map/ppermute | solution.py:212
  23.2 15.6 %copy-start = (f32[2,256,256]{2,1,0:T(8,128)S(1)}, f32[2,256,256]{2,1,0:T(8,128)}, u32[]{:S(2)}) copy-start(f32[2,256,256]{2,1,0:T(8,128)} %kx_ref.7) | copy-start | bytes 1572868
  23.3 15.6 %copy-start.1 = (f32[2,256,256]{2,1,0:T(8,128)S(1)}, f32[2,256,256]{2,1,0:T(8,128)}, u32[]{:S(2)}) copy-start(f32[2,256,256]{2,1,0:T(8,128)} %ky_ref.7) | copy-start | bytes 1572868
  31.1 7.8 %collective-permute-start.7 = (f32[512,256]{1,0:T(8,128)S(1)}, f32[512,256]{1,0:T(8,128)S(1)}, u32[]{:S(2)}, u32[]{:S(2)}) collective-permute-start(f32[512,256]{1,0:T(8,128)S(1)} %get-tuple-element.27.own_ref), channel_id=1, source_target_pairs={{0,1},{1,0},{2,3},{3,2},{4,5},{5,4},{6,7},{7,6},{8,9},{9,8},{10,11... | collective-permute-start | bytes 1572872 | tf_op jit(solution)/shard_map/ppermute | solution.py:212
  31.5 7.4 %collective-permute-start.8 = (f32[4,32,256]{2,1,0:T(8,128)S(1)}, f32[4,32,256]{2,1,0:T(8,128)S(1)}, u32[]{:S(2)}, u32[]{:S(2)}) collective-permute-start(f32[4,32,256]{2,1,0:T(8,128)S(1)} %get-tuple-element.29.cells_ref), channel_id=1, source_target_pairs={{0,24},{1,25},{2,26},{3,27},{4,0},{5,1},{6,2},{7,3},{8,12},{9,13},... | collective-permute-start | bytes 393224 | tf_op jit(solution)/shard_map/ppermute | solution.py:212
  35.1 13.8 %collective-permute-start.9 = (f32[2,32,256]{2,1,0:T(8,128)S(1)}, f32[2,32,256]{2,1,0:T(8,128)S(1)}, u32[]{:S(2)}, u32[]{:S(2)}) collective-permute-start(f32[2,32,256]{2,1,0:T(8,128)S(1)} %get-tuple-element.28), channel_id=1, source_target_pairs={{0,24},{1,25},{2,26},{3,27},{4,0},{5,1},{6,2},{7,3},{8,12},{9,13},... | collective-permute-start | bytes 196616 | tf_op jit(solution)/shard_map/ppermute | solution.py:212
  48.1 0.8 copy-start.2
  56.7 7.3 %collective-permute-start.10 = (f32[512,256]{1,0:T(8,128)S(1)}, f32[512,256]{1,0:T(8,128)S(1)}, u32[]{:S(2)}, u32[]{:S(2)}) collective-permute-start(f32[512,256]{1,0:T(8,128)S(1)} %get-tuple-element.32.own_ref), channel_id=1, source_target_pairs={{0,1},{1,0},{2,3},{3,2},{4,5},{5,4},{6,7},{7,6},{8,9},{9,8},{10,11... | collective-permute-start | bytes 1572872 | tf_op jit(solution)/shard_map/ppermute | solution.py:212
  56.7 7.2 %collective-permute-start.11 = (f32[4,32,256]{2,1,0:T(8,128)S(1)}, f32[4,32,256]{2,1,0:T(8,128)S(1)}, u32[]{:S(2)}, u32[]{:S(2)}) collective-permute-start(f32[4,32,256]{2,1,0:T(8,128)S(1)} %get-tuple-element.29.cells_ref), channel_id=1, source_target_pairs={{0,28},{1,29},{2,30},{3,31},{4,24},{5,25},{6,26},{7,27},{8,4},{9,5... | collective-permute-start | bytes 393224 | tf_op jit(solution)/shard_map/ppermute | solution.py:212
  60.1 14.2 %collective-permute-start.12 = (f32[2,32,256]{2,1,0:T(8,128)S(1)}, f32[2,32,256]{2,1,0:T(8,128)S(1)}, u32[]{:S(2)}, u32[]{:S(2)}) collective-permute-start(f32[2,32,256]{2,1,0:T(8,128)S(1)} %get-tuple-element.35), channel_id=1, source_target_pairs={{0,24},{1,25},{2,26},{3,27},{4,0},{5,1},{6,2},{7,3},{8,12},{9,13},... | collective-permute-start | bytes 196616 | tf_op jit(solution)/shard_map/ppermute | solution.py:212
  63.9 1.0 copy-start.3
  82.0 8.7 %collective-permute-start.13 = (f32[512,256]{1,0:T(8,128)S(1)}, f32[512,256]{1,0:T(8,128)S(1)}, u32[]{:S(2)}, u32[]{:S(2)}) collective-permute-start(f32[512,256]{1,0:T(8,128)S(1)} %get-tuple-element.36.own_ref), channel_id=1, source_target_pairs={{0,1},{1,0},{2,3},{3,2},{4,5},{5,4},{6,7},{7,6},{8,9},{9,8},{10,11... | collective-permute-start | bytes 1572872 | tf_op jit(solution)/shard_map/ppermute | solution.py:212
  82.1 8.6 %collective-permute-start.14 = (f32[4,32,256]{2,1,0:T(8,128)S(1)}, f32[4,32,256]{2,1,0:T(8,128)S(1)}, u32[]{:S(2)}, u32[]{:S(2)}) collective-permute-start(f32[4,32,256]{2,1,0:T(8,128)S(1)} %get-tuple-element.29.cells_ref), channel_id=1, source_target_pairs={{0,20},{1,21},{2,22},{3,23},{4,28},{5,29},{6,30},{7,31},{8,0},{9,1... | collective-permute-start | bytes 393224 | tf_op jit(solution)/shard_map/ppermute | solution.py:212
  84.9 15.1 %collective-permute-start.15 = (f32[2,32,256]{2,1,0:T(8,128)S(1)}, f32[2,32,256]{2,1,0:T(8,128)S(1)}, u32[]{:S(2)}, u32[]{:S(2)}) collective-permute-start(f32[2,32,256]{2,1,0:T(8,128)S(1)} %get-tuple-element.39), channel_id=1, source_target_pairs={{0,24},{1,25},{2,26},{3,27},{4,0},{5,1},{6,2},{7,3},{8,12},{9,13},... | collective-permute-start | bytes 196616 | tf_op jit(solution)/shard_map/ppermute | solution.py:212
  107.8 2.0 %collective-permute-start.16 = (f32[512,256]{1,0:T(8,128)S(1)}, f32[512,256]{1,0:T(8,128)S(1)}, u32[]{:S(2)}, u32[]{:S(2)}) collective-permute-start(f32[512,256]{1,0:T(8,128)S(1)} %get-tuple-element.40.own_ref), channel_id=1, source_target_pairs={{0,1},{1,0},{2,3},{3,2},{4,5},{5,4},{6,7},{7,6},{8,9},{9,8},{10,11... | collective-permute-start | bytes 1572872 | tf_op jit(solution)/shard_map/ppermute | solution.py:212
  111.0 7.7 %collective-permute-start.19 = (f32[2,8,256]{2,1,0:T(8,128)S(1)}, f32[2,8,256]{2,1,0:T(8,128)S(1)}, u32[]{:S(2)}, u32[]{:S(2)}) collective-permute-start(f32[2,8,256]{2,1,0:T(8,128)S(1)} %get-tuple-element.59), channel_id=1, source_target_pairs={{0,8},{1,9},{2,10},{3,11},{4,16},{5,17},{6,18},{7,19},{8,28},{9,29... | collective-permute-start | bytes 49160 | tf_op jit(solution)/shard_map/ppermute | solution.py:212
  112.6 6.5 %collective-permute-start.20 = (f32[2,8,256]{2,1,0:T(8,128)S(1)}, f32[2,8,256]{2,1,0:T(8,128)S(1)}, u32[]{:S(2)}, u32[]{:S(2)}) collective-permute-start(f32[2,8,256]{2,1,0:T(8,128)S(1)} %get-tuple-element.58), channel_id=1, source_target_pairs={{0,12},{1,13},{2,14},{3,15},{4,20},{5,21},{6,22},{7,23},{8,24},{9,... | collective-permute-start | bytes 49160 | tf_op jit(solution)/shard_map/ppermute | solution.py:212
  115.4 6.3 %collective-permute-start.17 = (f32[64,256]{1,0:T(8,128)S(1)}, f32[64,256]{1,0:T(8,128)S(1)}, u32[]{:S(2)}, u32[]{:S(2)}) collective-permute-start(f32[64,256]{1,0:T(8,128)S(1)} %get-tuple-element.55), channel_id=1, source_target_pairs={{0,16},{1,17},{2,18},{3,19},{4,20},{5,21},{6,22},{7,23},{8,24},{9,... | collective-permute-start | bytes 196616 | tf_op jit(solution)/shard_map/ppermute | solution.py:212
  118.7 8.2 %collective-permute-start.18 = (f32[64,256]{1,0:T(8,128)S(1)}, f32[64,256]{1,0:T(8,128)S(1)}, u32[]{:S(2)}, u32[]{:S(2)}) collective-permute-start(f32[64,256]{1,0:T(8,128)S(1)} %get-tuple-element.54), channel_id=1, source_target_pairs={{0,20},{1,21},{2,22},{3,23},{4,16},{5,17},{6,18},{7,19},{8,28},{9,... | collective-permute-start | bytes 196616 | tf_op jit(solution)/shard_map/ppermute | solution.py:212
where the time goes:
time: 128 us
  Pallas kernels  68.1 us (53%)
  starting transfers between devices  28.9 us (23%)
  waiting for transfers between devices  23.3 us (18%)
  local copies, waits for them, and re-layouts  5.81 us (5%)
  between operations  1.35 us (1%)
    pallas_call x9, Pallas kernels, call(): pl.pallas_call(kernel, out_shape=shapes, in_specs=[smem if array.dtype ==...  68.1 us
    ppermute x21, starting transfers between devices, move(): return lax.ppermute(value, ('cuts', 'dom'), route)  28.9 us
    ppermute x21, waiting for transfers between devices, move(): return lax.ppermute(value, ('cuts', 'dom'), route)  23.3 us
    unnamed x20, local copies, waits for them, and re-layouts  5.52 us
  transfers between devices with their start and end apart: 21, of which 11 were waited for; matrix products, arithmetic and copies ran while one was open for 1% of the time, Pallas kernels for 22%

commit v1 on v0

--- a/solution.py
+++ b/solution.py
@@ -10,8 +10,10 @@
 
 ITERS = 4
 TILE = 256
-BATCH = 8
-VMEM_LIMIT = 20 * 2**20
+BATCH = 16
+CHOICES = 64
+REST = 1e-4
+VMEM_LIMIT = 16 * 2**20
 
 coupling = 0.5
 phase_step = 1.0
@@ -38,9 +40,40 @@
     return product(left[0], right[0]) + product(left[1], right[0]) + product(left[0], right[1])
 
 
-def tent(rows, index, offset):
+def dot2(left, right, product=dot):
+    return product(left[0], right) + product(left[1], right)
+
+
+def tent(rows, index, low, high):
     distance = lax.broadcasted_iota(jnp.int32, (rows, index.shape[1]), 0).astype(f32) - index
-    return jnp.where(distance == 0.0, 1.0 - offset, jnp.where(distance == 1.0, offset, 0.0))
+    return jnp.where(distance == 0.0, low, jnp.where(distance == 1.0, high, 0.0))
+
+
+def weight_pair(offset):
+    small = jnp.minimum(offset, 1.0 - offset)
+    ratio = small / jnp.maximum(offset, 1.0 - offset)
+    best = jnp.full_like(offset, 2.0)
+    large = jnp.ones_like(offset)
+    for n in range(CHOICES):
+        choice = 1.0 + n / CHOICES
+        other = choice * ratio
+        miss = jnp.abs(other.astype(bf16).astype(f32) - other) * (1.0 / choice)
+        large = jnp.where(miss < best, choice, large)
+        best = jnp.minimum(miss, best)
+    little = (large * ratio).astype(bf16).astype(f32)
+    swap = offset > 0.5
+    return jnp.where(swap, little, large), jnp.where(swap, large, little)
+
+
+def scale_and_rest(cells_ref, rest_ref):
+    offset, low, high = cells_ref[3], cells_ref[4], cells_ref[5]
+    scale = ((1.0 - offset) * low + offset * high) / (low * low + high * high)
+    rest_low = (1.0 - offset) - scale * low
+    rest_high = offset - scale * high
+    rest_ref[0] = rest_low / scale
+    rest_ref[1] = rest_high / scale
+    miss = jnp.sum(rest_low * rest_low + rest_high * rest_high)
+    return scale, miss > (REST * REST) * 0.5 * offset.size
 
 
 def complex_rows(real, imag):
@@ -67,32 +100,62 @@
     return jnp.where(masks[0], spread(low), jnp.where(masks[1], spread(high), jnp.zeros(masks[0].shape, low.dtype)))
 
 
-def place_split(masks, low, high):
-    return tuple(place(masks, *pair) for pair in zip(split(low), split(high)))
-
-
-def gather_tiles(field_ref, cells_ref, high_ref, low_ref, amp_ref):
+def gather_tiles(field_ref, cells_ref, high_ref, low_ref, wx_ref, rest_ref, amp_ref):
     half = field_ref.shape[0] // 2
     columns = field_ref.shape[1]
+    tiles = cells_ref.shape[1]
     high, low = split(field_ref[...])
     high_ref[...] = high
     low_ref[...] = low
+    scale, more = scale_and_rest(cells_ref, rest_ref)
+    wx_ref[0] = scale * (1.0 - cells_ref[2])
+    wx_ref[1] = scale * cells_ref[2]
+
+    def amplitude(t, out):
+        row = lambda ref, n: ref[n, pl.ds(t, 1), :]
+        wx = tent(half, row(cells_ref, 0), row(wx_ref, 0), row(wx_ref, 1))
+        return [jnp.sum(part * wx, axis=0, keepdims=True) for part in (out[:half], out[half:])]
+
+    def weights(t, low, high):
+        return place(cell_masks(columns, cells_ref[1, pl.ds(t, 1), :]), low.astype(bf16), high.astype(bf16))
 
     def body(t, carry):
-        row = lambda n: cells_ref[n, pl.ds(t, 1), :]
-        wy = place_split(cell_masks(columns, row(1)), 1.0 - row(3), row(3))
-        wx = tent(half, row(0), row(2))
-        out = dot3((high_ref[...], low_ref[...]), wy)
-        amp_ref[0, pl.ds(t, 1), :] = jnp.sum(out[:half] * wx, axis=0, keepdims=True)
-        amp_ref[1, pl.ds(t, 1), :] = jnp.sum(out[half:] * wx, axis=0, keepdims=True)
+        wy = weights(t, cells_ref[4, pl.ds(t, 1), :], cells_ref[5, pl.ds(t, 1), :])
+        amp = amplitude(t, dot2((high_ref[...], low_ref[...]), wy))
+        amp_ref[0, pl.ds(t, 1), :], amp_ref[1, pl.ds(t, 1), :] = amp
         return carry
 
-    tiles = cells_ref.shape[1]
     lax.fori_loop(0, tiles, body, 0, unroll=math.gcd(tiles, BATCH))
 
+    @pl.when(more)
+    def _():
+        def body(t, carry):
+            wy = weights(t, rest_ref[0, pl.ds(t, 1), :], rest_ref[1, pl.ds(t, 1), :])
+            amp = amplitude(t, dot(high_ref[...], wy))
+            amp_ref[0, pl.ds(t, 1), :] += amp[0]
+            amp_ref[1, pl.ds(t, 1), :] += amp[1]
+            return carry
+
+        lax.fori_loop(0, tiles, body, 0)
+
+
+def pack_kernel(radiation_ref, electrons_ref, index_ref, offset_ref, out_ref):
+    rows, slices, width = radiation_ref.shape
+    tiles = electrons_ref.shape[2] // TILE
+    for n in range(slices):
+        out_ref[n, :rows, :] = radiation_ref[:, n, : width // 2]
+        out_ref[n, rows : 2 * rows, :] = radiation_ref[:, n, width // 2 :]
+        at = 2 * rows
+        for ref in (electrons_ref, index_ref, offset_ref):
+            for k in (0, 1):
+                for t in range(tiles):
+                    line = ref[k, n : n + 1, t * TILE : (t + 1) * TILE]
+                    out_ref[n, at : at + 1, :] = line.astype(f32)
+                    at += 1
+
 
 def first_kernel(where_ref, *refs):
-    *blocks, field_ref, amp_ref, state_ref, cells_ref, high_ref, low_ref = refs
+    *blocks, field_ref, amp_ref, state_ref, cells_ref, high_ref, low_ref, wx_ref, rest_ref = refs
     half = field_ref.shape[0] // 2
     count = len(blocks) // 2
     rows = half // len(blocks)
@@ -106,20 +169,18 @@
                 line = ref[2 * rows + k * tiles : 2 * rows + (k + 1) * tiles, :]
                 target = state_ref.at[k] if k < 2 else cells_ref.at[k - 2]
                 target[n * tiles : (n + 1) * tiles, :] = line
-    gather_tiles(field_ref, cells_ref, high_ref, low_ref, amp_ref)
-
-
-def gather_kernel(
-    fresh_ref, old_ref, own_ref, other_ref, kx_ref, ky_ref, cells_ref, field_ref, amp_ref, high_ref, low_ref
-):
+    cells_ref[4], cells_ref[5] = weight_pair(cells_ref[3])
+    gather_tiles(field_ref, cells_ref, high_ref, low_ref, wx_ref, rest_ref, amp_ref)
+
+
+def gather_kernel(fresh_ref, own_ref, other_ref, kx_ref, ky_ref, cells_ref, field_ref, amp_ref, *scratch):
     half = field_ref.shape[0] // 2
-    total = old_ref[...] + current_gain * (own_ref[...] + other_ref[...])
-    moved = propagate(total, kx_ref[...].reshape(2 * half, half), ky_ref)
+    moved = propagate(own_ref[...] + other_ref[...], kx_ref[...].reshape(2 * half, half), ky_ref)
     field_ref[...] = jnp.where(fresh_ref[0] == 1, 0.0, moved)
-    gather_tiles(field_ref, cells_ref, high_ref, low_ref, amp_ref)
-
-
-def push_kernel(amp_ref, state_ref, cells_ref, current_ref, out_ref, cos_ref, sin_ref):
+    gather_tiles(field_ref, cells_ref, *scratch, amp_ref)
+
+
+def push_kernel(amp_ref, state_ref, cells_ref, field_ref, current_ref, out_ref, values_ref, rest_ref):
     half = current_ref.shape[0] // 2
     columns = current_ref.shape[1]
     phase = state_ref[0]
@@ -127,39 +188,49 @@
     phase = phase + phase_step * energy
     out_ref[0] = phase
     out_ref[1] = energy
-    cos_ref[...] = jnp.cos(phase)
-    sin_ref[...] = -jnp.sin(phase)
-    current_ref[...] = jnp.zeros_like(current_ref)
+    scale, more = scale_and_rest(cells_ref, rest_ref)
+    for part, factor in enumerate((jnp.cos(phase), -jnp.sin(phase))):
+        for side, weight in enumerate((1.0 - cells_ref[2], cells_ref[2])):
+            high, low = split((current_gain * scale) * weight * factor)
+            values_ref[4 * part + side] = high.astype(f32)
+            values_ref[4 * part + 2 + side] = low.astype(f32)
+    current_ref[...] = 0.5 * field_ref[...]
     tiles = cells_ref.shape[1]
     batch = math.gcd(tiles, BATCH)
 
-    def weights(t):
-        row = lambda n: cells_ref[n, pl.ds(t, 1), :]
-        wy = place_split(cell_masks(columns, row(1)), 1.0 - row(3), row(3))
-        masks = cell_masks(half, row(0))
-        parts = []
-        for ref in (cos_ref, sin_ref):
-            value = ref[pl.ds(t, 1), :]
-            parts.append(place_split(masks, (1.0 - row(2)) * value, row(2) * value))
-        return wy, tuple(jnp.concatenate(pair, axis=0) for pair in zip(*parts))
+    def values(t, which):
+        masks = cell_masks(half, cells_ref[0, pl.ds(t, 1), :])
+        pair = lambda n: (values_ref[n + side, pl.ds(t, 1), :].astype(bf16) for side in (0, 1))
+        return [jnp.concatenate([place(masks, *pair(n)) for n in (first, 4 + first)], axis=0) for first in which]
+
+    def weights(t, low, high):
+        return place(cell_masks(columns, cells_ref[1, pl.ds(t, 1), :]), low.astype(bf16), high.astype(bf16))
 
     def body(n, carry):
-        built = [weights(n * batch + k) for k in range(batch)]
-        join = lambda side, part: jnp.concatenate([item[side][part] for item in built], axis=1)
-        wy = join(0, 0), join(0, 1)
-        values = join(1, 0), join(1, 1)
-        current_ref[...] += dot3(values, wy, dot_t)
+        built = []
+        for t in [n * batch + k for k in range(batch)]:
+            built.append(values(t, (0, 2)) + [weights(t, cells_ref[4, pl.ds(t, 1), :], cells_ref[5, pl.ds(t, 1), :])])
+        high, low, wy = (jnp.concatenate(parts, axis=1) for parts in zip(*built))
+        current_ref[...] += dot2((high, low), wy, dot_t)
         return carry
 
     lax.fori_loop(0, tiles // batch, body, 0)
 
-
-def last_kernel(where_ref, old_ref, own_ref, other_ref, kx_ref, ky_ref, rows_ref):
+    @pl.when(more)
+    def _():
+        def body(t, carry):
+            wy = weights(t, rest_ref[0, pl.ds(t, 1), :], rest_ref[1, pl.ds(t, 1), :])
+            current_ref[...] += dot_t(values(t, (0,))[0], wy)
+            return carry
+
+        lax.fori_loop(0, tiles, body, 0)
+
+
+def last_kernel(where_ref, own_ref, other_ref, kx_ref, ky_ref, rows_ref):
     count, rows = rows_ref.shape[0], rows_ref.shape[1] // 2
-    total = old_ref[...] + current_gain * (own_ref[...] + other_ref[...])
     starts = [pl.multiple_of(where_ref[n] * rows, rows) for n in range(count)]
     block = jnp.concatenate([kx_ref[part, pl.ds(at, rows), :] for part in (0, 1) for at in starts], axis=0)
-    moved = propagate(total, block, ky_ref)
+    moved = propagate(own_ref[...] + other_ref[...], block, ky_ref)
     for n in range(count):
         rows_ref[n, :rows] = moved[n * rows : (n + 1) * rows]
         rows_ref[n, rows:] = moved[(count + n) * rows : (count + n + 1) * rows]
@@ -175,7 +246,7 @@
     return pl.pallas_call(
         kernel,
         out_shape=shapes,
-        in_specs=[smem if array.dtype == jnp.int32 else vmem for array in inputs],
+        in_specs=[smem if array.ndim == 1 else vmem for array in inputs],
         out_specs=[vmem] * len(outs),
         scratch_shapes=scratch,
         compiler_params=pltpu.CompilerParams(vmem_limit_bytes=VMEM_LIMIT),
@@ -224,10 +295,9 @@
     def across(value):
         return move(value, lambda cut, place: (cut, place ^ 1))
 
-    parts = jnp.concatenate([electrons, cell_index.astype(f32), cell_offset], axis=0)
-    parts = parts.transpose(1, 0, 2).reshape(slices, 6 * tiles, TILE)
-    fields = jnp.concatenate([radiation[:, :, :columns], radiation[:, :, columns:]], axis=0).transpose(1, 0, 2)
-    payload = jnp.concatenate([fields, parts], axis=1)
+    (payload,) = call(
+        pack_kernel, [radiation, electrons, cell_index, cell_offset], [(slices, 2 * rows + 6 * tiles, columns)], [], 0
+    )
     masks = range(0, dom, 2)
     own_blocks = []
     for mask in masks:
@@ -240,9 +310,10 @@
 
     field_shape = (2 * half, columns)
     state_shape = (2, len(masks) * tiles, TILE)
-    cells_shape = (4,) + state_shape[1:]
-    splits = [pltpu.VMEM(field_shape, bf16)] * 2
-    work = 6 * 2 * half * columns * state_shape[1] * TILE
+    cells_shape = (6,) + state_shape[1:]
+    pair = pltpu.VMEM(state_shape, f32)
+    splits = [pltpu.VMEM(field_shape, bf16)] * 2 + [pair] * 2
+    work = 4 * 2 * half * columns * state_shape[1] * TILE
     field, amp, state, cells = call(
         first_kernel,
         [where] + own_blocks + other_blocks,
@@ -256,16 +327,16 @@
             fresh = ((group + step) % groups == 0).astype(jnp.int32).reshape(1)
             field, amp = call(
                 gather_kernel,
-                [fresh, field, own, other, kernel_x, kernel_y, cells_of[step]],
+                [fresh, own, other, kernel_x, kernel_y, cells_of[step]],
                 [field_shape, state_shape],
                 splits,
                 work,
             )
         own, state = call(
             push_kernel,
-            [amp, state, cells_of[step]],
+            [amp, state, cells_of[step], field],
             [field_shape, state_shape],
-            [pltpu.VMEM(state_shape[1:], f32)] * 2,
+            [pltpu.VMEM((8,) + state_shape[1:], f32), pair],
             work,
         )
         other = across(own)
@@ -282,7 +353,7 @@
     field_home = (group + ITERS) % groups
     (blocks,) = call(
         last_kernel,
-        [jnp.stack(places(field_home)).astype(jnp.int32), field, own, other, kernel_x, kernel_y],
+        [jnp.stack(places(field_home)).astype(jnp.int32), own, other, kernel_x, kernel_y],
         [(slices, 2 * rows, columns)],
         [],
         work // 16,

time: 128 us -> 111 us (0.87)
  Pallas kernels: 68.1 us -> 47.9 us
  waiting for transfers between devices: 23.3 us -> 29 us
  local copies, waits for them, and re-layouts: 5.81 us -> 3.14 us
    pallas_call x9 -> x10, Pallas kernels: 68.1 us -> 47.9 us  [call(): pl.pallas_call(kernel, out_shape=shapes, in_specs=[smem if array.ndim ==...]
    ppermute x21, waiting for transfers between devices: 23.3 us -> 29 us  [move(): return lax.ppermute(value, ('cuts', 'dom'), route)]
    unnamed x20 -> x14, local copies, waits for them, and re-layouts: 5.52 us -> 2.93 us
  transfers between devices with their start and end apart: 21 -> 21, of which waited for: 11 -> 10; matrix products, arithmetic and copies ran while one was open for 1% -> 1% of each run, Pallas kernels for 22% -> 18%
where the time goes in v1:
time: 111 us; the launch traced here: 110 us
  Pallas kernels  47.9 us (43%)
  waiting for transfers between devices  29 us (26%)
  starting transfers between devices  28.9 us (26%)
  local copies, waits for them, and re-layouts  3.14 us (3%)
  between operations  1.31 us (1%)
    pallas_call x10, Pallas kernels, call(): pl.pallas_call(kernel, out_shape=shapes, in_specs=[smem if array.ndim ==...  47.9 us
    ppermute x21, waiting for transfers between devices, move(): return lax.ppermute(value, ('cuts', 'dom'), route)  29 us
    ppermute x21, starting transfers between devices, move(): return lax.ppermute(value, ('cuts', 'dom'), route)  28.9 us
    unnamed x14, local copies, waits for them, and re-layouts  2.93 us
  transfers between devices with their start and end apart: 21, of which 10 were waited for; matrix products, arithmetic and copies ran while one was open for 1% of the time, Pallas kernels for 18%

profile of v1, /device:TPU:0, one launch (start us, length us, event | category | flops | bytes accessed | tf_op | source)
XLA Modules:
  0.0 110.4 jit_solution(3143851855180016840)
XLA Ops:
  0.8 0.7 copy-done.2
  1.5 0.8 copy-done.5
  2.4 3.0 %collective-permute-start = (f32[112,256]{1,0:T(8,128)S(1)}, f32[112,256]{1,0:T(8,128)S(1)}, u32[]{:S(2)}, u32[]{:S(2)}) collective-permute-start(f32[112,256]{1,0:T(8,128)S(1)} %get-tuple-element.50), channel_id=1, source_target_pairs={{0,2},{1,3},{2,0},{3,1},{4,6},{5,7},{6,4},{7,5},{8,10},{9,11},{10,... | collective-permute-start | bytes 344072 | tf_op jit(solution)/shard_map/ppermute | solution.py:283
  5.5 1.5 %collective-permute-start.1 = (f32[112,256]{1,0:T(8,128)S(1)}, f32[112,256]{1,0:T(8,128)S(1)}, u32[]{:S(2)}, u32[]{:S(2)}) collective-permute-start(f32[112,256]{1,0:T(8,128)S(1)} %get-tuple-element.49), channel_id=1, source_target_pairs={{0,4},{1,5},{2,6},{3,7},{4,0},{5,1},{6,2},{7,3},{8,12},{9,13},{10,... | collective-permute-start | bytes 344072 | tf_op jit(solution)/shard_map/ppermute | solution.py:283
  7.1 1.9 %collective-permute-done.refs_1_ = f32[112,256]{1,0:T(8,128)S(1)} collective-permute-done((f32[112,256]{1,0:T(8,128)S(1)}, f32[112,256]{1,0:T(8,128)S(1)}, u32[]{:S(2)}, u32[]{:S(2)}) %collective-permute-start) | collective-permute-done | bytes 114720 | tf_op jit(solution)/shard_map/ppermute | solution.py:283
  9.0 3.7 %collective-permute-done.1.refs_2_ = f32[112,256]{1,0:T(8,128)S(1)} collective-permute-done((f32[112,256]{1,0:T(8,128)S(1)}, f32[112,256]{1,0:T(8,128)S(1)}, u32[]{:S(2)}, u32[]{:S(2)}) %collective-permute-start.1) | collective-permute-done | bytes 114720 | tf_op jit(solution)/shard_map/ppermute | solution.py:283
  13.4 0.6 collective-permute-done.5.refs_6_
  14.2 6.2 %shard_map.78 = (f32[512,256]{1,0:T(8,128)S(1)}, f32[2,32,256]{2,1,0:T(8,128)S(1)}, f32[2,32,256]{2,1,0:T(8,128)S(1)}, f32[6,32,256]{2,1,0:T(8,128)S(1)}) custom-call(s32[8]{0:T(128)S(1)} %stack.77.where_ref, f32[112,256]{1,0:T(8,128)S(1)} %get-tuple-element.51.refs_0_, f32[112,256]{1,0:T(8,128)S(1)} %collective-permute-done.refs_1_, ...), custom_call_target="tpu_custom_call" | custom-call | flops 4294967296 | bytes 1572896 | tf_op jit(solution)/shard_map/pallas_call | solution.py:246
  20.5 5.1 %shard_map.79 = (f32[512,256]{1,0:T(8,128)S(1)}, f32[2,32,256]{2,1,0:T(8,128)S(1)}) custom-call(f32[2,32,256]{2,1,0:T(8,128)S(1)} %get-tuple-element.23.amp_ref, f32[2,32,256]{2,1,0:T(8,128)S(1)} %get-tuple-element.24.state_ref, f32[6,32,256]{2,1,0:T(8,128)S(1)} %get-tuple-element.29.cells_ref, f32[512,256]{1,0:T(8,128)S(1)} %get-tuple-element.26.field_ref), custom_call_target="tpu_custom_call" | custom-call | flops 4294967296 | bytes 1441792 | tf_op jit(solution)/shard_map/pallas_call | solution.py:246
  26.0 3.6 %collective-permute-start.8 = (f32[6,32,256]{2,1,0:T(8,128)S(1)}, f32[6,32,256]{2,1,0:T(8,128)S(1)}, u32[]{:S(2)}, u32[]{:S(2)}) collective-permute-start(f32[6,32,256]{2,1,0:T(8,128)S(1)} %get-tuple-element.29.cells_ref), channel_id=1, source_target_pairs={{0,24},{1,25},{2,26},{3,27},{4,0},{5,1},{6,2},{7,3},{8,12},{9,13},... | collective-permute-start | bytes 589832 | tf_op jit(solution)/shard_map/ppermute | solution.py:283
  29.6 1.3 %collective-permute-start.9 = (f32[2,32,256]{2,1,0:T(8,128)S(1)}, f32[2,32,256]{2,1,0:T(8,128)S(1)}, u32[]{:S(2)}, u32[]{:S(2)}) collective-permute-start(f32[2,32,256]{2,1,0:T(8,128)S(1)} %get-tuple-element.28), channel_id=1, source_target_pairs={{0,24},{1,25},{2,26},{3,27},{4,0},{5,1},{6,2},{7,3},{8,12},{9,13},... | collective-permute-start | bytes 196616 | tf_op jit(solution)/shard_map/ppermute | solution.py:283
  30.9 3.8 %collective-permute-done.8.cells_ref = f32[6,32,256]{2,1,0:T(8,128)S(1)} collective-permute-done((f32[6,32,256]{2,1,0:T(8,128)S(1)}, f32[6,32,256]{2,1,0:T(8,128)S(1)}, u32[]{:S(2)}, u32[]{:S(2)}) %collective-permute-start.8) | collective-permute-done | bytes 196640 | tf_op jit(solution)/shard_map/ppermute | solution.py:283
  34.8 6.8 %shard_map.80 = (f32[512,256]{1,0:T(8,128)S(1)}, f32[2,32,256]{2,1,0:T(8,128)S(1)}) custom-call(s32[1]{0:T(128)} %bitcast.4.fresh_ref, f32[512,256]{1,0:T(8,128)S(1)} %get-tuple-element.27.own_ref, f32[512,256]{1,0:T(8,128)S(1)} %collective-permute-done.7.other_ref, f32[2,256,256]{2,1,0:T(8,128)S(1)} %copy-done, f32[2,256,256]{2,1,0:T(8,128)S(1)} %copy-done.1, ...), custom_call_target="tpu_custom_call" | custom-call | flops 4294967296 | bytes 2883588 | tf_op jit(solution)/shard_map/pallas_call | solution.py:246
  41.6 5.1 %shard_map.81 = (f32[512,256]{1,0:T(8,128)S(1)}, f32[2,32,256]{2,1,0:T(8,128)S(1)}) custom-call(f32[2,32,256]{2,1,0:T(8,128)S(1)} %get-tuple-element.30.amp_ref, f32[2,32,256]{2,1,0:T(8,128)S(1)} %collective-permute-done.9.state_ref, f32[6,32,256]{2,1,0:T(8,128)S(1)} %collective-permute-done.8.cells_ref, f32[512,256]{1,0:T(8,128)S(1)} %get-tuple-element.31.field_ref), custom_call_target="tpu_custom_call" | custom-call | flops 4294967296 | bytes 1441792 | tf_op jit(solution)/shard_map/pallas_call | solution.py:246
  46.8 3.3 %collective-permute-start.11 = (f32[6,32,256]{2,1,0:T(8,128)S(1)}, f32[6,32,256]{2,1,0:T(8,128)S(1)}, u32[]{:S(2)}, u32[]{:S(2)}) collective-permute-start(f32[6,32,256]{2,1,0:T(8,128)S(1)} %get-tuple-element.29.cells_ref), channel_id=1, source_target_pairs={{0,28},{1,29},{2,30},{3,31},{4,24},{5,25},{6,26},{7,27},{8,4},{9,5... | collective-permute-start | bytes 589832 | tf_op jit(solution)/shard_map/ppermute | solution.py:283
  50.1 1.1 %collective-permute-start.12 = (f32[2,32,256]{2,1,0:T(8,128)S(1)}, f32[2,32,256]{2,1,0:T(8,128)S(1)}, u32[]{:S(2)}, u32[]{:S(2)}) collective-permute-start(f32[2,32,256]{2,1,0:T(8,128)S(1)} %get-tuple-element.34), channel_id=1, source_target_pairs={{0,24},{1,25},{2,26},{3,27},{4,0},{5,1},{6,2},{7,3},{8,12},{9,13},... | collective-permute-start | bytes 196616 | tf_op jit(solution)/shard_map/ppermute | solution.py:283
  51.2 4.2 %collective-permute-done.11.cells_ref = f32[6,32,256]{2,1,0:T(8,128)S(1)} collective-permute-done((f32[6,32,256]{2,1,0:T(8,128)S(1)}, f32[6,32,256]{2,1,0:T(8,128)S(1)}, u32[]{:S(2)}, u32[]{:S(2)}) %collective-permute-start.11) | collective-permute-done | bytes 196640 | tf_op jit(solution)/shard_map/ppermute | solution.py:283
  55.4 6.6 %shard_map.82 = (f32[512,256]{1,0:T(8,128)S(1)}, f32[2,32,256]{2,1,0:T(8,128)S(1)}) custom-call(s32[1]{0:T(128)} %bitcast.3.fresh_ref, f32[512,256]{1,0:T(8,128)S(1)} %get-tuple-element.32.own_ref, f32[512,256]{1,0:T(8,128)S(1)} %collective-permute-done.10.other_ref, f32[2,256,256]{2,1,0:T(8,128)S(1)} %copy-done, f32[2,256,256]{2,1,0:T(8,128)S(1)} %copy-done.1, ...), custom_call_target="tpu_custom_call" | custom-call | flops 4294967296 | bytes 2883588 | tf_op jit(solution)/shard_map/pallas_call | solution.py:246
  62.0 5.1 %shard_map.83 = (f32[512,256]{1,0:T(8,128)S(1)}, f32[2,32,256]{2,1,0:T(8,128)S(1)}) custom-call(f32[2,32,256]{2,1,0:T(8,128)S(1)} %get-tuple-element.33.amp_ref, f32[2,32,256]{2,1,0:T(8,128)S(1)} %collective-permute-done.12.state_ref, f32[6,32,256]{2,1,0:T(8,128)S(1)} %collective-permute-done.11.cells_ref, f32[512,256]{1,0:T(8,128)S(1)} %get-tuple-element.35.field_ref), custom_call_target="tpu_custom_call" | custom-call | flops 4294967296 | bytes 1441792 | tf_op jit(solution)/shard_map/pallas_call | solution.py:246
  67.2 2.8 %collective-permute-start.14 = (f32[6,32,256]{2,1,0:T(8,128)S(1)}, f32[6,32,256]{2,1,0:T(8,128)S(1)}, u32[]{:S(2)}, u32[]{:S(2)}) collective-permute-start(f32[6,32,256]{2,1,0:T(8,128)S(1)} %get-tuple-element.29.cells_ref), channel_id=1, source_target_pairs={{0,20},{1,21},{2,22},{3,23},{4,28},{5,29},{6,30},{7,31},{8,0},{9,1... | collective-permute-start | bytes 589832 | tf_op jit(solution)/shard_map/ppermute | solution.py:283
  69.9 3.3 %collective-permute-start.15 = (f32[2,32,256]{2,1,0:T(8,128)S(1)}, f32[2,32,256]{2,1,0:T(8,128)S(1)}, u32[]{:S(2)}, u32[]{:S(2)}) collective-permute-start(f32[2,32,256]{2,1,0:T(8,128)S(1)} %get-tuple-element.38), channel_id=1, source_target_pairs={{0,24},{1,25},{2,26},{3,27},{4,0},{5,1},{6,2},{7,3},{8,12},{9,13},... | collective-permute-start | bytes 196616 | tf_op jit(solution)/shard_map/ppermute | solution.py:283
  73.2 5.5 %collective-permute-done.14.cells_ref = f32[6,32,256]{2,1,0:T(8,128)S(1)} collective-permute-done((f32[6,32,256]{2,1,0:T(8,128)S(1)}, f32[6,32,256]{2,1,0:T(8,128)S(1)}, u32[]{:S(2)}, u32[]{:S(2)}) %collective-permute-start.14) | collective-permute-done | bytes 196640 | tf_op jit(solution)/shard_map/ppermute | solution.py:283
  78.7 6.6 %shard_map.84 = (f32[512,256]{1,0:T(8,128)S(1)}, f32[2,32,256]{2,1,0:T(8,128)S(1)}) custom-call(s32[1]{0:T(128)} %bitcast.2.fresh_ref, f32[512,256]{1,0:T(8,128)S(1)} %get-tuple-element.36.own_ref, f32[512,256]{1,0:T(8,128)S(1)} %collective-permute-done.13.other_ref, f32[2,256,256]{2,1,0:T(8,128)S(1)} %copy-done, f32[2,256,256]{2,1,0:T(8,128)S(1)} %copy-done.1, ...), custom_call_target="tpu_custom_call" | custom-call | flops 4294967296 | bytes 2883588 | tf_op jit(solution)/shard_map/pallas_call | solution.py:246
  85.4 5.1 %shard_map.85 = (f32[512,256]{1,0:T(8,128)S(1)}, f32[2,32,256]{2,1,0:T(8,128)S(1)}) custom-call(f32[2,32,256]{2,1,0:T(8,128)S(1)} %get-tuple-element.37.amp_ref, f32[2,32,256]{2,1,0:T(8,128)S(1)} %collective-permute-done.15.state_ref, f32[6,32,256]{2,1,0:T(8,128)S(1)} %collective-permute-done.14.cells_ref, f32[512,256]{1,0:T(8,128)S(1)} %get-tuple-element.39.field_ref), custom_call_target="tpu_custom_call" | custom-call | flops 4294967296 | bytes 1441792 | tf_op jit(solution)/shard_map/pallas_call | solution.py:246
  90.8 1.6 %collective-permute-done.16.other_ref = f32[512,256]{1,0:T(8,128)S(1)} collective-permute-done((f32[512,256]{1,0:T(8,128)S(1)}, f32[512,256]{1,0:T(8,128)S(1)}, u32[]{:S(2)}, u32[]{:S(2)}) %collective-permute-start.16) | collective-permute-done | bytes 524320 | tf_op jit(solution)/shard_map/ppermute | solution.py:283
  92.4 1.2 %shard_map.86 = f32[2,64,256]{2,1,0:T(8,128)S(1)} custom-call(s32[2]{0:T(128)S(1)} %pad_add_fusion.where_ref, f32[512,256]{1,0:T(8,128)S(1)} %get-tuple-element.40.own_ref, f32[512,256]{1,0:T(8,128)S(1)} %collective-permute-done.16.other_ref, f32[2,256,256]{2,1,0:T(8,128)S(1)} %copy-done, f32[2,256,256]{2,1,0:T(8,128)S(1)} %copy-done.1), custom_call_target="tpu_custom_call" | custom-call | flops 268435456 | bytes 2228232 | tf_op jit(solution)/shard_map/pallas_call | solution.py:246
  93.8 4.2 %collective-permute-start.20 = (f32[2,8,256]{2,1,0:T(8,128)S(1)}, f32[2,8,256]{2,1,0:T(8,128)S(1)}, u32[]{:S(2)}, u32[]{:S(2)}) collective-permute-start(f32[2,8,256]{2,1,0:T(8,128)S(1)} %get-tuple-element.56), channel_id=1, source_target_pairs={{0,12},{1,13},{2,14},{3,15},{4,20},{5,21},{6,22},{7,23},{8,24},{9,... | collective-permute-start | bytes 49160 | tf_op jit(solution)/shard_map/ppermute | solution.py:283
  98.0 3.4 %collective-permute-start.17 = (f32[64,256]{1,0:T(8,128)S(1)}, f32[64,256]{1,0:T(8,128)S(1)}, u32[]{:S(2)}, u32[]{:S(2)}) collective-permute-start(f32[64,256]{1,0:T(8,128)S(1)} %get-tuple-element.55), channel_id=1, source_target_pairs={{0,16},{1,17},{2,18},{3,19},{4,20},{5,21},{6,22},{7,23},{8,24},{9,... | collective-permute-start | bytes 196616 | tf_op jit(solution)/shard_map/ppermute | solution.py:283
  101.4 0.6 copy.10
  102.1 2.9 %collective-permute-done.17 = f32[64,256]{1,0:T(8,128)S(1)} collective-permute-done((f32[64,256]{1,0:T(8,128)S(1)}, f32[64,256]{1,0:T(8,128)S(1)}, u32[]{:S(2)}, u32[]{:S(2)}) %collective-permute-start.17) | collective-permute-done | bytes 65568 | tf_op jit(solution)/shard_map/ppermute | solution.py:283
  105.0 4.5 %collective-permute-done.18 = f32[64,256]{1,0:T(8,128)S(1)} collective-permute-done((f32[64,256]{1,0:T(8,128)S(1)}, f32[64,256]{1,0:T(8,128)S(1)}, u32[]{:S(2)}, u32[]{:S(2)}) %collective-permute-start.18) | collective-permute-done | bytes 65568 | tf_op jit(solution)/shard_map/ppermute | solution.py:283
  109.6 0.8 copy.9
  (52 shorter events, 2.2 us)
Async XLA Ops:
  0.6 0.9 copy-start.2
  0.7 0.8 copy-start.4
  0.7 0.8 copy-start.3
  1.5 0.8 copy-start.5
  2.4 6.6 %collective-permute-start = (f32[112,256]{1,0:T(8,128)S(1)}, f32[112,256]{1,0:T(8,128)S(1)}, u32[]{:S(2)}, u32[]{:S(2)}) collective-permute-start(f32[112,256]{1,0:T(8,128)S(1)} %get-tuple-element.50), channel_id=1, source_target_pairs={{0,2},{1,3},{2,0},{3,1},{4,6},{5,7},{6,4},{7,5},{8,10},{9,11},{10,... | collective-permute-start | bytes 344072 | tf_op jit(solution)/shard_map/ppermute | solution.py:283
  5.5 7.2 %collective-permute-start.1 = (f32[112,256]{1,0:T(8,128)S(1)}, f32[112,256]{1,0:T(8,128)S(1)}, u32[]{:S(2)}, u32[]{:S(2)}) collective-permute-start(f32[112,256]{1,0:T(8,128)S(1)} %get-tuple-element.49), channel_id=1, source_target_pairs={{0,4},{1,5},{2,6},{3,7},{4,0},{5,1},{6,2},{7,3},{8,12},{9,13},{10,... | collective-permute-start | bytes 344072 | tf_op jit(solution)/shard_map/ppermute | solution.py:283
  7.0 5.7 %collective-permute-start.2 = (f32[112,256]{1,0:T(8,128)S(1)}, f32[112,256]{1,0:T(8,128)S(1)}, u32[]{:S(2)}, u32[]{:S(2)}) collective-permute-start(f32[112,256]{1,0:T(8,128)S(1)} %get-tuple-element.48), channel_id=1, source_target_pairs={{0,6},{1,7},{2,4},{3,5},{4,2},{5,3},{6,0},{7,1},{8,14},{9,15},{10,... | collective-permute-start | bytes 344072 | tf_op jit(solution)/shard_map/ppermute | solution.py:283
  7.0 6.4 %collective-permute-start.3 = (f32[64,256]{1,0:T(8,128)S(1)}, f32[64,256]{1,0:T(8,128)S(1)}, u32[]{:S(2)}, u32[]{:S(2)}) collective-permute-start(f32[64,256]{1,0:T(8,128)S(1)} %dynamic-slice_bitcast_fusion.4), channel_id=1, source_target_pairs={{0,1},{1,0},{2,3},{3,2},{4,5},{5,4},{6,7},{7,6},{8,9},{9,8},{10,11... | collective-permute-start | bytes 196616 | tf_op jit(solution)/shard_map/ppermute | solution.py:283
  9.0 4.4 %collective-permute-start.4 = (f32[64,256]{1,0:T(8,128)S(1)}, f32[64,256]{1,0:T(8,128)S(1)}, u32[]{:S(2)}, u32[]{:S(2)}) collective-permute-start(f32[64,256]{1,0:T(8,128)S(1)} %slice.61), channel_id=1, source_target_pairs={{0,1},{1,0},{2,3},{3,2},{4,5},{5,4},{6,7},{7,6},{8,9},{9,8},{10,11... | collective-permute-start | bytes 196616 | tf_op jit(solution)/shard_map/ppermute | solution.py:283
  12.7 1.3 %collective-permute-start.5 = (f32[64,256]{1,0:T(8,128)S(1)}, f32[64,256]{1,0:T(8,128)S(1)}, u32[]{:S(2)}, u32[]{:S(2)}) collective-permute-start(f32[64,256]{1,0:T(8,128)S(1)} %slice.62), channel_id=1, source_target_pairs={{0,1},{1,0},{2,3},{3,2},{4,5},{5,4},{6,7},{7,6},{8,9},{9,8},{10,11... | collective-permute-start | bytes 196616 | tf_op jit(solution)/shard_map/ppermute | solution.py:283
  12.8 1.5 %collective-permute-start.6 = (f32[64,256]{1,0:T(8,128)S(1)}, f32[64,256]{1,0:T(8,128)S(1)}, u32[]{:S(2)}, u32[]{:S(2)}) collective-permute-start(f32[64,256]{1,0:T(8,128)S(1)} %slice.63), channel_id=1, source_target_pairs={{0,1},{1,0},{2,3},{3,2},{4,5},{5,4},{6,7},{7,6},{8,9},{9,8},{10,11... | collective-permute-start | bytes 196616 | tf_op jit(solution)/shard_map/ppermute | solution.py:283
  20.5 14.3 %copy-start = (f32[2,256,256]{2,1,0:T(8,128)S(1)}, f32[2,256,256]{2,1,0:T(8,128)}, u32[]{:S(2)}) copy-start(f32[2,256,256]{2,1,0:T(8,128)} %kx_ref.7) | copy-start | bytes 1572868
  20.5 14.3 %copy-start.1 = (f32[2,256,256]{2,1,0:T(8,128)S(1)}, f32[2,256,256]{2,1,0:T(8,128)}, u32[]{:S(2)}) copy-start(f32[2,256,256]{2,1,0:T(8,128)} %ky_ref.7) | copy-start | bytes 1572868
  25.6 9.2 %collective-permute-start.7 = (f32[512,256]{1,0:T(8,128)S(1)}, f32[512,256]{1,0:T(8,128)S(1)}, u32[]{:S(2)}, u32[]{:S(2)}) collective-permute-start(f32[512,256]{1,0:T(8,128)S(1)} %get-tuple-element.27.own_ref), channel_id=1, source_target_pairs={{0,1},{1,0},{2,3},{3,2},{4,5},{5,4},{6,7},{7,6},{8,9},{9,8},{10,11... | collective-permute-start | bytes 1572872 | tf_op jit(solution)/shard_map/ppermute | solution.py:283
  26.0 8.8 %collective-permute-start.8 = (f32[6,32,256]{2,1,0:T(8,128)S(1)}, f32[6,32,256]{2,1,0:T(8,128)S(1)}, u32[]{:S(2)}, u32[]{:S(2)}) collective-permute-start(f32[6,32,256]{2,1,0:T(8,128)S(1)} %get-tuple-element.29.cells_ref), channel_id=1, source_target_pairs={{0,24},{1,25},{2,26},{3,27},{4,0},{5,1},{6,2},{7,3},{8,12},{9,13},... | collective-permute-start | bytes 589832 | tf_op jit(solution)/shard_map/ppermute | solution.py:283
  29.6 12.0 %collective-permute-start.9 = (f32[2,32,256]{2,1,0:T(8,128)S(1)}, f32[2,32,256]{2,1,0:T(8,128)S(1)}, u32[]{:S(2)}, u32[]{:S(2)}) collective-permute-start(f32[2,32,256]{2,1,0:T(8,128)S(1)} %get-tuple-element.28), channel_id=1, source_target_pairs={{0,24},{1,25},{2,26},{3,27},{4,0},{5,1},{6,2},{7,3},{8,12},{9,13},... | collective-permute-start | bytes 196616 | tf_op jit(solution)/shard_map/ppermute | solution.py:283
  46.7 8.7 %collective-permute-start.10 = (f32[512,256]{1,0:T(8,128)S(1)}, f32[512,256]{1,0:T(8,128)S(1)}, u32[]{:S(2)}, u32[]{:S(2)}) collective-permute-start(f32[512,256]{1,0:T(8,128)S(1)} %get-tuple-element.32.own_ref), channel_id=1, source_target_pairs={{0,1},{1,0},{2,3},{3,2},{4,5},{5,4},{6,7},{7,6},{8,9},{9,8},{10,11... | collective-permute-start | bytes 1572872 | tf_op jit(solution)/shard_map/ppermute | solution.py:283
  46.8 8.6 %collective-permute-start.11 = (f32[6,32,256]{2,1,0:T(8,128)S(1)}, f32[6,32,256]{2,1,0:T(8,128)S(1)}, u32[]{:S(2)}, u32[]{:S(2)}) collective-permute-start(f32[6,32,256]{2,1,0:T(8,128)S(1)} %get-tuple-element.29.cells_ref), channel_id=1, source_target_pairs={{0,28},{1,29},{2,30},{3,31},{4,24},{5,25},{6,26},{7,27},{8,4},{9,5... | collective-permute-start | bytes 589832 | tf_op jit(solution)/shard_map/ppermute | solution.py:283
  50.1 12.0 %collective-permute-start.12 = (f32[2,32,256]{2,1,0:T(8,128)S(1)}, f32[2,32,256]{2,1,0:T(8,128)S(1)}, u32[]{:S(2)}, u32[]{:S(2)}) collective-permute-start(f32[2,32,256]{2,1,0:T(8,128)S(1)} %get-tuple-element.34), channel_id=1, source_target_pairs={{0,24},{1,25},{2,26},{3,27},{4,0},{5,1},{6,2},{7,3},{8,12},{9,13},... | collective-permute-start | bytes 196616 | tf_op jit(solution)/shard_map/ppermute | solution.py:283
  67.1 11.6 %collective-permute-start.13 = (f32[512,256]{1,0:T(8,128)S(1)}, f32[512,256]{1,0:T(8,128)S(1)}, u32[]{:S(2)}, u32[]{:S(2)}) collective-permute-start(f32[512,256]{1,0:T(8,128)S(1)} %get-tuple-element.36.own_ref), channel_id=1, source_target_pairs={{0,1},{1,0},{2,3},{3,2},{4,5},{5,4},{6,7},{7,6},{8,9},{9,8},{10,11... | collective-permute-start | bytes 1572872 | tf_op jit(solution)/shard_map/ppermute | solution.py:283
  67.2 11.5 %collective-permute-start.14 = (f32[6,32,256]{2,1,0:T(8,128)S(1)}, f32[6,32,256]{2,1,0:T(8,128)S(1)}, u32[]{:S(2)}, u32[]{:S(2)}) collective-permute-start(f32[6,32,256]{2,1,0:T(8,128)S(1)} %get-tuple-element.29.cells_ref), channel_id=1, source_target_pairs={{0,20},{1,21},{2,22},{3,23},{4,28},{5,29},{6,30},{7,31},{8,0},{9,1... | collective-permute-start | bytes 589832 | tf_op jit(solution)/shard_map/ppermute | solution.py:283
  69.9 15.4 %collective-permute-start.15 = (f32[2,32,256]{2,1,0:T(8,128)S(1)}, f32[2,32,256]{2,1,0:T(8,128)S(1)}, u32[]{:S(2)}, u32[]{:S(2)}) collective-permute-start(f32[2,32,256]{2,1,0:T(8,128)S(1)} %get-tuple-element.38), channel_id=1, source_target_pairs={{0,24},{1,25},{2,26},{3,27},{4,0},{5,1},{6,2},{7,3},{8,12},{9,13},... | collective-permute-start | bytes 196616 | tf_op jit(solution)/shard_map/ppermute | solution.py:283
  90.4 2.0 %collective-permute-start.16 = (f32[512,256]{1,0:T(8,128)S(1)}, f32[512,256]{1,0:T(8,128)S(1)}, u32[]{:S(2)}, u32[]{:S(2)}) collective-permute-start(f32[512,256]{1,0:T(8,128)S(1)} %get-tuple-element.40.own_ref), channel_id=1, source_target_pairs={{0,1},{1,0},{2,3},{3,2},{4,5},{5,4},{6,7},{7,6},{8,9},{9,8},{10,11... | collective-permute-start | bytes 1572872 | tf_op jit(solution)/shard_map/ppermute | solution.py:283
  93.6 7.7 %collective-permute-start.19 = (f32[2,8,256]{2,1,0:T(8,128)S(1)}, f32[2,8,256]{2,1,0:T(8,128)S(1)}, u32[]{:S(2)}, u32[]{:S(2)}) collective-permute-start(f32[2,8,256]{2,1,0:T(8,128)S(1)} %get-tuple-element.57), channel_id=1, source_target_pairs={{0,8},{1,9},{2,10},{3,11},{4,16},{5,17},{6,18},{7,19},{8,28},{9,29... | collective-permute-start | bytes 49160 | tf_op jit(solution)/shard_map/ppermute | solution.py:283
  93.8 7.5 %collective-permute-start.20 = (f32[2,8,256]{2,1,0:T(8,128)S(1)}, f32[2,8,256]{2,1,0:T(8,128)S(1)}, u32[]{:S(2)}, u32[]{:S(2)}) collective-permute-start(f32[2,8,256]{2,1,0:T(8,128)S(1)} %get-tuple-element.56), channel_id=1, source_target_pairs={{0,12},{1,13},{2,14},{3,15},{4,20},{5,21},{6,22},{7,23},{8,24},{9,... | collective-permute-start | bytes 49160 | tf_op jit(solution)/shard_map/ppermute | solution.py:283
  98.0 7.0 %collective-permute-start.17 = (f32[64,256]{1,0:T(8,128)S(1)}, f32[64,256]{1,0:T(8,128)S(1)}, u32[]{:S(2)}, u32[]{:S(2)}) collective-permute-start(f32[64,256]{1,0:T(8,128)S(1)} %get-tuple-element.55), channel_id=1, source_target_pairs={{0,16},{1,17},{2,18},{3,19},{4,20},{5,21},{6,22},{7,23},{8,24},{9,... | collective-permute-start | bytes 196616 | tf_op jit(solution)/shard_map/ppermute | solution.py:283
  101.3 8.2 %collective-permute-start.18 = (f32[64,256]{1,0:T(8,128)S(1)}, f32[64,256]{1,0:T(8,128)S(1)}, u32[]{:S(2)}, u32[]{:S(2)}) collective-permute-start(f32[64,256]{1,0:T(8,128)S(1)} %get-tuple-element.54), channel_id=1, source_target_pairs={{0,20},{1,21},{2,22},{3,23},{4,16},{5,17},{6,18},{7,19},{8,28},{9,... | collective-permute-start | bytes 196616 | tf_op jit(solution)/shard_map/ppermute | solution.py:283

commit v2 on v1

--- a/solution.py
+++ b/solution.py
@@ -45,8 +45,8 @@
 
 
 def tent(rows, index, low, high):
-    distance = lax.broadcasted_iota(jnp.int32, (rows, index.shape[1]), 0).astype(f32) - index
-    return jnp.where(distance == 0.0, low, jnp.where(distance == 1.0, high, 0.0))
+    cell = lax.broadcasted_iota(jnp.int32, (rows, index.shape[1]), 0).astype(f32)
+    return jnp.where(cell == index, low, jnp.where(cell == index + 1.0, high, 0.0))
 
 
 def weight_pair(offset):
@@ -154,22 +154,25 @@
                     at += 1
 
 
-def first_kernel(where_ref, *refs):
-    *blocks, field_ref, amp_ref, state_ref, cells_ref, high_ref, low_ref, wx_ref, rest_ref = refs
+def lay_kernel(*refs):
+    *blocks, state_ref, cells_ref = refs
+    tiles = cells_ref.shape[1] // len(blocks)
+    for n, ref in enumerate(blocks):
+        above = ref.shape[0] - 6 * tiles
+        for k in range(6):
+            target = state_ref.at[k] if k < 2 else cells_ref.at[k - 2]
+            target[n * tiles : (n + 1) * tiles, :] = ref[above + k * tiles : above + (k + 1) * tiles, :]
+    cells_ref[4], cells_ref[5] = weight_pair(cells_ref[3])
+
+
+def first_kernel(where_ref, cells_ref, *refs):
+    *blocks, field_ref, amp_ref, high_ref, low_ref, wx_ref, rest_ref = refs
     half = field_ref.shape[0] // 2
-    count = len(blocks) // 2
     rows = half // len(blocks)
-    tiles = cells_ref.shape[1] // count
     for n, ref in enumerate(blocks):
         at = pl.multiple_of(where_ref[n] * rows, rows)
         field_ref[pl.ds(at, rows), :] = ref[:rows, :]
         field_ref[pl.ds(half + at, rows), :] = ref[rows : 2 * rows, :]
-        if n < count:
-            for k in range(6):
-                line = ref[2 * rows + k * tiles : 2 * rows + (k + 1) * tiles, :]
-                target = state_ref.at[k] if k < 2 else cells_ref.at[k - 2]
-                target[n * tiles : (n + 1) * tiles, :] = line
-    cells_ref[4], cells_ref[5] = weight_pair(cells_ref[3])
     gather_tiles(field_ref, cells_ref, high_ref, low_ref, wx_ref, rest_ref, amp_ref)
 
 
@@ -236,11 +239,28 @@
         rows_ref[n, rows:] = moved[(count + n) * rows : (count + n + 1) * rows]
 
 
+def final_kernel(order_ref, zero_ref, *refs):
+    *blocks, radiation_ref, electrons_ref = refs
+    rows, slices, width = radiation_ref.shape
+    tiles = electrons_ref.shape[2] // TILE
+    for n in range(slices):
+        for turn in range(slices):
+
+            @pl.when(order_ref[n] == turn)
+            def _():
+                block, state = blocks[turn], blocks[slices + turn]
+                radiation_ref[:, n, : width // 2] = jnp.where(zero_ref[n] == 1, 0.0, block[:rows, :])
+                radiation_ref[:, n, width // 2 :] = jnp.where(zero_ref[n] == 1, 0.0, block[rows:, :])
+                for k in (0, 1):
+                    for t in range(tiles):
+                        electrons_ref[k, n : n + 1, t * TILE : (t + 1) * TILE] = state[k, t : t + 1, :]
+
+
 vmem = pl.BlockSpec(memory_space=pltpu.VMEM)
 smem = pl.BlockSpec(memory_space=pltpu.SMEM)
 
 
-def call(kernel, inputs, outs, scratch, flops):
+def call(kernel, inputs, outs, scratch, flops, limit=VMEM_LIMIT):
     shapes = [jax.ShapeDtypeStruct(shape, f32) for shape in outs]
     moved = sum(4 * array.size for array in inputs) + sum(4 * shape.size for shape in shapes)
     return pl.pallas_call(
@@ -249,7 +269,7 @@
         in_specs=[smem if array.ndim == 1 else vmem for array in inputs],
         out_specs=[vmem] * len(outs),
         scratch_shapes=scratch,
-        compiler_params=pltpu.CompilerParams(vmem_limit_bytes=VMEM_LIMIT),
+        compiler_params=pltpu.CompilerParams(vmem_limit_bytes=limit),
         cost_estimate=pl.CostEstimate(flops=flops, bytes_accessed=moved, transcendentals=0),
     )(*inputs)
 
@@ -305,7 +325,9 @@
         if mask:
             block = move(block, lambda cut, place: (cut, place ^ mask))
         own_blocks.append(block)
-    other_blocks = [across(block[: 2 * rows]) for block in own_blocks]
+    other_blocks = []
+    for block in own_blocks:
+        other_blocks.append(across(block[: 2 * rows]))
     where = jnp.stack([me ^ mask for mask in masks] + [me ^ 1 ^ mask for mask in masks]).astype(jnp.int32)
 
     field_shape = (2 * half, columns)
@@ -314,14 +336,13 @@
     pair = pltpu.VMEM(state_shape, f32)
     splits = [pltpu.VMEM(field_shape, bf16)] * 2 + [pair] * 2
     work = 4 * 2 * half * columns * state_shape[1] * TILE
-    field, amp, state, cells = call(
-        first_kernel,
-        [where] + own_blocks + other_blocks,
-        [field_shape, state_shape, state_shape, cells_shape],
-        splits,
-        work,
+    state, cells = call(lay_kernel, own_blocks, [state_shape, cells_shape], [], 0)
+    cells_of = [cells]
+    for later in range(1, ITERS):
+        cells_of.append(move(cells, to_group(-later)))
+    field, amp = call(
+        first_kernel, [where, cells] + own_blocks + other_blocks, [field_shape, state_shape], splits, work
     )
-    cells_of = [cells]
     for step in range(ITERS):
         if step > 0:
             fresh = ((group + step) % groups == 0).astype(jnp.int32).reshape(1)
@@ -340,10 +361,6 @@
             work,
         )
         other = across(own)
-        if step == 0:
-            cells, _ = lax.optimization_barrier((cells, state))
-            for later in range(1, ITERS):
-                cells_of.append(move(cells, to_group(-later)))
         if step < ITERS - 1:
             state = move(state, to_group(-1))
 
@@ -369,14 +386,9 @@
         chunk = (seats[turn] ^ seats[0]) // 2
         block = lax.dynamic_slice_in_dim(state, chunk * tiles, tiles, 1)
         returned.append(move(block, to_group(ITERS - 1, turn)))
-    order = [(seat(cut, mine) - number) % slices for number in range(slices)]
-    landed = jnp.stack(landed)
-    landed = [pick(landed, which) for which in order]
-    returned = jnp.stack(returned)
-    returned = [pick(returned, which).reshape(2, tiles * TILE) for which in order]
-    landed[0] = jnp.where(cut == 0, 0.0, landed[0])
-    radiation_out = jnp.stack([jnp.concatenate([block[:rows], block[rows:]], axis=1) for block in landed], axis=1)
-    return radiation_out, jnp.stack(returned, axis=1)
+    order = jnp.stack([(seat(cut, mine) - n) % slices for n in range(slices)]).astype(jnp.int32)
+    zero = jnp.stack([group - seat(cut, mine) + n == 0 for n in range(slices)]).astype(jnp.int32)
+    return tuple(call(final_kernel, [order, zero] + landed + returned, [radiation.shape, electrons.shape], [], 0))
 
 
 def solution(mesh):

time: 111 us -> 110 us (level)
  local copies, waits for them, and re-layouts: 3.14 us -> 1.7 us
  Pallas kernels: 47.9 us -> 49.2 us
    unnamed x14 -> x12, local copies, waits for them, and re-layouts: 2.93 us -> 1.53 us
    pallas_call x10 -> x12, Pallas kernels: 47.9 us -> 49.2 us  [call(): pl.pallas_call(kernel, out_shape=shapes, in_specs=[smem if array.ndim ==...]
  transfers between devices with their start and end apart: 21 -> 21, of which waited for: 10 -> 9; matrix products, arithmetic and copies ran while one was open for 1% -> 0% of each run, Pallas kernels for 18% -> 19%
where the time goes in v2:
time: 110 us
  Pallas kernels  49.2 us (45%)
  starting transfers between devices  28.9 us (26%)
  waiting for transfers between devices  28.9 us (26%)
  local copies, waits for them, and re-layouts  1.7 us (2%)
  between operations  1.26 us (1%)
    pallas_call x12, Pallas kernels, call(): pl.pallas_call(kernel, out_shape=shapes, in_specs=[smem if array.ndim ==...  49.2 us
    ppermute x21, waiting for transfers between devices, move(): return lax.ppermute(value, ('cuts', 'dom'), route)  28.9 us
    ppermute x21, starting transfers between devices, move(): return lax.ppermute(value, ('cuts', 'dom'), route)  28.9 us
  transfers between devices with their start and end apart: 21, of which 9 were waited for; matrix products, arithmetic and copies ran while one was open for 0% of the time, Pallas kernels for 19%

profile of v2, /device:TPU:0, one launch (start us, length us, event | category | flops | bytes accessed | tf_op | source)
XLA Modules:
  0.0 110.2 jit_solution(3604332791221868876)
XLA Ops:
  0.8 0.7 copy-done.2
  1.5 0.8 copy-done.5
  2.4 3.0 %collective-permute-start = (f32[112,256]{1,0:T(8,128)S(1)}, f32[112,256]{1,0:T(8,128)S(1)}, u32[]{:S(2)}, u32[]{:S(2)}) collective-permute-start(f32[112,256]{1,0:T(8,128)S(1)} %get-tuple-element.44), channel_id=1, source_target_pairs={{0,2},{1,3},{2,0},{3,1},{4,6},{5,7},{6,4},{7,5},{8,10},{9,11},{10,... | collective-permute-start | bytes 344072 | tf_op jit(solution)/shard_map/ppermute | solution.py:303
  5.5 1.5 %collective-permute-start.1 = (f32[112,256]{1,0:T(8,128)S(1)}, f32[112,256]{1,0:T(8,128)S(1)}, u32[]{:S(2)}, u32[]{:S(2)}) collective-permute-start(f32[112,256]{1,0:T(8,128)S(1)} %get-tuple-element.43), channel_id=1, source_target_pairs={{0,4},{1,5},{2,6},{3,7},{4,0},{5,1},{6,2},{7,3},{8,12},{9,13},{10,... | collective-permute-start | bytes 344072 | tf_op jit(solution)/shard_map/ppermute | solution.py:303
  7.1 1.9 %collective-permute-done.refs_1_ = f32[112,256]{1,0:T(8,128)S(1)} collective-permute-done((f32[112,256]{1,0:T(8,128)S(1)}, f32[112,256]{1,0:T(8,128)S(1)}, u32[]{:S(2)}, u32[]{:S(2)}) %collective-permute-start) | collective-permute-done | bytes 114720 | tf_op jit(solution)/shard_map/ppermute | solution.py:303
  9.0 3.7 %collective-permute-done.1.refs_2_ = f32[112,256]{1,0:T(8,128)S(1)} collective-permute-done((f32[112,256]{1,0:T(8,128)S(1)}, f32[112,256]{1,0:T(8,128)S(1)}, u32[]{:S(2)}, u32[]{:S(2)}) %collective-permute-start.1) | collective-permute-done | bytes 114720 | tf_op jit(solution)/shard_map/ppermute | solution.py:303
  12.8 0.6 collective-permute-start.6
  13.4 0.6 shard_map.78
  14.2 5.7 %shard_map.79 = (f32[512,256]{1,0:T(8,128)S(1)}, f32[2,32,256]{2,1,0:T(8,128)S(1)}) custom-call(s32[8]{0:T(128)S(1)} %stack.71.where_ref, f32[6,32,256]{2,1,0:T(8,128)S(1)} %get-tuple-element.22.cells_ref, f32[112,256]{1,0:T(8,128)S(1)} %get-tuple-element.45.refs_0_, f32[112,256]{1,0:T(8,128)S(1)} %collective-permute-done.refs_1_, ...), custom_call_target="tpu_custom_call" | custom-call | flops 4294967296 | bytes 1507360 | tf_op jit(solution)/shard_map/pallas_call | solution.py:266
  19.9 5.1 %shard_map.80 = (f32[512,256]{1,0:T(8,128)S(1)}, f32[2,32,256]{2,1,0:T(8,128)S(1)}) custom-call(f32[2,32,256]{2,1,0:T(8,128)S(1)} %get-tuple-element.23.amp_ref, f32[2,32,256]{2,1,0:T(8,128)S(1)} %get-tuple-element.24.state_ref, f32[6,32,256]{2,1,0:T(8,128)S(1)} %get-tuple-element.22.cells_ref, f32[512,256]{1,0:T(8,128)S(1)} %get-tuple-element.25.field_ref), custom_call_target="tpu_custom_call" | custom-call | flops 4294967296 | bytes 1441792 | tf_op jit(solution)/shard_map/pallas_call | solution.py:266
  25.4 3.6 %collective-permute-start.8 = (f32[6,32,256]{2,1,0:T(8,128)S(1)}, f32[6,32,256]{2,1,0:T(8,128)S(1)}, u32[]{:S(2)}, u32[]{:S(2)}) collective-permute-start(f32[6,32,256]{2,1,0:T(8,128)S(1)} %get-tuple-element.22.cells_ref), channel_id=1, source_target_pairs={{0,24},{1,25},{2,26},{3,27},{4,0},{5,1},{6,2},{7,3},{8,12},{9,13},... | collective-permute-start | bytes 589832 | tf_op jit(solution)/shard_map/ppermute | solution.py:303
  29.0 1.3 %collective-permute-start.9 = (f32[2,32,256]{2,1,0:T(8,128)S(1)}, f32[2,32,256]{2,1,0:T(8,128)S(1)}, u32[]{:S(2)}, u32[]{:S(2)}) collective-permute-start(f32[2,32,256]{2,1,0:T(8,128)S(1)} %get-tuple-element.28), channel_id=1, source_target_pairs={{0,24},{1,25},{2,26},{3,27},{4,0},{5,1},{6,2},{7,3},{8,12},{9,13},... | collective-permute-start | bytes 196616 | tf_op jit(solution)/shard_map/ppermute | solution.py:303
  30.3 3.9 %collective-permute-done.8.cells_ref = f32[6,32,256]{2,1,0:T(8,128)S(1)} collective-permute-done((f32[6,32,256]{2,1,0:T(8,128)S(1)}, f32[6,32,256]{2,1,0:T(8,128)S(1)}, u32[]{:S(2)}, u32[]{:S(2)}) %collective-permute-start.8) | collective-permute-done | bytes 196640 | tf_op jit(solution)/shard_map/ppermute | solution.py:303
  34.2 6.8 %shard_map.81 = (f32[512,256]{1,0:T(8,128)S(1)}, f32[2,32,256]{2,1,0:T(8,128)S(1)}) custom-call(s32[1]{0:T(128)} %bitcast.8.fresh_ref, f32[512,256]{1,0:T(8,128)S(1)} %get-tuple-element.26.own_ref, f32[512,256]{1,0:T(8,128)S(1)} %collective-permute-done.7.other_ref, f32[2,256,256]{2,1,0:T(8,128)S(1)} %copy-done, f32[2,256,256]{2,1,0:T(8,128)S(1)} %copy-done.1, ...), custom_call_target="tpu_custom_call" | custom-call | flops 4294967296 | bytes 2883588 | tf_op jit(solution)/shard_map/pallas_call | solution.py:266
  41.0 5.1 %shard_map.82 = (f32[512,256]{1,0:T(8,128)S(1)}, f32[2,32,256]{2,1,0:T(8,128)S(1)}) custom-call(f32[2,32,256]{2,1,0:T(8,128)S(1)} %get-tuple-element.27.amp_ref, f32[2,32,256]{2,1,0:T(8,128)S(1)} %collective-permute-done.9.state_ref, f32[6,32,256]{2,1,0:T(8,128)S(1)} %collective-permute-done.8.cells_ref, f32[512,256]{1,0:T(8,128)S(1)} %get-tuple-element.29.field_ref), custom_call_target="tpu_custom_call" | custom-call | flops 4294967296 | bytes 1441792 | tf_op jit(solution)/shard_map/pallas_call | solution.py:266
  46.2 3.3 %collective-permute-start.11 = (f32[6,32,256]{2,1,0:T(8,128)S(1)}, f32[6,32,256]{2,1,0:T(8,128)S(1)}, u32[]{:S(2)}, u32[]{:S(2)}) collective-permute-start(f32[6,32,256]{2,1,0:T(8,128)S(1)} %get-tuple-element.22.cells_ref), channel_id=1, source_target_pairs={{0,28},{1,29},{2,30},{3,31},{4,24},{5,25},{6,26},{7,27},{8,4},{9,5... | collective-permute-start | bytes 589832 | tf_op jit(solution)/shard_map/ppermute | solution.py:303
  49.5 1.1 %collective-permute-start.12 = (f32[2,32,256]{2,1,0:T(8,128)S(1)}, f32[2,32,256]{2,1,0:T(8,128)S(1)}, u32[]{:S(2)}, u32[]{:S(2)}) collective-permute-start(f32[2,32,256]{2,1,0:T(8,128)S(1)} %get-tuple-element.32), channel_id=1, source_target_pairs={{0,24},{1,25},{2,26},{3,27},{4,0},{5,1},{6,2},{7,3},{8,12},{9,13},... | collective-permute-start | bytes 196616 | tf_op jit(solution)/shard_map/ppermute | solution.py:303
  50.6 4.2 %collective-permute-done.11.cells_ref = f32[6,32,256]{2,1,0:T(8,128)S(1)} collective-permute-done((f32[6,32,256]{2,1,0:T(8,128)S(1)}, f32[6,32,256]{2,1,0:T(8,128)S(1)}, u32[]{:S(2)}, u32[]{:S(2)}) %collective-permute-start.11) | collective-permute-done | bytes 196640 | tf_op jit(solution)/shard_map/ppermute | solution.py:303
  54.8 6.6 %shard_map.83 = (f32[512,256]{1,0:T(8,128)S(1)}, f32[2,32,256]{2,1,0:T(8,128)S(1)}) custom-call(s32[1]{0:T(128)} %bitcast.7.fresh_ref, f32[512,256]{1,0:T(8,128)S(1)} %get-tuple-element.30.own_ref, f32[512,256]{1,0:T(8,128)S(1)} %collective-permute-done.10.other_ref, f32[2,256,256]{2,1,0:T(8,128)S(1)} %copy-done, f32[2,256,256]{2,1,0:T(8,128)S(1)} %copy-done.1, ...), custom_call_target="tpu_custom_call" | custom-call | flops 4294967296 | bytes 2883588 | tf_op jit(solution)/shard_map/pallas_call | solution.py:266
  61.4 5.1 %shard_map.84 = (f32[512,256]{1,0:T(8,128)S(1)}, f32[2,32,256]{2,1,0:T(8,128)S(1)}) custom-call(f32[2,32,256]{2,1,0:T(8,128)S(1)} %get-tuple-element.31.amp_ref, f32[2,32,256]{2,1,0:T(8,128)S(1)} %collective-permute-done.12.state_ref, f32[6,32,256]{2,1,0:T(8,128)S(1)} %collective-permute-done.11.cells_ref, f32[512,256]{1,0:T(8,128)S(1)} %get-tuple-element.33.field_ref), custom_call_target="tpu_custom_call" | custom-call | flops 4294967296 | bytes 1441792 | tf_op jit(solution)/shard_map/pallas_call | solution.py:266
  66.6 2.8 %collective-permute-start.14 = (f32[6,32,256]{2,1,0:T(8,128)S(1)}, f32[6,32,256]{2,1,0:T(8,128)S(1)}, u32[]{:S(2)}, u32[]{:S(2)}) collective-permute-start(f32[6,32,256]{2,1,0:T(8,128)S(1)} %get-tuple-element.22.cells_ref), channel_id=1, source_target_pairs={{0,20},{1,21},{2,22},{3,23},{4,28},{5,29},{6,30},{7,31},{8,0},{9,1... | collective-permute-start | bytes 589832 | tf_op jit(solution)/shard_map/ppermute | solution.py:303
  69.4 3.3 %collective-permute-start.15 = (f32[2,32,256]{2,1,0:T(8,128)S(1)}, f32[2,32,256]{2,1,0:T(8,128)S(1)}, u32[]{:S(2)}, u32[]{:S(2)}) collective-permute-start(f32[2,32,256]{2,1,0:T(8,128)S(1)} %get-tuple-element.36), channel_id=1, source_target_pairs={{0,24},{1,25},{2,26},{3,27},{4,0},{5,1},{6,2},{7,3},{8,12},{9,13},... | collective-permute-start | bytes 196616 | tf_op jit(solution)/shard_map/ppermute | solution.py:303
  72.7 5.5 %collective-permute-done.14.cells_ref = f32[6,32,256]{2,1,0:T(8,128)S(1)} collective-permute-done((f32[6,32,256]{2,1,0:T(8,128)S(1)}, f32[6,32,256]{2,1,0:T(8,128)S(1)}, u32[]{:S(2)}, u32[]{:S(2)}) %collective-permute-start.14) | collective-permute-done | bytes 196640 | tf_op jit(solution)/shard_map/ppermute | solution.py:303
  78.1 6.6 %shard_map.85 = (f32[512,256]{1,0:T(8,128)S(1)}, f32[2,32,256]{2,1,0:T(8,128)S(1)}) custom-call(s32[1]{0:T(128)} %bitcast.6.fresh_ref, f32[512,256]{1,0:T(8,128)S(1)} %get-tuple-element.34.own_ref, f32[512,256]{1,0:T(8,128)S(1)} %collective-permute-done.13.other_ref, f32[2,256,256]{2,1,0:T(8,128)S(1)} %copy-done, f32[2,256,256]{2,1,0:T(8,128)S(1)} %copy-done.1, ...), custom_call_target="tpu_custom_call" | custom-call | flops 4294967296 | bytes 2883588 | tf_op jit(solution)/shard_map/pallas_call | solution.py:266
  84.8 5.1 %shard_map.86 = (f32[512,256]{1,0:T(8,128)S(1)}, f32[2,32,256]{2,1,0:T(8,128)S(1)}) custom-call(f32[2,32,256]{2,1,0:T(8,128)S(1)} %get-tuple-element.35.amp_ref, f32[2,32,256]{2,1,0:T(8,128)S(1)} %collective-permute-done.15.state_ref, f32[6,32,256]{2,1,0:T(8,128)S(1)} %collective-permute-done.14.cells_ref, f32[512,256]{1,0:T(8,128)S(1)} %get-tuple-element.37.field_ref), custom_call_target="tpu_custom_call" | custom-call | flops 4294967296 | bytes 1441792 | tf_op jit(solution)/shard_map/pallas_call | solution.py:266
  90.3 1.5 %collective-permute-done.16.other_ref = f32[512,256]{1,0:T(8,128)S(1)} collective-permute-done((f32[512,256]{1,0:T(8,128)S(1)}, f32[512,256]{1,0:T(8,128)S(1)}, u32[]{:S(2)}, u32[]{:S(2)}) %collective-permute-start.16) | collective-permute-done | bytes 524320 | tf_op jit(solution)/shard_map/ppermute | solution.py:303
  91.8 1.2 %shard_map.87 = f32[2,64,256]{2,1,0:T(8,128)S(1)} custom-call(s32[2]{0:T(128)S(1)} %pad_add_fusion.1.where_ref, f32[512,256]{1,0:T(8,128)S(1)} %get-tuple-element.38.own_ref, f32[512,256]{1,0:T(8,128)S(1)} %collective-permute-done.16.other_ref, f32[2,256,256]{2,1,0:T(8,128)S(1)} %copy-done, f32[2,256,256]{2,1,0:T(8,128)S(1)} %copy-done.1), custom_call_target="tpu_custom_call" | custom-call | flops 268435456 | bytes 2228232 | tf_op jit(solution)/shard_map/pallas_call | solution.py:266
  93.2 4.2 %collective-permute-start.20 = (f32[2,8,256]{2,1,0:T(8,128)S(1)}, f32[2,8,256]{2,1,0:T(8,128)S(1)}, u32[]{:S(2)}, u32[]{:S(2)}) collective-permute-start(f32[2,8,256]{2,1,0:T(8,128)S(1)} %get-tuple-element.48), channel_id=1, source_target_pairs={{0,12},{1,13},{2,14},{3,15},{4,20},{5,21},{6,22},{7,23},{8,24},{9,... | collective-permute-start | bytes 49160 | tf_op jit(solution)/shard_map/ppermute | solution.py:303
  97.4 3.4 %collective-permute-start.17 = (f32[64,256]{1,0:T(8,128)S(1)}, f32[64,256]{1,0:T(8,128)S(1)}, u32[]{:S(2)}, u32[]{:S(2)}) collective-permute-start(f32[64,256]{1,0:T(8,128)S(1)} %get-tuple-element.47), channel_id=1, source_target_pairs={{0,16},{1,17},{2,18},{3,19},{4,20},{5,21},{6,22},{7,23},{8,24},{9,... | collective-permute-start | bytes 196616 | tf_op jit(solution)/shard_map/ppermute | solution.py:303
  100.8 3.6 %collective-permute-done.17.refs_0_ = f32[64,256]{1,0:T(8,128)S(1)} collective-permute-done((f32[64,256]{1,0:T(8,128)S(1)}, f32[64,256]{1,0:T(8,128)S(1)}, u32[]{:S(2)}, u32[]{:S(2)}) %collective-permute-start.17) | collective-permute-done | bytes 65568 | tf_op jit(solution)/shard_map/ppermute | solution.py:303
  104.4 4.5 %collective-permute-done.18.refs_1_ = f32[64,256]{1,0:T(8,128)S(1)} collective-permute-done((f32[64,256]{1,0:T(8,128)S(1)}, f32[64,256]{1,0:T(8,128)S(1)}, u32[]{:S(2)}, u32[]{:S(2)}) %collective-permute-start.18) | collective-permute-done | bytes 65568 | tf_op jit(solution)/shard_map/ppermute | solution.py:303
  108.9 1.3 %shard_map.88 = (f32[32,2,512]{2,1,0:T(2,128)}, f32[2,2,2048]{2,1,0:T(2,128)}) custom-call(s32[2]{0:T(128)S(1)} %pad_add_fusion.order_ref, s32[2]{0:T(128)S(1)} %add_convert_fusion.zero_ref, f32[64,256]{1,0:T(8,128)S(1)} %collective-permute-done.17.refs_0_, f32[64,256]{1,0:T(8,128)S(1)} %collective-permute-done.18.refs_1_, ...), custom_call_target="tpu_custom_call" | custom-call | bytes 327696 | tf_op jit(solution)/shard_map/pallas_call | solution.py:266
  (45 shorter events, 1.6 us)
Async XLA Ops:
  0.6 0.9 copy-start.2
  0.7 0.8 copy-start.4
  0.7 0.8 copy-start.3
  1.5 0.8 copy-start.5
  2.4 6.6 %collective-permute-start = (f32[112,256]{1,0:T(8,128)S(1)}, f32[112,256]{1,0:T(8,128)S(1)}, u32[]{:S(2)}, u32[]{:S(2)}) collective-permute-start(f32[112,256]{1,0:T(8,128)S(1)} %get-tuple-element.44), channel_id=1, source_target_pairs={{0,2},{1,3},{2,0},{3,1},{4,6},{5,7},{6,4},{7,5},{8,10},{9,11},{10,... | collective-permute-start | bytes 344072 | tf_op jit(solution)/shard_map/ppermute | solution.py:303
  5.5 7.2 %collective-permute-start.1 = (f32[112,256]{1,0:T(8,128)S(1)}, f32[112,256]{1,0:T(8,128)S(1)}, u32[]{:S(2)}, u32[]{:S(2)}) collective-permute-start(f32[112,256]{1,0:T(8,128)S(1)} %get-tuple-element.43), channel_id=1, source_target_pairs={{0,4},{1,5},{2,6},{3,7},{4,0},{5,1},{6,2},{7,3},{8,12},{9,13},{10,... | collective-permute-start | bytes 344072 | tf_op jit(solution)/shard_map/ppermute | solution.py:303
  7.0 5.7 %collective-permute-start.2 = (f32[112,256]{1,0:T(8,128)S(1)}, f32[112,256]{1,0:T(8,128)S(1)}, u32[]{:S(2)}, u32[]{:S(2)}) collective-permute-start(f32[112,256]{1,0:T(8,128)S(1)} %get-tuple-element.42), channel_id=1, source_target_pairs={{0,6},{1,7},{2,4},{3,5},{4,2},{5,3},{6,0},{7,1},{8,14},{9,15},{10,... | collective-permute-start | bytes 344072 | tf_op jit(solution)/shard_map/ppermute | solution.py:303
  7.0 7.0 %collective-permute-start.3 = (f32[64,256]{1,0:T(8,128)S(1)}, f32[64,256]{1,0:T(8,128)S(1)}, u32[]{:S(2)}, u32[]{:S(2)}) collective-permute-start(f32[64,256]{1,0:T(8,128)S(1)} %dynamic-slice_bitcast_fusion.4), channel_id=1, source_target_pairs={{0,1},{1,0},{2,3},{3,2},{4,5},{5,4},{6,7},{7,6},{8,9},{9,8},{10,11... | collective-permute-start | bytes 196616 | tf_op jit(solution)/shard_map/ppermute | solution.py:303
  9.0 5.0 %collective-permute-start.4 = (f32[64,256]{1,0:T(8,128)S(1)}, f32[64,256]{1,0:T(8,128)S(1)}, u32[]{:S(2)}, u32[]{:S(2)}) collective-permute-start(f32[64,256]{1,0:T(8,128)S(1)} %slice.29), channel_id=1, source_target_pairs={{0,1},{1,0},{2,3},{3,2},{4,5},{5,4},{6,7},{7,6},{8,9},{9,8},{10,11... | collective-permute-start | bytes 196616 | tf_op jit(solution)/shard_map/ppermute | solution.py:303
  12.7 1.3 %collective-permute-start.5 = (f32[64,256]{1,0:T(8,128)S(1)}, f32[64,256]{1,0:T(8,128)S(1)}, u32[]{:S(2)}, u32[]{:S(2)}) collective-permute-start(f32[64,256]{1,0:T(8,128)S(1)} %slice.30), channel_id=1, source_target_pairs={{0,1},{1,0},{2,3},{3,2},{4,5},{5,4},{6,7},{7,6},{8,9},{9,8},{10,11... | collective-permute-start | bytes 196616 | tf_op jit(solution)/shard_map/ppermute | solution.py:303
  12.8 1.5 %collective-permute-start.6 = (f32[64,256]{1,0:T(8,128)S(1)}, f32[64,256]{1,0:T(8,128)S(1)}, u32[]{:S(2)}, u32[]{:S(2)}) collective-permute-start(f32[64,256]{1,0:T(8,128)S(1)} %slice.31), channel_id=1, source_target_pairs={{0,1},{1,0},{2,3},{3,2},{4,5},{5,4},{6,7},{7,6},{8,9},{9,8},{10,11... | collective-permute-start | bytes 196616 | tf_op jit(solution)/shard_map/ppermute | solution.py:303
  19.9 14.3 %copy-start = (f32[2,256,256]{2,1,0:T(8,128)S(1)}, f32[2,256,256]{2,1,0:T(8,128)}, u32[]{:S(2)}) copy-start(f32[2,256,256]{2,1,0:T(8,128)} %kx_ref.7) | copy-start | bytes 1572868
  19.9 14.3 %copy-start.1 = (f32[2,256,256]{2,1,0:T(8,128)S(1)}, f32[2,256,256]{2,1,0:T(8,128)}, u32[]{:S(2)}) copy-start(f32[2,256,256]{2,1,0:T(8,128)} %ky_ref.7) | copy-start | bytes 1572868
  25.0 9.2 %collective-permute-start.7 = (f32[512,256]{1,0:T(8,128)S(1)}, f32[512,256]{1,0:T(8,128)S(1)}, u32[]{:S(2)}, u32[]{:S(2)}) collective-permute-start(f32[512,256]{1,0:T(8,128)S(1)} %get-tuple-element.26.own_ref), channel_id=1, source_target_pairs={{0,1},{1,0},{2,3},{3,2},{4,5},{5,4},{6,7},{7,6},{8,9},{9,8},{10,11... | collective-permute-start | bytes 1572872 | tf_op jit(solution)/shard_map/ppermute | solution.py:303
  25.4 8.8 %collective-permute-start.8 = (f32[6,32,256]{2,1,0:T(8,128)S(1)}, f32[6,32,256]{2,1,0:T(8,128)S(1)}, u32[]{:S(2)}, u32[]{:S(2)}) collective-permute-start(f32[6,32,256]{2,1,0:T(8,128)S(1)} %get-tuple-element.22.cells_ref), channel_id=1, source_target_pairs={{0,24},{1,25},{2,26},{3,27},{4,0},{5,1},{6,2},{7,3},{8,12},{9,13},... | collective-permute-start | bytes 589832 | tf_op jit(solution)/shard_map/ppermute | solution.py:303
  29.0 12.0 %collective-permute-start.9 = (f32[2,32,256]{2,1,0:T(8,128)S(1)}, f32[2,32,256]{2,1,0:T(8,128)S(1)}, u32[]{:S(2)}, u32[]{:S(2)}) collective-permute-start(f32[2,32,256]{2,1,0:T(8,128)S(1)} %get-tuple-element.28), channel_id=1, source_target_pairs={{0,24},{1,25},{2,26},{3,27},{4,0},{5,1},{6,2},{7,3},{8,12},{9,13},... | collective-permute-start | bytes 196616 | tf_op jit(solution)/shard_map/ppermute | solution.py:303
  46.1 8.7 %collective-permute-start.10 = (f32[512,256]{1,0:T(8,128)S(1)}, f32[512,256]{1,0:T(8,128)S(1)}, u32[]{:S(2)}, u32[]{:S(2)}) collective-permute-start(f32[512,256]{1,0:T(8,128)S(1)} %get-tuple-element.30.own_ref), channel_id=1, source_target_pairs={{0,1},{1,0},{2,3},{3,2},{4,5},{5,4},{6,7},{7,6},{8,9},{9,8},{10,11... | collective-permute-start | bytes 1572872 | tf_op jit(solution)/shard_map/ppermute | solution.py:303
  46.2 8.6 %collective-permute-start.11 = (f32[6,32,256]{2,1,0:T(8,128)S(1)}, f32[6,32,256]{2,1,0:T(8,128)S(1)}, u32[]{:S(2)}, u32[]{:S(2)}) collective-permute-start(f32[6,32,256]{2,1,0:T(8,128)S(1)} %get-tuple-element.22.cells_ref), channel_id=1, source_target_pairs={{0,28},{1,29},{2,30},{3,31},{4,24},{5,25},{6,26},{7,27},{8,4},{9,5... | collective-permute-start | bytes 589832 | tf_op jit(solution)/shard_map/ppermute | solution.py:303
  49.5 11.9 %collective-permute-start.12 = (f32[2,32,256]{2,1,0:T(8,128)S(1)}, f32[2,32,256]{2,1,0:T(8,128)S(1)}, u32[]{:S(2)}, u32[]{:S(2)}) collective-permute-start(f32[2,32,256]{2,1,0:T(8,128)S(1)} %get-tuple-element.32), channel_id=1, source_target_pairs={{0,24},{1,25},{2,26},{3,27},{4,0},{5,1},{6,2},{7,3},{8,12},{9,13},... | collective-permute-start | bytes 196616 | tf_op jit(solution)/shard_map/ppermute | solution.py:303
  66.5 11.6 %collective-permute-start.13 = (f32[512,256]{1,0:T(8,128)S(1)}, f32[512,256]{1,0:T(8,128)S(1)}, u32[]{:S(2)}, u32[]{:S(2)}) collective-permute-start(f32[512,256]{1,0:T(8,128)S(1)} %get-tuple-element.34.own_ref), channel_id=1, source_target_pairs={{0,1},{1,0},{2,3},{3,2},{4,5},{5,4},{6,7},{7,6},{8,9},{9,8},{10,11... | collective-permute-start | bytes 1572872 | tf_op jit(solution)/shard_map/ppermute | solution.py:303
  66.6 11.5 %collective-permute-start.14 = (f32[6,32,256]{2,1,0:T(8,128)S(1)}, f32[6,32,256]{2,1,0:T(8,128)S(1)}, u32[]{:S(2)}, u32[]{:S(2)}) collective-permute-start(f32[6,32,256]{2,1,0:T(8,128)S(1)} %get-tuple-element.22.cells_ref), channel_id=1, source_target_pairs={{0,20},{1,21},{2,22},{3,23},{4,28},{5,29},{6,30},{7,31},{8,0},{9,1... | collective-permute-start | bytes 589832 | tf_op jit(solution)/shard_map/ppermute | solution.py:303
  69.4 15.4 %collective-permute-start.15 = (f32[2,32,256]{2,1,0:T(8,128)S(1)}, f32[2,32,256]{2,1,0:T(8,128)S(1)}, u32[]{:S(2)}, u32[]{:S(2)}) collective-permute-start(f32[2,32,256]{2,1,0:T(8,128)S(1)} %get-tuple-element.36), channel_id=1, source_target_pairs={{0,24},{1,25},{2,26},{3,27},{4,0},{5,1},{6,2},{7,3},{8,12},{9,13},... | collective-permute-start | bytes 196616 | tf_op jit(solution)/shard_map/ppermute | solution.py:303
  89.9 2.0 %collective-permute-start.16 = (f32[512,256]{1,0:T(8,128)S(1)}, f32[512,256]{1,0:T(8,128)S(1)}, u32[]{:S(2)}, u32[]{:S(2)}) collective-permute-start(f32[512,256]{1,0:T(8,128)S(1)} %get-tuple-element.38.own_ref), channel_id=1, source_target_pairs={{0,1},{1,0},{2,3},{3,2},{4,5},{5,4},{6,7},{7,6},{8,9},{9,8},{10,11... | collective-permute-start | bytes 1572872 | tf_op jit(solution)/shard_map/ppermute | solution.py:303
  93.1 7.8 %collective-permute-start.19 = (f32[2,8,256]{2,1,0:T(8,128)S(1)}, f32[2,8,256]{2,1,0:T(8,128)S(1)}, u32[]{:S(2)}, u32[]{:S(2)}) collective-permute-start(f32[2,8,256]{2,1,0:T(8,128)S(1)} %get-tuple-element.49), channel_id=1, source_target_pairs={{0,8},{1,9},{2,10},{3,11},{4,16},{5,17},{6,18},{7,19},{8,28},{9,29... | collective-permute-start | bytes 49160 | tf_op jit(solution)/shard_map/ppermute | solution.py:303
  93.2 7.6 %collective-permute-start.20 = (f32[2,8,256]{2,1,0:T(8,128)S(1)}, f32[2,8,256]{2,1,0:T(8,128)S(1)}, u32[]{:S(2)}, u32[]{:S(2)}) collective-permute-start(f32[2,8,256]{2,1,0:T(8,128)S(1)} %get-tuple-element.48), channel_id=1, source_target_pairs={{0,12},{1,13},{2,14},{3,15},{4,20},{5,21},{6,22},{7,23},{8,24},{9,... | collective-permute-start | bytes 49160 | tf_op jit(solution)/shard_map/ppermute | solution.py:303
  97.4 7.0 %collective-permute-start.17 = (f32[64,256]{1,0:T(8,128)S(1)}, f32[64,256]{1,0:T(8,128)S(1)}, u32[]{:S(2)}, u32[]{:S(2)}) collective-permute-start(f32[64,256]{1,0:T(8,128)S(1)} %get-tuple-element.47), channel_id=1, source_target_pairs={{0,16},{1,17},{2,18},{3,19},{4,20},{5,21},{6,22},{7,23},{8,24},{9,... | collective-permute-start | bytes 196616 | tf_op jit(solution)/shard_map/ppermute | solution.py:303
  100.7 8.2 %collective-permute-start.18 = (f32[64,256]{1,0:T(8,128)S(1)}, f32[64,256]{1,0:T(8,128)S(1)}, u32[]{:S(2)}, u32[]{:S(2)}) collective-permute-start(f32[64,256]{1,0:T(8,128)S(1)} %get-tuple-element.46), channel_id=1, source_target_pairs={{0,20},{1,21},{2,22},{3,23},{4,16},{5,17},{6,18},{7,19},{8,28},{9,... | collective-permute-start | bytes 196616 | tf_op jit(solution)/shard_map/ppermute | solution.py:303

commit v3 on v2

--- a/solution.py
+++ b/solution.py
@@ -76,16 +76,26 @@
     return scale, miss > (REST * REST) * 0.5 * offset.size
 
 
-def complex_rows(real, imag):
-    rows = real.shape[0] // 2
-    return jnp.concatenate([real[:rows] - imag[rows:], real[rows:] + imag[:rows]], axis=0)
-
-
-def propagate(field, kernel_x, kernel_y):
+def parts_kernel(kx_ref, ky_ref, *outs):
+    for ref, out_ref in zip((kx_ref, ky_ref), outs):
+        for n, value in enumerate((ref[0], ref[1], ref[0] + ref[1])):
+            out_ref[2 * n], out_ref[2 * n + 1] = split(value)
+
+
+def complex_product(left, right):
+    real, imag, both = (dot3(*pair) for pair in zip(left, right))
+    return real - imag, both - real - imag
+
+
+def triple(real, imag):
+    return split(real), split(imag), split(real + imag)
+
+
+def propagate(field, kernel_x, ky_ref):
     half = field.shape[0] // 2
-    left = split(kernel_x)
-    mixed = split(complex_rows(dot3(left, split(field[:half])), dot3(left, split(field[half:]))))
-    return complex_rows(dot3(mixed, split(kernel_y[0])), dot3(mixed, split(kernel_y[1])))
+    right = [(ky_ref[2 * n], ky_ref[2 * n + 1]) for n in range(3)]
+    mixed = complex_product(kernel_x, triple(field[:half], field[half:]))
+    return jnp.concatenate(complex_product(triple(*mixed), right), axis=0)
 
 
 def cell_masks(rows, index):
@@ -125,7 +135,7 @@
         amp_ref[0, pl.ds(t, 1), :], amp_ref[1, pl.ds(t, 1), :] = amp
         return carry
 
-    lax.fori_loop(0, tiles, body, 0, unroll=math.gcd(tiles, BATCH))
+    lax.fori_loop(0, tiles, body, 0, unroll=math.gcd(tiles, 2 * BATCH))
 
     @pl.when(more)
     def _():
@@ -177,8 +187,8 @@
 
 
 def gather_kernel(fresh_ref, own_ref, other_ref, kx_ref, ky_ref, cells_ref, field_ref, amp_ref, *scratch):
-    half = field_ref.shape[0] // 2
-    moved = propagate(own_ref[...] + other_ref[...], kx_ref[...].reshape(2 * half, half), ky_ref)
+    left = [(kx_ref[2 * n], kx_ref[2 * n + 1]) for n in range(3)]
+    moved = propagate(own_ref[...] + other_ref[...], left, ky_ref)
     field_ref[...] = jnp.where(fresh_ref[0] == 1, 0.0, moved)
     gather_tiles(field_ref, cells_ref, *scratch, amp_ref)
 
@@ -232,7 +242,8 @@
 def last_kernel(where_ref, own_ref, other_ref, kx_ref, ky_ref, rows_ref):
     count, rows = rows_ref.shape[0], rows_ref.shape[1] // 2
     starts = [pl.multiple_of(where_ref[n] * rows, rows) for n in range(count)]
-    block = jnp.concatenate([kx_ref[part, pl.ds(at, rows), :] for part in (0, 1) for at in starts], axis=0)
+    take = lambda part: jnp.concatenate([kx_ref[part, pl.ds(at, rows), :] for at in starts], axis=0)
+    block = [(take(2 * n), take(2 * n + 1)) for n in range(3)]
     moved = propagate(own_ref[...] + other_ref[...], block, ky_ref)
     for n in range(count):
         rows_ref[n, :rows] = moved[n * rows : (n + 1) * rows]
@@ -261,7 +272,7 @@
 
 
 def call(kernel, inputs, outs, scratch, flops, limit=VMEM_LIMIT):
-    shapes = [jax.ShapeDtypeStruct(shape, f32) for shape in outs]
+    shapes = [jax.ShapeDtypeStruct(shape, f32) if isinstance(shape, tuple) else shape for shape in outs]
     moved = sum(4 * array.size for array in inputs) + sum(4 * shape.size for shape in shapes)
     return pl.pallas_call(
         kernel,
@@ -317,6 +328,9 @@
 
     (payload,) = call(
         pack_kernel, [radiation, electrons, cell_index, cell_offset], [(slices, 2 * rows + 6 * tiles, columns)], [], 0
+    )
+    kx_parts, ky_parts = call(
+        parts_kernel, [kernel_x, kernel_y], [jax.ShapeDtypeStruct((6,) + kernel_x.shape[1:], bf16)] * 2, [], 0
     )
     masks = range(0, dom, 2)
     own_blocks = []
@@ -348,7 +362,7 @@
             fresh = ((group + step) % groups == 0).astype(jnp.int32).reshape(1)
             field, amp = call(
                 gather_kernel,
-                [fresh, own, other, kernel_x, kernel_y, cells_of[step]],
+                [fresh, own, other, kx_parts, ky_parts, cells_of[step]],
                 [field_shape, state_shape],
                 splits,
                 work,
@@ -370,7 +384,7 @@
     field_home = (group + ITERS) % groups
     (blocks,) = call(
         last_kernel,
-        [jnp.stack(places(field_home)).astype(jnp.int32), own, other, kernel_x, kernel_y],
+        [jnp.stack(places(field_home)).astype(jnp.int32), own, other, kx_parts, ky_parts],
         [(slices, 2 * rows, columns)],
         [],
         work // 16,

time: 110 us -> 108 us (0.982)
  Pallas kernels: 49.2 us -> 46.1 us
  local copies, waits for them, and re-layouts: 1.7 us -> 2.92 us
    pallas_call x12 -> x13, Pallas kernels: 49.2 us -> 46.1 us  [call(): pl.pallas_call(kernel, out_shape=shapes, in_specs=[smem if array.ndim ==...]
    unnamed x12 -> x16, local copies, waits for them, and re-layouts: 1.53 us -> 2.75 us
    ppermute x21, waiting for transfers between devices: 28.9 us -> 27.8 us  [move(): return lax.ppermute(value, ('cuts', 'dom'), route)]
  transfers between devices with their start and end apart: 21 -> 21, of which waited for: 9 -> 9; matrix products, arithmetic and copies ran while one was open for 0% -> 0% of each run, Pallas kernels for 19% -> 17%
where the time goes in v3:
time: 108 us; the launch traced here: 107 us
  Pallas kernels  46.1 us (43%)
  starting transfers between devices  29.1 us (27%)
  waiting for transfers between devices  27.8 us (26%)
  local copies, waits for them, and re-layouts  2.92 us (3%)
  between operations  1.26 us (1%)
    pallas_call x13, Pallas kernels, call(): pl.pallas_call(kernel, out_shape=shapes, in_specs=[smem if array.ndim ==...  46.1 us
    ppermute x21, starting transfers between devices, move(): return lax.ppermute(value, ('cuts', 'dom'), route)  29.1 us
    ppermute x21, waiting for transfers between devices, move(): return lax.ppermute(value, ('cuts', 'dom'), route)  27.8 us
    unnamed x16, local copies, waits for them, and re-layouts  2.75 us
  transfers between devices with their start and end apart: 21, of which 9 were waited for; matrix products, arithmetic and copies ran while one was open for 0% of the time, Pallas kernels for 17%

profile of v3, /device:TPU:0, one launch (start us, length us, event | category | flops | bytes accessed | tf_op | source)
XLA Modules:
  0.0 107.4 jit_solution(11375413389966570059)
XLA Ops:
  0.8 0.7 copy-done.2
  1.5 0.8 copy-done.5
  2.4 3.0 %collective-permute-start = (f32[112,256]{1,0:T(8,128)S(1)}, f32[112,256]{1,0:T(8,128)S(1)}, u32[]{:S(2)}, u32[]{:S(2)}) collective-permute-start(f32[112,256]{1,0:T(8,128)S(1)} %get-tuple-element.48), channel_id=1, source_target_pairs={{0,2},{1,3},{2,0},{3,1},{4,6},{5,7},{6,4},{7,5},{8,10},{9,11},{10,... | collective-permute-start | bytes 344072 | tf_op jit(solution)/shard_map/ppermute | solution.py:314
  5.5 1.5 %collective-permute-start.1 = (f32[112,256]{1,0:T(8,128)S(1)}, f32[112,256]{1,0:T(8,128)S(1)}, u32[]{:S(2)}, u32[]{:S(2)}) collective-permute-start(f32[112,256]{1,0:T(8,128)S(1)} %get-tuple-element.47), channel_id=1, source_target_pairs={{0,4},{1,5},{2,6},{3,7},{4,0},{5,1},{6,2},{7,3},{8,12},{9,13},{10,... | collective-permute-start | bytes 344072 | tf_op jit(solution)/shard_map/ppermute | solution.py:314
  7.1 1.9 %collective-permute-done.refs_1_ = f32[112,256]{1,0:T(8,128)S(1)} collective-permute-done((f32[112,256]{1,0:T(8,128)S(1)}, f32[112,256]{1,0:T(8,128)S(1)}, u32[]{:S(2)}, u32[]{:S(2)}) %collective-permute-start) | collective-permute-done | bytes 114720 | tf_op jit(solution)/shard_map/ppermute | solution.py:314
  9.0 3.7 %collective-permute-done.1.refs_2_ = f32[112,256]{1,0:T(8,128)S(1)} collective-permute-done((f32[112,256]{1,0:T(8,128)S(1)}, f32[112,256]{1,0:T(8,128)S(1)}, u32[]{:S(2)}, u32[]{:S(2)}) %collective-permute-start.1) | collective-permute-done | bytes 114720 | tf_op jit(solution)/shard_map/ppermute | solution.py:314
  14.2 5.2 %shard_map.79 = (f32[512,256]{1,0:T(8,128)S(1)}, f32[2,32,256]{2,1,0:T(8,128)S(1)}) custom-call(s32[8]{0:T(128)S(1)} %stack.71.where_ref, f32[6,32,256]{2,1,0:T(8,128)S(1)} %get-tuple-element.24.cells_ref, f32[112,256]{1,0:T(8,128)S(1)} %get-tuple-element.49.refs_0_, f32[112,256]{1,0:T(8,128)S(1)} %collective-permute-done.refs_1_, ...), custom_call_target="tpu_custom_call" | custom-call | flops 4294967296 | bytes 1507360 | tf_op jit(solution)/shard_map/pallas_call | solution.py:277
  19.4 5.1 %shard_map.80 = (f32[512,256]{1,0:T(8,128)S(1)}, f32[2,32,256]{2,1,0:T(8,128)S(1)}) custom-call(f32[2,32,256]{2,1,0:T(8,128)S(1)} %get-tuple-element.25.amp_ref, f32[2,32,256]{2,1,0:T(8,128)S(1)} %get-tuple-element.26.state_ref, f32[6,32,256]{2,1,0:T(8,128)S(1)} %get-tuple-element.24.cells_ref, f32[512,256]{1,0:T(8,128)S(1)} %get-tuple-element.27.field_ref), custom_call_target="tpu_custom_call" | custom-call | flops 4294967296 | bytes 1441792 | tf_op jit(solution)/shard_map/pallas_call | solution.py:277
  24.5 0.6 copy-done.6
  25.5 3.6 %collective-permute-start.8 = (f32[6,32,256]{2,1,0:T(8,128)S(1)}, f32[6,32,256]{2,1,0:T(8,128)S(1)}, u32[]{:S(2)}, u32[]{:S(2)}) collective-permute-start(f32[6,32,256]{2,1,0:T(8,128)S(1)} %get-tuple-element.24.cells_ref), channel_id=1, source_target_pairs={{0,24},{1,25},{2,26},{3,27},{4,0},{5,1},{6,2},{7,3},{8,12},{9,13},... | collective-permute-start | bytes 589832 | tf_op jit(solution)/shard_map/ppermute | solution.py:314
  29.3 0.6 copy-done.7
  29.9 1.3 %collective-permute-start.9 = (f32[2,32,256]{2,1,0:T(8,128)S(1)}, f32[2,32,256]{2,1,0:T(8,128)S(1)}, u32[]{:S(2)}, u32[]{:S(2)}) collective-permute-start(f32[2,32,256]{2,1,0:T(8,128)S(1)} %copy-done.7), channel_id=1, source_target_pairs={{0,24},{1,25},{2,26},{3,27},{4,0},{5,1},{6,2},{7,3},{8,12},{9,13},... | collective-permute-start | bytes 196616 | tf_op jit(solution)/shard_map/ppermute | solution.py:314
  31.3 3.0 %collective-permute-done.8.cells_ref = f32[6,32,256]{2,1,0:T(8,128)S(1)} collective-permute-done((f32[6,32,256]{2,1,0:T(8,128)S(1)}, f32[6,32,256]{2,1,0:T(8,128)S(1)}, u32[]{:S(2)}, u32[]{:S(2)}) %collective-permute-start.8) | collective-permute-done | bytes 196640 | tf_op jit(solution)/shard_map/ppermute | solution.py:314
  34.3 6.5 %shard_map.82 = (f32[512,256]{1,0:T(8,128)S(1)}, f32[2,32,256]{2,1,0:T(8,128)S(1)}) custom-call(s32[1]{0:T(128)} %bitcast.8.fresh_ref, f32[512,256]{1,0:T(8,128)S(1)} %get-tuple-element.28.own_ref, f32[512,256]{1,0:T(8,128)} %collective-permute-done.7.other_ref, bf16[6,256,256]{2,1,0:T(8,128)(2,1)S(1)} %get-tuple-element.29.kx_ref, ...), custom_call_target="tpu_custom_call" | custom-call | flops 4294967296 | bytes 4980740 | tf_op jit(solution)/shard_map/pallas_call | solution.py:277
  40.8 5.1 %shard_map.83 = (f32[512,256]{1,0:T(8,128)S(1)}, f32[2,32,256]{2,1,0:T(8,128)S(1)}) custom-call(f32[2,32,256]{2,1,0:T(8,128)S(1)} %get-tuple-element.31.amp_ref, f32[2,32,256]{2,1,0:T(8,128)S(1)} %collective-permute-done.9.state_ref, f32[6,32,256]{2,1,0:T(8,128)S(1)} %collective-permute-done.8.cells_ref, f32[512,256]{1,0:T(8,128)S(1)} %get-tuple-element.33.field_ref), custom_call_target="tpu_custom_call" | custom-call | flops 4294967296 | bytes 1441792 | tf_op jit(solution)/shard_map/pallas_call | solution.py:277
  45.9 3.3 %collective-permute-start.11 = (f32[6,32,256]{2,1,0:T(8,128)S(1)}, f32[6,32,256]{2,1,0:T(8,128)S(1)}, u32[]{:S(2)}, u32[]{:S(2)}) collective-permute-start(f32[6,32,256]{2,1,0:T(8,128)S(1)} %get-tuple-element.24.cells_ref), channel_id=1, source_target_pairs={{0,28},{1,29},{2,30},{3,31},{4,24},{5,25},{6,26},{7,27},{8,4},{9,5... | collective-permute-start | bytes 589832 | tf_op jit(solution)/shard_map/ppermute | solution.py:314
  49.2 1.3 %collective-permute-start.12 = (f32[2,32,256]{2,1,0:T(8,128)S(1)}, f32[2,32,256]{2,1,0:T(8,128)S(1)}, u32[]{:S(2)}, u32[]{:S(2)}) collective-permute-start(f32[2,32,256]{2,1,0:T(8,128)S(1)} %get-tuple-element.36), channel_id=1, source_target_pairs={{0,24},{1,25},{2,26},{3,27},{4,0},{5,1},{6,2},{7,3},{8,12},{9,13},... | collective-permute-start | bytes 196616 | tf_op jit(solution)/shard_map/ppermute | solution.py:314
  50.5 4.0 %collective-permute-done.11.cells_ref = f32[6,32,256]{2,1,0:T(8,128)S(1)} collective-permute-done((f32[6,32,256]{2,1,0:T(8,128)S(1)}, f32[6,32,256]{2,1,0:T(8,128)S(1)}, u32[]{:S(2)}, u32[]{:S(2)}) %collective-permute-start.11) | collective-permute-done | bytes 196640 | tf_op jit(solution)/shard_map/ppermute | solution.py:314
  54.5 5.4 %shard_map.84 = (f32[512,256]{1,0:T(8,128)S(1)}, f32[2,32,256]{2,1,0:T(8,128)S(1)}) custom-call(s32[1]{0:T(128)} %bitcast.7.fresh_ref, f32[512,256]{1,0:T(8,128)S(1)} %get-tuple-element.34.own_ref, f32[512,256]{1,0:T(8,128)S(1)} %collective-permute-done.10.other_ref, bf16[6,256,256]{2,1,0:T(8,128)(2,1)S(1)} %get-tuple-element.29.kx_ref, ...), custom_call_target="tpu_custom_call" | custom-call | flops 4294967296 | bytes 4980740 | tf_op jit(solution)/shard_map/pallas_call | solution.py:277
  59.9 5.1 %shard_map.85 = (f32[512,256]{1,0:T(8,128)S(1)}, f32[2,32,256]{2,1,0:T(8,128)S(1)}) custom-call(f32[2,32,256]{2,1,0:T(8,128)S(1)} %get-tuple-element.35.amp_ref, f32[2,32,256]{2,1,0:T(8,128)S(1)} %collective-permute-done.12.state_ref, f32[6,32,256]{2,1,0:T(8,128)S(1)} %collective-permute-done.11.cells_ref, f32[512,256]{1,0:T(8,128)S(1)} %get-tuple-element.37.field_ref), custom_call_target="tpu_custom_call" | custom-call | flops 4294967296 | bytes 1441792 | tf_op jit(solution)/shard_map/pallas_call | solution.py:277
  65.1 2.8 %collective-permute-start.14 = (f32[6,32,256]{2,1,0:T(8,128)S(1)}, f32[6,32,256]{2,1,0:T(8,128)S(1)}, u32[]{:S(2)}, u32[]{:S(2)}) collective-permute-start(f32[6,32,256]{2,1,0:T(8,128)S(1)} %get-tuple-element.24.cells_ref), channel_id=1, source_target_pairs={{0,20},{1,21},{2,22},{3,23},{4,28},{5,29},{6,30},{7,31},{8,0},{9,1... | collective-permute-start | bytes 589832 | tf_op jit(solution)/shard_map/ppermute | solution.py:314
  67.9 3.3 %collective-permute-start.15 = (f32[2,32,256]{2,1,0:T(8,128)S(1)}, f32[2,32,256]{2,1,0:T(8,128)S(1)}, u32[]{:S(2)}, u32[]{:S(2)}) collective-permute-start(f32[2,32,256]{2,1,0:T(8,128)S(1)} %get-tuple-element.40), channel_id=1, source_target_pairs={{0,24},{1,25},{2,26},{3,27},{4,0},{5,1},{6,2},{7,3},{8,12},{9,13},... | collective-permute-start | bytes 196616 | tf_op jit(solution)/shard_map/ppermute | solution.py:314
  71.2 5.4 %collective-permute-done.14.cells_ref = f32[6,32,256]{2,1,0:T(8,128)S(1)} collective-permute-done((f32[6,32,256]{2,1,0:T(8,128)S(1)}, f32[6,32,256]{2,1,0:T(8,128)S(1)}, u32[]{:S(2)}, u32[]{:S(2)}) %collective-permute-start.14) | collective-permute-done | bytes 196640 | tf_op jit(solution)/shard_map/ppermute | solution.py:314
  76.6 5.4 %shard_map.86 = (f32[512,256]{1,0:T(8,128)S(1)}, f32[2,32,256]{2,1,0:T(8,128)S(1)}) custom-call(s32[1]{0:T(128)} %bitcast.6.fresh_ref, f32[512,256]{1,0:T(8,128)S(1)} %get-tuple-element.38.own_ref, f32[512,256]{1,0:T(8,128)S(1)} %collective-permute-done.13.other_ref, bf16[6,256,256]{2,1,0:T(8,128)(2,1)S(1)} %get-tuple-element.29.kx_ref, ...), custom_call_target="tpu_custom_call" | custom-call | flops 4294967296 | bytes 4980740 | tf_op jit(solution)/shard_map/pallas_call | solution.py:277
  82.0 5.1 %shard_map.87 = (f32[512,256]{1,0:T(8,128)S(1)}, f32[2,32,256]{2,1,0:T(8,128)S(1)}) custom-call(f32[2,32,256]{2,1,0:T(8,128)S(1)} %get-tuple-element.39.amp_ref, f32[2,32,256]{2,1,0:T(8,128)S(1)} %collective-permute-done.15.state_ref, f32[6,32,256]{2,1,0:T(8,128)S(1)} %collective-permute-done.14.cells_ref, f32[512,256]{1,0:T(8,128)S(1)} %get-tuple-element.41.field_ref), custom_call_target="tpu_custom_call" | custom-call | flops 4294967296 | bytes 1441792 | tf_op jit(solution)/shard_map/pallas_call | solution.py:277
  87.6 1.5 %collective-permute-done.16.other_ref = f32[512,256]{1,0:T(8,128)S(1)} collective-permute-done((f32[512,256]{1,0:T(8,128)S(1)}, f32[512,256]{1,0:T(8,128)S(1)}, u32[]{:S(2)}, u32[]{:S(2)}) %collective-permute-start.16) | collective-permute-done | bytes 524320 | tf_op jit(solution)/shard_map/ppermute | solution.py:314
  89.1 1.2 %shard_map.88 = f32[2,64,256]{2,1,0:T(8,128)S(1)} custom-call(s32[2]{0:T(128)S(1)} %pad_add_fusion.1.where_ref, f32[512,256]{1,0:T(8,128)S(1)} %get-tuple-element.42.own_ref, f32[512,256]{1,0:T(8,128)S(1)} %collective-permute-done.16.other_ref, bf16[6,256,256]{2,1,0:T(8,128)(2,1)S(1)} %get-tuple-element.29.kx_ref, ...), custom_call_target="tpu_custom_call" | custom-call | flops 268435456 | bytes 4325384 | tf_op jit(solution)/shard_map/pallas_call | solution.py:277
  90.4 4.2 %collective-permute-start.20 = (f32[2,8,256]{2,1,0:T(8,128)S(1)}, f32[2,8,256]{2,1,0:T(8,128)S(1)}, u32[]{:S(2)}, u32[]{:S(2)}) collective-permute-start(f32[2,8,256]{2,1,0:T(8,128)S(1)} %get-tuple-element.52), channel_id=1, source_target_pairs={{0,12},{1,13},{2,14},{3,15},{4,20},{5,21},{6,22},{7,23},{8,24},{9,... | collective-permute-start | bytes 49160 | tf_op jit(solution)/shard_map/ppermute | solution.py:314
  94.6 3.4 %collective-permute-start.17 = (f32[64,256]{1,0:T(8,128)S(1)}, f32[64,256]{1,0:T(8,128)S(1)}, u32[]{:S(2)}, u32[]{:S(2)}) collective-permute-start(f32[64,256]{1,0:T(8,128)S(1)} %get-tuple-element.51), channel_id=1, source_target_pairs={{0,16},{1,17},{2,18},{3,19},{4,20},{5,21},{6,22},{7,23},{8,24},{9,... | collective-permute-start | bytes 196616 | tf_op jit(solution)/shard_map/ppermute | solution.py:314
  98.0 2.9 %collective-permute-done.17.refs_0_ = f32[64,256]{1,0:T(8,128)S(1)} collective-permute-done((f32[64,256]{1,0:T(8,128)S(1)}, f32[64,256]{1,0:T(8,128)S(1)}, u32[]{:S(2)}, u32[]{:S(2)}) %collective-permute-start.17) | collective-permute-done | bytes 65568 | tf_op jit(solution)/shard_map/ppermute | solution.py:314
  100.9 5.2 %collective-permute-done.18.refs_1_ = f32[64,256]{1,0:T(8,128)S(1)} collective-permute-done((f32[64,256]{1,0:T(8,128)S(1)}, f32[64,256]{1,0:T(8,128)S(1)}, u32[]{:S(2)}, u32[]{:S(2)}) %collective-permute-start.18) | collective-permute-done | bytes 65568 | tf_op jit(solution)/shard_map/ppermute | solution.py:314
  106.1 1.3 %shard_map.89 = (f32[32,2,512]{2,1,0:T(2,128)}, f32[2,2,2048]{2,1,0:T(2,128)}) custom-call(s32[2]{0:T(128)S(1)} %pad_add_fusion.order_ref, s32[2]{0:T(128)S(1)} %add_convert_fusion.zero_ref, f32[64,256]{1,0:T(8,128)S(1)} %collective-permute-done.17.refs_0_, f32[64,256]{1,0:T(8,128)S(1)} %collective-permute-done.18.refs_1_, ...), custom_call_target="tpu_custom_call" | custom-call | bytes 327696 | tf_op jit(solution)/shard_map/pallas_call | solution.py:277
  (50 shorter events, 2.9 us)
Async XLA Ops:
  0.6 0.9 copy-start.2
  0.7 0.8 copy-start.4
  0.7 0.8 copy-start.3
  1.5 0.8 copy-start.5
  2.4 6.6 %collective-permute-start = (f32[112,256]{1,0:T(8,128)S(1)}, f32[112,256]{1,0:T(8,128)S(1)}, u32[]{:S(2)}, u32[]{:S(2)}) collective-permute-start(f32[112,256]{1,0:T(8,128)S(1)} %get-tuple-element.48), channel_id=1, source_target_pairs={{0,2},{1,3},{2,0},{3,1},{4,6},{5,7},{6,4},{7,5},{8,10},{9,11},{10,... | collective-permute-start | bytes 344072 | tf_op jit(solution)/shard_map/ppermute | solution.py:314
  5.5 7.2 %collective-permute-start.1 = (f32[112,256]{1,0:T(8,128)S(1)}, f32[112,256]{1,0:T(8,128)S(1)}, u32[]{:S(2)}, u32[]{:S(2)}) collective-permute-start(f32[112,256]{1,0:T(8,128)S(1)} %get-tuple-element.47), channel_id=1, source_target_pairs={{0,4},{1,5},{2,6},{3,7},{4,0},{5,1},{6,2},{7,3},{8,12},{9,13},{10,... | collective-permute-start | bytes 344072 | tf_op jit(solution)/shard_map/ppermute | solution.py:314
  7.0 5.7 %collective-permute-start.2 = (f32[112,256]{1,0:T(8,128)S(1)}, f32[112,256]{1,0:T(8,128)S(1)}, u32[]{:S(2)}, u32[]{:S(2)}) collective-permute-start(f32[112,256]{1,0:T(8,128)S(1)} %get-tuple-element.46), channel_id=1, source_target_pairs={{0,6},{1,7},{2,4},{3,5},{4,2},{5,3},{6,0},{7,1},{8,14},{9,15},{10,... | collective-permute-start | bytes 344072 | tf_op jit(solution)/shard_map/ppermute | solution.py:314
  7.0 7.0 %collective-permute-start.3 = (f32[64,256]{1,0:T(8,128)S(1)}, f32[64,256]{1,0:T(8,128)S(1)}, u32[]{:S(2)}, u32[]{:S(2)}) collective-permute-start(f32[64,256]{1,0:T(8,128)S(1)} %dynamic-slice_bitcast_fusion.4), channel_id=1, source_target_pairs={{0,1},{1,0},{2,3},{3,2},{4,5},{5,4},{6,7},{7,6},{8,9},{9,8},{10,11... | collective-permute-start | bytes 196616 | tf_op jit(solution)/shard_map/ppermute | solution.py:314
  9.0 5.0 %collective-permute-start.4 = (f32[64,256]{1,0:T(8,128)S(1)}, f32[64,256]{1,0:T(8,128)S(1)}, u32[]{:S(2)}, u32[]{:S(2)}) collective-permute-start(f32[64,256]{1,0:T(8,128)S(1)} %slice.29), channel_id=1, source_target_pairs={{0,1},{1,0},{2,3},{3,2},{4,5},{5,4},{6,7},{7,6},{8,9},{9,8},{10,11... | collective-permute-start | bytes 196616 | tf_op jit(solution)/shard_map/ppermute | solution.py:314
  12.7 1.3 %collective-permute-start.5 = (f32[64,256]{1,0:T(8,128)S(1)}, f32[64,256]{1,0:T(8,128)S(1)}, u32[]{:S(2)}, u32[]{:S(2)}) collective-permute-start(f32[64,256]{1,0:T(8,128)S(1)} %slice.30), channel_id=1, source_target_pairs={{0,1},{1,0},{2,3},{3,2},{4,5},{5,4},{6,7},{7,6},{8,9},{9,8},{10,11... | collective-permute-start | bytes 196616 | tf_op jit(solution)/shard_map/ppermute | solution.py:314
  12.8 1.5 %collective-permute-start.6 = (f32[64,256]{1,0:T(8,128)S(1)}, f32[64,256]{1,0:T(8,128)S(1)}, u32[]{:S(2)}, u32[]{:S(2)}) collective-permute-start(f32[64,256]{1,0:T(8,128)S(1)} %slice.31), channel_id=1, source_target_pairs={{0,1},{1,0},{2,3},{3,2},{4,5},{5,4},{6,7},{7,6},{8,9},{9,8},{10,11... | collective-permute-start | bytes 196616 | tf_op jit(solution)/shard_map/ppermute | solution.py:314
  19.4 9.7 %copy-start = (f32[2,256,256]{2,1,0:T(8,128)S(1)}, f32[2,256,256]{2,1,0:T(8,128)}, u32[]{:S(2)}) copy-start(f32[2,256,256]{2,1,0:T(8,128)} %kx_ref.1) | copy-start | bytes 1572868
  19.4 9.7 %copy-start.1 = (f32[2,256,256]{2,1,0:T(8,128)S(1)}, f32[2,256,256]{2,1,0:T(8,128)}, u32[]{:S(2)}) copy-start(f32[2,256,256]{2,1,0:T(8,128)} %ky_ref.1) | copy-start | bytes 1572868
  24.5 0.6 copy-start.6
  25.1 9.1 %collective-permute-start.7 = (f32[512,256]{1,0:T(8,128)S(1)}, f32[512,256]{1,0:T(8,128)}, u32[]{:S(2)}, u32[]{:S(2)}) collective-permute-start(f32[512,256]{1,0:T(8,128)S(1)} %get-tuple-element.28.own_ref), channel_id=1, source_target_pairs={{0,1},{1,0},{2,3},{3,2},{4,5},{5,4},{6,7},{7,6},{8,9},{9,8},{10,11... | collective-permute-start | bytes 1572872 | tf_op jit(solution)/shard_map/ppermute | solution.py:314
  25.5 8.8 %collective-permute-start.8 = (f32[6,32,256]{2,1,0:T(8,128)S(1)}, f32[6,32,256]{2,1,0:T(8,128)S(1)}, u32[]{:S(2)}, u32[]{:S(2)}) collective-permute-start(f32[6,32,256]{2,1,0:T(8,128)S(1)} %get-tuple-element.24.cells_ref), channel_id=1, source_target_pairs={{0,24},{1,25},{2,26},{3,27},{4,0},{5,1},{6,2},{7,3},{8,12},{9,13},... | collective-permute-start | bytes 589832 | tf_op jit(solution)/shard_map/ppermute | solution.py:314
  29.1 0.8 copy-start.7
  29.9 10.8 %collective-permute-start.9 = (f32[2,32,256]{2,1,0:T(8,128)S(1)}, f32[2,32,256]{2,1,0:T(8,128)S(1)}, u32[]{:S(2)}, u32[]{:S(2)}) collective-permute-start(f32[2,32,256]{2,1,0:T(8,128)S(1)} %copy-done.7), channel_id=1, source_target_pairs={{0,24},{1,25},{2,26},{3,27},{4,0},{5,1},{6,2},{7,3},{8,12},{9,13},... | collective-permute-start | bytes 196616 | tf_op jit(solution)/shard_map/ppermute | solution.py:314
  45.8 8.7 %collective-permute-start.10 = (f32[512,256]{1,0:T(8,128)S(1)}, f32[512,256]{1,0:T(8,128)S(1)}, u32[]{:S(2)}, u32[]{:S(2)}) collective-permute-start(f32[512,256]{1,0:T(8,128)S(1)} %get-tuple-element.34.own_ref), channel_id=1, source_target_pairs={{0,1},{1,0},{2,3},{3,2},{4,5},{5,4},{6,7},{7,6},{8,9},{9,8},{10,11... | collective-permute-start | bytes 1572872 | tf_op jit(solution)/shard_map/ppermute | solution.py:314
  45.9 8.6 %collective-permute-start.11 = (f32[6,32,256]{2,1,0:T(8,128)S(1)}, f32[6,32,256]{2,1,0:T(8,128)S(1)}, u32[]{:S(2)}, u32[]{:S(2)}) collective-permute-start(f32[6,32,256]{2,1,0:T(8,128)S(1)} %get-tuple-element.24.cells_ref), channel_id=1, source_target_pairs={{0,28},{1,29},{2,30},{3,31},{4,24},{5,25},{6,26},{7,27},{8,4},{9,5... | collective-permute-start | bytes 589832 | tf_op jit(solution)/shard_map/ppermute | solution.py:314
  49.2 10.7 %collective-permute-start.12 = (f32[2,32,256]{2,1,0:T(8,128)S(1)}, f32[2,32,256]{2,1,0:T(8,128)S(1)}, u32[]{:S(2)}, u32[]{:S(2)}) collective-permute-start(f32[2,32,256]{2,1,0:T(8,128)S(1)} %get-tuple-element.36), channel_id=1, source_target_pairs={{0,24},{1,25},{2,26},{3,27},{4,0},{5,1},{6,2},{7,3},{8,12},{9,13},... | collective-permute-start | bytes 196616 | tf_op jit(solution)/shard_map/ppermute | solution.py:314
  65.0 11.6 %collective-permute-start.13 = (f32[512,256]{1,0:T(8,128)S(1)}, f32[512,256]{1,0:T(8,128)S(1)}, u32[]{:S(2)}, u32[]{:S(2)}) collective-permute-start(f32[512,256]{1,0:T(8,128)S(1)} %get-tuple-element.38.own_ref), channel_id=1, source_target_pairs={{0,1},{1,0},{2,3},{3,2},{4,5},{5,4},{6,7},{7,6},{8,9},{9,8},{10,11... | collective-permute-start | bytes 1572872 | tf_op jit(solution)/shard_map/ppermute | solution.py:314
  65.1 11.5 %collective-permute-start.14 = (f32[6,32,256]{2,1,0:T(8,128)S(1)}, f32[6,32,256]{2,1,0:T(8,128)S(1)}, u32[]{:S(2)}, u32[]{:S(2)}) collective-permute-start(f32[6,32,256]{2,1,0:T(8,128)S(1)} %get-tuple-element.24.cells_ref), channel_id=1, source_target_pairs={{0,20},{1,21},{2,22},{3,23},{4,28},{5,29},{6,30},{7,31},{8,0},{9,1... | collective-permute-start | bytes 589832 | tf_op jit(solution)/shard_map/ppermute | solution.py:314
  67.9 14.2 %collective-permute-start.15 = (f32[2,32,256]{2,1,0:T(8,128)S(1)}, f32[2,32,256]{2,1,0:T(8,128)S(1)}, u32[]{:S(2)}, u32[]{:S(2)}) collective-permute-start(f32[2,32,256]{2,1,0:T(8,128)S(1)} %get-tuple-element.40), channel_id=1, source_target_pairs={{0,24},{1,25},{2,26},{3,27},{4,0},{5,1},{6,2},{7,3},{8,12},{9,13},... | collective-permute-start | bytes 196616 | tf_op jit(solution)/shard_map/ppermute | solution.py:314
  87.1 2.0 %collective-permute-start.16 = (f32[512,256]{1,0:T(8,128)S(1)}, f32[512,256]{1,0:T(8,128)S(1)}, u32[]{:S(2)}, u32[]{:S(2)}) collective-permute-start(f32[512,256]{1,0:T(8,128)S(1)} %get-tuple-element.42.own_ref), channel_id=1, source_target_pairs={{0,1},{1,0},{2,3},{3,2},{4,5},{5,4},{6,7},{7,6},{8,9},{9,8},{10,11... | collective-permute-start | bytes 1572872 | tf_op jit(solution)/shard_map/ppermute | solution.py:314
  90.3 7.8 %collective-permute-start.19 = (f32[2,8,256]{2,1,0:T(8,128)S(1)}, f32[2,8,256]{2,1,0:T(8,128)S(1)}, u32[]{:S(2)}, u32[]{:S(2)}) collective-permute-start(f32[2,8,256]{2,1,0:T(8,128)S(1)} %get-tuple-element.53), channel_id=1, source_target_pairs={{0,8},{1,9},{2,10},{3,11},{4,16},{5,17},{6,18},{7,19},{8,28},{9,29... | collective-permute-start | bytes 49160 | tf_op jit(solution)/shard_map/ppermute | solution.py:314
  90.4 7.6 %collective-permute-start.20 = (f32[2,8,256]{2,1,0:T(8,128)S(1)}, f32[2,8,256]{2,1,0:T(8,128)S(1)}, u32[]{:S(2)}, u32[]{:S(2)}) collective-permute-start(f32[2,8,256]{2,1,0:T(8,128)S(1)} %get-tuple-element.52), channel_id=1, source_target_pairs={{0,12},{1,13},{2,14},{3,15},{4,20},{5,21},{6,22},{7,23},{8,24},{9,... | collective-permute-start | bytes 49160 | tf_op jit(solution)/shard_map/ppermute | solution.py:314
  94.6 6.3 %collective-permute-start.17 = (f32[64,256]{1,0:T(8,128)S(1)}, f32[64,256]{1,0:T(8,128)S(1)}, u32[]{:S(2)}, u32[]{:S(2)}) collective-permute-start(f32[64,256]{1,0:T(8,128)S(1)} %get-tuple-element.51), channel_id=1, source_target_pairs={{0,16},{1,17},{2,18},{3,19},{4,20},{5,21},{6,22},{7,23},{8,24},{9,... | collective-permute-start | bytes 196616 | tf_op jit(solution)/shard_map/ppermute | solution.py:314
  98.0 8.2 %collective-permute-start.18 = (f32[64,256]{1,0:T(8,128)S(1)}, f32[64,256]{1,0:T(8,128)S(1)}, u32[]{:S(2)}, u32[]{:S(2)}) collective-permute-start(f32[64,256]{1,0:T(8,128)S(1)} %get-tuple-element.50), channel_id=1, source_target_pairs={{0,20},{1,21},{2,22},{3,23},{4,16},{5,17},{6,18},{7,19},{8,28},{9,... | collective-permute-start | bytes 196616 | tf_op jit(solution)/shard_map/ppermute | solution.py:314

commit v4 on v3

--- a/solution.py
+++ b/solution.py
@@ -327,7 +327,11 @@
         return move(value, lambda cut, place: (cut, place ^ 1))
 
     (payload,) = call(
-        pack_kernel, [radiation, electrons, cell_index, cell_offset], [(slices, 2 * rows + 6 * tiles, columns)], [], 0
+        pack_kernel,
+        [pltpu.with_memory_space_constraint(array, pltpu.HBM) for array in (radiation, electrons, cell_index, cell_offset)],
+        [(slices, 2 * rows + 6 * tiles, columns)],
+        [],
+        0,
     )
     kx_parts, ky_parts = call(
         parts_kernel, [kernel_x, kernel_y], [jax.ShapeDtypeStruct((6,) + kernel_x.shape[1:], bf16)] * 2, [], 0
@@ -352,8 +356,8 @@
     work = 4 * 2 * half * columns * state_shape[1] * TILE
     state, cells = call(lay_kernel, own_blocks, [state_shape, cells_shape], [], 0)
     cells_of = [cells]
-    for later in range(1, ITERS):
-        cells_of.append(move(cells, to_group(-later)))
+    for _ in range(1, ITERS):
+        cells_of.append(move(cells_of[-1], to_group(-1)))
     field, amp = call(
         first_kernel, [where, cells] + own_blocks + other_blocks, [field_shape, state_shape], splits, work
     )

time: 108 us -> 104 us (0.963)
  starting transfers between devices: 29.1 us -> 26.8 us
  local copies, waits for them, and re-layouts: 2.92 us -> 1.4 us
  waiting for transfers between devices: 27.8 us -> 26.7 us
    ppermute x21, starting transfers between devices: 29.1 us -> 26.8 us  [move(): return lax.ppermute(value, ('cuts', 'dom'), route)]
    unnamed x16 -> x8, local copies, waits for them, and re-layouts: 2.75 us -> 1.23 us
    ppermute x21, waiting for transfers between devices: 27.8 us -> 26.7 us  [move(): return lax.ppermute(value, ('cuts', 'dom'), route)]
  transfers between devices with their start and end apart: 21 -> 21, of which waited for: 9 -> 9; matrix products, arithmetic and copies ran while one was open for 0% -> 0% of each run, Pallas kernels for 17% -> 18%
where the time goes in v4:
time: 104 us; the launch traced here: 103 us
  Pallas kernels  47 us (45%)
  starting transfers between devices  26.8 us (26%)
  waiting for transfers between devices  26.7 us (26%)
  local copies, waits for them, and re-layouts  1.4 us (1%)
  between operations  1.26 us (1%)
    pallas_call x13, Pallas kernels, call(): pl.pallas_call(kernel, out_shape=shapes, in_specs=[smem if array.ndim ==...  47 us
    ppermute x21, starting transfers between devices, move(): return lax.ppermute(value, ('cuts', 'dom'), route)  26.8 us
    ppermute x21, waiting for transfers between devices, move(): return lax.ppermute(value, ('cuts', 'dom'), route)  26.7 us
  transfers between devices with their start and end apart: 21, of which 9 were waited for; matrix products, arithmetic and copies ran while one was open for 0% of the time, Pallas kernels for 18%

profile of v4, /device:TPU:0, one launch (start us, length us, event | category | flops | bytes accessed | tf_op | source)
XLA Modules:
  0.0 103.4 jit_solution(9687585658342096760)
XLA Ops:
  0.8 1.0 shard_map.77
  1.8 3.0 %collective-permute-start = (f32[112,256]{1,0:T(8,128)S(1)}, f32[112,256]{1,0:T(8,128)S(1)}, u32[]{:S(2)}, u32[]{:S(2)}) collective-permute-start(f32[112,256]{1,0:T(8,128)S(1)} %get-tuple-element.48), channel_id=1, source_target_pairs={{0,2},{1,3},{2,0},{3,1},{4,6},{5,7},{6,4},{7,5},{8,10},{9,11},{10,... | collective-permute-start | bytes 344072 | tf_op jit(solution)/shard_map/ppermute | solution.py:314
  4.9 1.5 %collective-permute-start.1 = (f32[112,256]{1,0:T(8,128)S(1)}, f32[112,256]{1,0:T(8,128)S(1)}, u32[]{:S(2)}, u32[]{:S(2)}) collective-permute-start(f32[112,256]{1,0:T(8,128)S(1)} %get-tuple-element.47), channel_id=1, source_target_pairs={{0,4},{1,5},{2,6},{3,7},{4,0},{5,1},{6,2},{7,3},{8,12},{9,13},{10,... | collective-permute-start | bytes 344072 | tf_op jit(solution)/shard_map/ppermute | solution.py:314
  6.5 1.9 %collective-permute-done.refs_1_ = f32[112,256]{1,0:T(8,128)S(1)} collective-permute-done((f32[112,256]{1,0:T(8,128)S(1)}, f32[112,256]{1,0:T(8,128)S(1)}, u32[]{:S(2)}, u32[]{:S(2)}) %collective-permute-start) | collective-permute-done | bytes 114720 | tf_op jit(solution)/shard_map/ppermute | solution.py:314
  8.4 3.7 %collective-permute-done.1.refs_2_ = f32[112,256]{1,0:T(8,128)S(1)} collective-permute-done((f32[112,256]{1,0:T(8,128)S(1)}, f32[112,256]{1,0:T(8,128)S(1)}, u32[]{:S(2)}, u32[]{:S(2)}) %collective-permute-start.1) | collective-permute-done | bytes 114720 | tf_op jit(solution)/shard_map/ppermute | solution.py:314
  12.2 0.6 collective-permute-start.6
  12.8 0.6 shard_map.78
  13.6 5.2 %shard_map.79 = (f32[512,256]{1,0:T(8,128)S(1)}, f32[2,32,256]{2,1,0:T(8,128)S(1)}) custom-call(s32[8]{0:T(128)S(1)} %stack.71.where_ref, f32[6,32,256]{2,1,0:T(8,128)S(1)} %get-tuple-element.24.cells_ref, f32[112,256]{1,0:T(8,128)S(1)} %get-tuple-element.49.refs_0_, f32[112,256]{1,0:T(8,128)S(1)} %collective-permute-done.refs_1_, ...), custom_call_target="tpu_custom_call" | custom-call | flops 4294967296 | bytes 1507360 | tf_op jit(solution)/shard_map/pallas_call | solution.py:277
  18.8 5.1 %shard_map.80 = (f32[512,256]{1,0:T(8,128)S(1)}, f32[2,32,256]{2,1,0:T(8,128)S(1)}) custom-call(f32[2,32,256]{2,1,0:T(8,128)S(1)} %get-tuple-element.25.amp_ref, f32[2,32,256]{2,1,0:T(8,128)S(1)} %get-tuple-element.26.state_ref, f32[6,32,256]{2,1,0:T(8,128)S(1)} %get-tuple-element.24.cells_ref, f32[512,256]{1,0:T(8,128)S(1)} %get-tuple-element.27.field_ref), custom_call_target="tpu_custom_call" | custom-call | flops 4294967296 | bytes 1441792 | tf_op jit(solution)/shard_map/pallas_call | solution.py:277
  23.9 0.6 copy-done.2
  24.9 3.6 %collective-permute-start.8 = (f32[6,32,256]{2,1,0:T(8,128)S(1)}, f32[6,32,256]{2,1,0:T(8,128)S(1)}, u32[]{:S(2)}, u32[]{:S(2)}) collective-permute-start(f32[6,32,256]{2,1,0:T(8,128)S(1)} %get-tuple-element.24.cells_ref), channel_id=1, source_target_pairs={{0,24},{1,25},{2,26},{3,27},{4,0},{5,1},{6,2},{7,3},{8,12},{9,13},... | collective-permute-start | bytes 589832 | tf_op jit(solution)/shard_map/ppermute | solution.py:314
  28.7 0.6 copy-done.3
  29.3 1.3 %collective-permute-start.9 = (f32[2,32,256]{2,1,0:T(8,128)S(1)}, f32[2,32,256]{2,1,0:T(8,128)S(1)}, u32[]{:S(2)}, u32[]{:S(2)}) collective-permute-start(f32[2,32,256]{2,1,0:T(8,128)S(1)} %copy-done.3), channel_id=1, source_target_pairs={{0,24},{1,25},{2,26},{3,27},{4,0},{5,1},{6,2},{7,3},{8,12},{9,13},... | collective-permute-start | bytes 196616 | tf_op jit(solution)/shard_map/ppermute | solution.py:314
  30.7 3.0 %collective-permute-done.8.cells_ref = f32[6,32,256]{2,1,0:T(8,128)S(1)} collective-permute-done((f32[6,32,256]{2,1,0:T(8,128)S(1)}, f32[6,32,256]{2,1,0:T(8,128)S(1)}, u32[]{:S(2)}, u32[]{:S(2)}) %collective-permute-start.8) | collective-permute-done | bytes 196640 | tf_op jit(solution)/shard_map/ppermute | solution.py:314
  33.7 6.5 %shard_map.82 = (f32[512,256]{1,0:T(8,128)S(1)}, f32[2,32,256]{2,1,0:T(8,128)S(1)}) custom-call(s32[1]{0:T(128)} %bitcast.8.fresh_ref, f32[512,256]{1,0:T(8,128)S(1)} %get-tuple-element.28.own_ref, f32[512,256]{1,0:T(8,128)} %collective-permute-done.7.other_ref, bf16[6,256,256]{2,1,0:T(8,128)(2,1)S(1)} %get-tuple-element.29.kx_ref, ...), custom_call_target="tpu_custom_call" | custom-call | flops 4294967296 | bytes 4980740 | tf_op jit(solution)/shard_map/pallas_call | solution.py:277
  40.1 5.1 %shard_map.83 = (f32[512,256]{1,0:T(8,128)S(1)}, f32[2,32,256]{2,1,0:T(8,128)S(1)}) custom-call(f32[2,32,256]{2,1,0:T(8,128)S(1)} %get-tuple-element.31.amp_ref, f32[2,32,256]{2,1,0:T(8,128)S(1)} %collective-permute-done.9.state_ref, f32[6,32,256]{2,1,0:T(8,128)S(1)} %collective-permute-done.8.cells_ref, f32[512,256]{1,0:T(8,128)S(1)} %get-tuple-element.33.field_ref), custom_call_target="tpu_custom_call" | custom-call | flops 4294967296 | bytes 1441792 | tf_op jit(solution)/shard_map/pallas_call | solution.py:277
  45.3 4.3 %collective-permute-start.11 = (f32[6,32,256]{2,1,0:T(8,128)S(1)}, f32[6,32,256]{2,1,0:T(8,128)S(1)}, u32[]{:S(2)}, u32[]{:S(2)}) collective-permute-start(f32[6,32,256]{2,1,0:T(8,128)S(1)} %collective-permute-done.8.cells_ref), channel_id=1, source_target_pairs={{0,24},{1,25},{2,26},{3,27},{4,0},{5,1},{6,2},{7,3},{8,12},{9,13},... | collective-permute-start | bytes 589832 | tf_op jit(solution)/shard_map/ppermute | solution.py:314
  49.9 5.0 %collective-permute-done.11.cells_ref = f32[6,32,256]{2,1,0:T(8,128)S(1)} collective-permute-done((f32[6,32,256]{2,1,0:T(8,128)S(1)}, f32[6,32,256]{2,1,0:T(8,128)S(1)}, u32[]{:S(2)}, u32[]{:S(2)}) %collective-permute-start.11) | collective-permute-done | bytes 196640 | tf_op jit(solution)/shard_map/ppermute | solution.py:314
  54.9 5.4 %shard_map.84 = (f32[512,256]{1,0:T(8,128)S(1)}, f32[2,32,256]{2,1,0:T(8,128)S(1)}) custom-call(s32[1]{0:T(128)} %bitcast.7.fresh_ref, f32[512,256]{1,0:T(8,128)S(1)} %get-tuple-element.34.own_ref, f32[512,256]{1,0:T(8,128)S(1)} %collective-permute-done.10.other_ref, bf16[6,256,256]{2,1,0:T(8,128)(2,1)S(1)} %get-tuple-element.29.kx_ref, ...), custom_call_target="tpu_custom_call" | custom-call | flops 4294967296 | bytes 4980740 | tf_op jit(solution)/shard_map/pallas_call | solution.py:277
  60.4 5.1 %shard_map.85 = (f32[512,256]{1,0:T(8,128)S(1)}, f32[2,32,256]{2,1,0:T(8,128)S(1)}) custom-call(f32[2,32,256]{2,1,0:T(8,128)S(1)} %get-tuple-element.35.amp_ref, f32[2,32,256]{2,1,0:T(8,128)S(1)} %collective-permute-done.12.state_ref, f32[6,32,256]{2,1,0:T(8,128)S(1)} %collective-permute-done.11.cells_ref, f32[512,256]{1,0:T(8,128)S(1)} %get-tuple-element.37.field_ref), custom_call_target="tpu_custom_call" | custom-call | flops 4294967296 | bytes 1441792 | tf_op jit(solution)/shard_map/pallas_call | solution.py:277
  65.5 4.3 %collective-permute-start.14 = (f32[6,32,256]{2,1,0:T(8,128)S(1)}, f32[6,32,256]{2,1,0:T(8,128)S(1)}, u32[]{:S(2)}, u32[]{:S(2)}) collective-permute-start(f32[6,32,256]{2,1,0:T(8,128)S(1)} %collective-permute-done.11.cells_ref), channel_id=1, source_target_pairs={{0,24},{1,25},{2,26},{3,27},{4,0},{5,1},{6,2},{7,3},{8,12},{9,13},... | collective-permute-start | bytes 589832 | tf_op jit(solution)/shard_map/ppermute | solution.py:314
  69.8 0.3 collective-permute-start.15
  70.2 4.9 %collective-permute-done.14.cells_ref = f32[6,32,256]{2,1,0:T(8,128)S(1)} collective-permute-done((f32[6,32,256]{2,1,0:T(8,128)S(1)}, f32[6,32,256]{2,1,0:T(8,128)S(1)}, u32[]{:S(2)}, u32[]{:S(2)}) %collective-permute-start.14) | collective-permute-done | bytes 196640 | tf_op jit(solution)/shard_map/ppermute | solution.py:314
  75.1 5.4 %shard_map.86 = (f32[512,256]{1,0:T(8,128)S(1)}, f32[2,32,256]{2,1,0:T(8,128)S(1)}) custom-call(s32[1]{0:T(128)} %bitcast.6.fresh_ref, f32[512,256]{1,0:T(8,128)S(1)} %get-tuple-element.38.own_ref, f32[512,256]{1,0:T(8,128)S(1)} %collective-permute-done.13.other_ref, bf16[6,256,256]{2,1,0:T(8,128)(2,1)S(1)} %get-tuple-element.29.kx_ref, ...), custom_call_target="tpu_custom_call" | custom-call | flops 4294967296 | bytes 4980740 | tf_op jit(solution)/shard_map/pallas_call | solution.py:277
  80.6 5.1 %shard_map.87 = (f32[512,256]{1,0:T(8,128)S(1)}, f32[2,32,256]{2,1,0:T(8,128)S(1)}) custom-call(f32[2,32,256]{2,1,0:T(8,128)S(1)} %get-tuple-element.39.amp_ref, f32[2,32,256]{2,1,0:T(8,128)S(1)} %collective-permute-done.15.state_ref, f32[6,32,256]{2,1,0:T(8,128)S(1)} %collective-permute-done.14.cells_ref, f32[512,256]{1,0:T(8,128)S(1)} %get-tuple-element.41.field_ref), custom_call_target="tpu_custom_call" | custom-call | flops 4294967296 | bytes 1441792 | tf_op jit(solution)/shard_map/pallas_call | solution.py:277
  86.1 1.5 %collective-permute-done.16.other_ref = f32[512,256]{1,0:T(8,128)S(1)} collective-permute-done((f32[512,256]{1,0:T(8,128)S(1)}, f32[512,256]{1,0:T(8,128)S(1)}, u32[]{:S(2)}, u32[]{:S(2)}) %collective-permute-start.16) | collective-permute-done | bytes 524320 | tf_op jit(solution)/shard_map/ppermute | solution.py:314
  87.6 1.2 %shard_map.88 = f32[2,64,256]{2,1,0:T(8,128)S(1)} custom-call(s32[2]{0:T(128)S(1)} %pad_add_fusion.1.where_ref, f32[512,256]{1,0:T(8,128)S(1)} %get-tuple-element.42.own_ref, f32[512,256]{1,0:T(8,128)S(1)} %collective-permute-done.16.other_ref, bf16[6,256,256]{2,1,0:T(8,128)(2,1)S(1)} %get-tuple-element.29.kx_ref, ...), custom_call_target="tpu_custom_call" | custom-call | flops 268435456 | bytes 4325384 | tf_op jit(solution)/shard_map/pallas_call | solution.py:277
  88.9 4.8 %collective-permute-start.17 = (f32[64,256]{1,0:T(8,128)S(1)}, f32[64,256]{1,0:T(8,128)S(1)}, u32[]{:S(2)}, u32[]{:S(2)}) collective-permute-start(f32[64,256]{1,0:T(8,128)S(1)} %get-tuple-element.51), channel_id=1, source_target_pairs={{0,16},{1,17},{2,18},{3,19},{4,20},{5,21},{6,22},{7,23},{8,24},{9,... | collective-permute-start | bytes 196616 | tf_op jit(solution)/shard_map/ppermute | solution.py:314
  93.8 1.9 %collective-permute-start.18 = (f32[64,256]{1,0:T(8,128)S(1)}, f32[64,256]{1,0:T(8,128)S(1)}, u32[]{:S(2)}, u32[]{:S(2)}) collective-permute-start(f32[64,256]{1,0:T(8,128)S(1)} %get-tuple-element.50), channel_id=1, source_target_pairs={{0,20},{1,21},{2,22},{3,23},{4,16},{5,17},{6,18},{7,19},{8,28},{9,... | collective-permute-start | bytes 196616 | tf_op jit(solution)/shard_map/ppermute | solution.py:314
  95.8 0.8 collective-permute-done.17.refs_0_
  96.6 5.6 %collective-permute-done.18.refs_1_ = f32[64,256]{1,0:T(8,128)S(1)} collective-permute-done((f32[64,256]{1,0:T(8,128)S(1)}, f32[64,256]{1,0:T(8,128)S(1)}, u32[]{:S(2)}, u32[]{:S(2)}) %collective-permute-start.18) | collective-permute-done | bytes 65568 | tf_op jit(solution)/shard_map/ppermute | solution.py:314
  102.1 1.3 %shard_map.89 = (f32[32,2,512]{2,1,0:T(2,128)}, f32[2,2,2048]{2,1,0:T(2,128)}) custom-call(s32[2]{0:T(128)S(1)} %pad_add_fusion.order_ref, s32[2]{0:T(128)S(1)} %add_convert_fusion.zero_ref, f32[64,256]{1,0:T(8,128)S(1)} %collective-permute-done.17.refs_0_, f32[64,256]{1,0:T(8,128)S(1)} %collective-permute-done.18.refs_1_, ...), custom_call_target="tpu_custom_call" | custom-call | bytes 327696 | tf_op jit(solution)/shard_map/pallas_call | solution.py:277
  (42 shorter events, 1.9 us)
Async XLA Ops:
  1.8 6.6 %collective-permute-start = (f32[112,256]{1,0:T(8,128)S(1)}, f32[112,256]{1,0:T(8,128)S(1)}, u32[]{:S(2)}, u32[]{:S(2)}) collective-permute-start(f32[112,256]{1,0:T(8,128)S(1)} %get-tuple-element.48), channel_id=1, source_target_pairs={{0,2},{1,3},{2,0},{3,1},{4,6},{5,7},{6,4},{7,5},{8,10},{9,11},{10,... | collective-permute-start | bytes 344072 | tf_op jit(solution)/shard_map/ppermute | solution.py:314
  4.9 7.2 %collective-permute-start.1 = (f32[112,256]{1,0:T(8,128)S(1)}, f32[112,256]{1,0:T(8,128)S(1)}, u32[]{:S(2)}, u32[]{:S(2)}) collective-permute-start(f32[112,256]{1,0:T(8,128)S(1)} %get-tuple-element.47), channel_id=1, source_target_pairs={{0,4},{1,5},{2,6},{3,7},{4,0},{5,1},{6,2},{7,3},{8,12},{9,13},{10,... | collective-permute-start | bytes 344072 | tf_op jit(solution)/shard_map/ppermute | solution.py:314
  6.4 5.7 %collective-permute-start.2 = (f32[112,256]{1,0:T(8,128)S(1)}, f32[112,256]{1,0:T(8,128)S(1)}, u32[]{:S(2)}, u32[]{:S(2)}) collective-permute-start(f32[112,256]{1,0:T(8,128)S(1)} %get-tuple-element.46), channel_id=1, source_target_pairs={{0,6},{1,7},{2,4},{3,5},{4,2},{5,3},{6,0},{7,1},{8,14},{9,15},{10,... | collective-permute-start | bytes 344072 | tf_op jit(solution)/shard_map/ppermute | solution.py:314
  6.4 7.0 %collective-permute-start.3 = (f32[64,256]{1,0:T(8,128)S(1)}, f32[64,256]{1,0:T(8,128)S(1)}, u32[]{:S(2)}, u32[]{:S(2)}) collective-permute-start(f32[64,256]{1,0:T(8,128)S(1)} %dynamic-slice_bitcast_fusion.4), channel_id=1, source_target_pairs={{0,1},{1,0},{2,3},{3,2},{4,5},{5,4},{6,7},{7,6},{8,9},{9,8},{10,11... | collective-permute-start | bytes 196616 | tf_op jit(solution)/shard_map/ppermute | solution.py:314
  8.4 5.0 %collective-permute-start.4 = (f32[64,256]{1,0:T(8,128)S(1)}, f32[64,256]{1,0:T(8,128)S(1)}, u32[]{:S(2)}, u32[]{:S(2)}) collective-permute-start(f32[64,256]{1,0:T(8,128)S(1)} %slice.29), channel_id=1, source_target_pairs={{0,1},{1,0},{2,3},{3,2},{4,5},{5,4},{6,7},{7,6},{8,9},{9,8},{10,11... | collective-permute-start | bytes 196616 | tf_op jit(solution)/shard_map/ppermute | solution.py:314
  12.1 1.3 %collective-permute-start.5 = (f32[64,256]{1,0:T(8,128)S(1)}, f32[64,256]{1,0:T(8,128)S(1)}, u32[]{:S(2)}, u32[]{:S(2)}) collective-permute-start(f32[64,256]{1,0:T(8,128)S(1)} %slice.30), channel_id=1, source_target_pairs={{0,1},{1,0},{2,3},{3,2},{4,5},{5,4},{6,7},{7,6},{8,9},{9,8},{10,11... | collective-permute-start | bytes 196616 | tf_op jit(solution)/shard_map/ppermute | solution.py:314
  12.2 1.5 %collective-permute-start.6 = (f32[64,256]{1,0:T(8,128)S(1)}, f32[64,256]{1,0:T(8,128)S(1)}, u32[]{:S(2)}, u32[]{:S(2)}) collective-permute-start(f32[64,256]{1,0:T(8,128)S(1)} %slice.31), channel_id=1, source_target_pairs={{0,1},{1,0},{2,3},{3,2},{4,5},{5,4},{6,7},{7,6},{8,9},{9,8},{10,11... | collective-permute-start | bytes 196616 | tf_op jit(solution)/shard_map/ppermute | solution.py:314
  18.8 9.7 %copy-start = (f32[2,256,256]{2,1,0:T(8,128)S(1)}, f32[2,256,256]{2,1,0:T(8,128)}, u32[]{:S(2)}) copy-start(f32[2,256,256]{2,1,0:T(8,128)} %kx_ref.1) | copy-start | bytes 1572868
  18.8 9.7 %copy-start.1 = (f32[2,256,256]{2,1,0:T(8,128)S(1)}, f32[2,256,256]{2,1,0:T(8,128)}, u32[]{:S(2)}) copy-start(f32[2,256,256]{2,1,0:T(8,128)} %ky_ref.1) | copy-start | bytes 1572868
  23.9 0.6 copy-start.2
  24.5 9.1 %collective-permute-start.7 = (f32[512,256]{1,0:T(8,128)S(1)}, f32[512,256]{1,0:T(8,128)}, u32[]{:S(2)}, u32[]{:S(2)}) collective-permute-start(f32[512,256]{1,0:T(8,128)S(1)} %get-tuple-element.28.own_ref), channel_id=1, source_target_pairs={{0,1},{1,0},{2,3},{3,2},{4,5},{5,4},{6,7},{7,6},{8,9},{9,8},{10,11... | collective-permute-start | bytes 1572872 | tf_op jit(solution)/shard_map/ppermute | solution.py:314
  24.9 8.8 %collective-permute-start.8 = (f32[6,32,256]{2,1,0:T(8,128)S(1)}, f32[6,32,256]{2,1,0:T(8,128)S(1)}, u32[]{:S(2)}, u32[]{:S(2)}) collective-permute-start(f32[6,32,256]{2,1,0:T(8,128)S(1)} %get-tuple-element.24.cells_ref), channel_id=1, source_target_pairs={{0,24},{1,25},{2,26},{3,27},{4,0},{5,1},{6,2},{7,3},{8,12},{9,13},... | collective-permute-start | bytes 589832 | tf_op jit(solution)/shard_map/ppermute | solution.py:314
  28.5 0.8 copy-start.3
  29.3 10.8 %collective-permute-start.9 = (f32[2,32,256]{2,1,0:T(8,128)S(1)}, f32[2,32,256]{2,1,0:T(8,128)S(1)}, u32[]{:S(2)}, u32[]{:S(2)}) collective-permute-start(f32[2,32,256]{2,1,0:T(8,128)S(1)} %copy-done.3), channel_id=1, source_target_pairs={{0,24},{1,25},{2,26},{3,27},{4,0},{5,1},{6,2},{7,3},{8,12},{9,13},... | collective-permute-start | bytes 196616 | tf_op jit(solution)/shard_map/ppermute | solution.py:314
  45.2 9.7 %collective-permute-start.10 = (f32[512,256]{1,0:T(8,128)S(1)}, f32[512,256]{1,0:T(8,128)S(1)}, u32[]{:S(2)}, u32[]{:S(2)}) collective-permute-start(f32[512,256]{1,0:T(8,128)S(1)} %get-tuple-element.34.own_ref), channel_id=1, source_target_pairs={{0,1},{1,0},{2,3},{3,2},{4,5},{5,4},{6,7},{7,6},{8,9},{9,8},{10,11... | collective-permute-start | bytes 1572872 | tf_op jit(solution)/shard_map/ppermute | solution.py:314
  45.3 9.6 %collective-permute-start.11 = (f32[6,32,256]{2,1,0:T(8,128)S(1)}, f32[6,32,256]{2,1,0:T(8,128)S(1)}, u32[]{:S(2)}, u32[]{:S(2)}) collective-permute-start(f32[6,32,256]{2,1,0:T(8,128)S(1)} %collective-permute-done.8.cells_ref), channel_id=1, source_target_pairs={{0,24},{1,25},{2,26},{3,27},{4,0},{5,1},{6,2},{7,3},{8,12},{9,13},... | collective-permute-start | bytes 589832 | tf_op jit(solution)/shard_map/ppermute | solution.py:314
  49.6 10.7 %collective-permute-start.12 = (f32[2,32,256]{2,1,0:T(8,128)S(1)}, f32[2,32,256]{2,1,0:T(8,128)S(1)}, u32[]{:S(2)}, u32[]{:S(2)}) collective-permute-start(f32[2,32,256]{2,1,0:T(8,128)S(1)} %get-tuple-element.36), channel_id=1, source_target_pairs={{0,24},{1,25},{2,26},{3,27},{4,0},{5,1},{6,2},{7,3},{8,12},{9,13},... | collective-permute-start | bytes 196616 | tf_op jit(solution)/shard_map/ppermute | solution.py:314
  65.4 9.7 %collective-permute-start.13 = (f32[512,256]{1,0:T(8,128)S(1)}, f32[512,256]{1,0:T(8,128)S(1)}, u32[]{:S(2)}, u32[]{:S(2)}) collective-permute-start(f32[512,256]{1,0:T(8,128)S(1)} %get-tuple-element.38.own_ref), channel_id=1, source_target_pairs={{0,1},{1,0},{2,3},{3,2},{4,5},{5,4},{6,7},{7,6},{8,9},{9,8},{10,11... | collective-permute-start | bytes 1572872 | tf_op jit(solution)/shard_map/ppermute | solution.py:314
  65.5 9.6 %collective-permute-start.14 = (f32[6,32,256]{2,1,0:T(8,128)S(1)}, f32[6,32,256]{2,1,0:T(8,128)S(1)}, u32[]{:S(2)}, u32[]{:S(2)}) collective-permute-start(f32[6,32,256]{2,1,0:T(8,128)S(1)} %collective-permute-done.11.cells_ref), channel_id=1, source_target_pairs={{0,24},{1,25},{2,26},{3,27},{4,0},{5,1},{6,2},{7,3},{8,12},{9,13},... | collective-permute-start | bytes 589832 | tf_op jit(solution)/shard_map/ppermute | solution.py:314
  69.8 10.7 %collective-permute-start.15 = (f32[2,32,256]{2,1,0:T(8,128)S(1)}, f32[2,32,256]{2,1,0:T(8,128)S(1)}, u32[]{:S(2)}, u32[]{:S(2)}) collective-permute-start(f32[2,32,256]{2,1,0:T(8,128)S(1)} %get-tuple-element.40), channel_id=1, source_target_pairs={{0,24},{1,25},{2,26},{3,27},{4,0},{5,1},{6,2},{7,3},{8,12},{9,13},... | collective-permute-start | bytes 196616 | tf_op jit(solution)/shard_map/ppermute | solution.py:314
  85.6 2.0 %collective-permute-start.16 = (f32[512,256]{1,0:T(8,128)S(1)}, f32[512,256]{1,0:T(8,128)S(1)}, u32[]{:S(2)}, u32[]{:S(2)}) collective-permute-start(f32[512,256]{1,0:T(8,128)S(1)} %get-tuple-element.42.own_ref), channel_id=1, source_target_pairs={{0,1},{1,0},{2,3},{3,2},{4,5},{5,4},{6,7},{7,6},{8,9},{9,8},{10,11... | collective-permute-start | bytes 1572872 | tf_op jit(solution)/shard_map/ppermute | solution.py:314
  88.8 7.0 %collective-permute-start.19 = (f32[2,8,256]{2,1,0:T(8,128)S(1)}, f32[2,8,256]{2,1,0:T(8,128)S(1)}, u32[]{:S(2)}, u32[]{:S(2)}) collective-permute-start(f32[2,8,256]{2,1,0:T(8,128)S(1)} %get-tuple-element.53), channel_id=1, source_target_pairs={{0,8},{1,9},{2,10},{3,11},{4,16},{5,17},{6,18},{7,19},{8,28},{9,29... | collective-permute-start | bytes 49160 | tf_op jit(solution)/shard_map/ppermute | solution.py:314
  88.9 6.9 %collective-permute-start.20 = (f32[2,8,256]{2,1,0:T(8,128)S(1)}, f32[2,8,256]{2,1,0:T(8,128)S(1)}, u32[]{:S(2)}, u32[]{:S(2)}) collective-permute-start(f32[2,8,256]{2,1,0:T(8,128)S(1)} %get-tuple-element.52), channel_id=1, source_target_pairs={{0,12},{1,13},{2,14},{3,15},{4,20},{5,21},{6,22},{7,23},{8,24},{9,... | collective-permute-start | bytes 49160 | tf_op jit(solution)/shard_map/ppermute | solution.py:314
  88.9 7.6 %collective-permute-start.17 = (f32[64,256]{1,0:T(8,128)S(1)}, f32[64,256]{1,0:T(8,128)S(1)}, u32[]{:S(2)}, u32[]{:S(2)}) collective-permute-start(f32[64,256]{1,0:T(8,128)S(1)} %get-tuple-element.51), channel_id=1, source_target_pairs={{0,16},{1,17},{2,18},{3,19},{4,20},{5,21},{6,22},{7,23},{8,24},{9,... | collective-permute-start | bytes 196616 | tf_op jit(solution)/shard_map/ppermute | solution.py:314
  93.8 8.4 %collective-permute-start.18 = (f32[64,256]{1,0:T(8,128)S(1)}, f32[64,256]{1,0:T(8,128)S(1)}, u32[]{:S(2)}, u32[]{:S(2)}) collective-permute-start(f32[64,256]{1,0:T(8,128)S(1)} %get-tuple-element.50), channel_id=1, source_target_pairs={{0,20},{1,21},{2,22},{3,23},{4,16},{5,17},{6,18},{7,19},{8,28},{9,... | collective-permute-start | bytes 196616 | tf_op jit(solution)/shard_map/ppermute | solution.py:314
